TPU v7x, 512 devices: a whole 4x8x8 slice. The times are simulated.
512 devices in a mesh: cfg: 16 (over z, core), tm: 32 (over y, x).
Axes of the slice: x: 4, y: 8, z: 8, core: 2. Of those that a mesh axis runs over, the one named last changes fastest.
Arguments:
- linv: bfloat16 [65536, 1024], P(('cfg', 'tm')), parts along dimension 0, as said below
- sub: bfloat16 [65536, 1024], P(('cfg', 'tm')), parts along dimension 0, may hold values from -0.046875 to 0.046875
- owner: int32 [64], P('cfg'), parts along dimension 0, may hold values from 0 to 31, as said below
Outputs:
- diag_cov: bfloat16 [65536, 1024], P(('cfg', 'tm')), parts along dimension 0
- off_cov: bfloat16 [65536, 1024], P(('cfg', 'tm')), parts along dimension 0
- owned_var: float32 [1024, 1024], P(('cfg', 'tm')), parts along dimension 0
There are 16 independent parts, one for each index of `cfg`. A program takes and returns all parts, laid end to end along the dimension named above; each array names one. Nothing has to cross between parts.
Inputs may be any that keep to these rules, and one draw needn't show every extreme that they name: Each block of 1024 rows of linv is lower triangular with a positive diagonal. Exactly two time blocks, adjacent in time, share an owner; all other time blocks have distinct owners, so no owner receives more than 2 blocks and one receives exactly 2.
All inputs are finite; a program needn't handle non-finite values.
Results may differ from a plain program's by a relative error of at most 0.0075.
Values may be sent and summed in bfloat16 or wider, within the bound.
No kernel may reach another device: no remote copies, remote signals or barrier semaphores. Data moves between devices by JAX's collectives and lax.ppermute only.
A program may use at most 64 MiB of HBM per device.

v0:
```python
import jax
import jax.numpy as jnp
from jax import lax
from jax.experimental import pallas as pl
from jax.experimental.pallas import tpu as pltpu
from jax.sharding import PartitionSpec as P


TB = 4
SLOTS = 2
NX = 4
N = 1024
BLK = 128
AXES = ("cfg", "tm")
ROW_OF = ((0, 3, 5, 6), (0, 2, 5, 7))


NN = (((1,), (0,)), ((), ()))
NT = (((1,), (1,)), ((), ()))
BF16 = jnp.bfloat16
F32 = jnp.float32


def mine(x, core):
    return x // 2 == core


def send(value, fn):
    n_cfg, n_tm = lax.axis_size("cfg"), lax.axis_size("tm")
    route = []
    for cfg in range(n_cfg):
        for tm in range(n_tm):
            y, x = divmod(tm, NX)
            to = fn(x, y, cfg % 2)
            if to is not None:
                route.append((cfg * n_tm + tm, cfg * n_tm + to[1] * NX + to[0]))
    return lax.ppermute(value, AXES, route)


def load_from(dx, parity):
    def fn(x, y, core):
        to = (x - dx) % NX
        return (to, ROW_OF[core][y // 2]) if y % 2 == parity and mine(to, core) else None

    return fn


def load_above(x, y, core):
    return (x, y ^ 1) if mine(x, core) and y ^ 1 == ROW_OF[core][y // 2] else None


def replica_to(t, u):
    def fn(x, y, core):
        return (x, ROW_OF[core][u]) if mine(x, core) and y == ROW_OF[core][t] else None

    return fn


def spread(across, other):
    def fn(x, y, core):
        if not mine(x, core) or y != ROW_OF[core][y // 2]:
            return None
        return (3 - x if across else x, y ^ 1 if other else y)

    return fn


def block(b):
    return pl.ds(pl.multiple_of(b * BLK, BLK), BLK)


def tile(i):
    return slice(i * 256, (i + 1) * 256)


def here():
    x = lax.rem(lax.axis_index("tm"), NX)
    y = lax.div(lax.axis_index("tm"), NX)
    return x, lax.rem(y, 2), lax.div(y, 2)


def dot(a, b, dims):
    return lax.dot_general(a, b, dims, preferred_element_type=F32)


def pack(pack_ref, s_ref):
    for p in range(4):
        rows = slice(p * BLK, (p + 1) * BLK)
        width = (8 - p) * BLK
        pack_ref[rows, :width] = s_ref[(7 - p) * BLK:(8 - p) * BLK, :width]
        pack_ref[rows, width:] = s_ref[p * BLK:(p + 1) * BLK, :(p + 1) * BLK]


def unpack(s_ref, pack_ref):
    for p in range(4):
        rows = slice(p * BLK, (p + 1) * BLK)
        width = (8 - p) * BLK
        s_ref[(7 - p) * BLK:(8 - p) * BLK, :width] = pack_ref[rows, :width]
        s_ref[p * BLK:(p + 1) * BLK, :(p + 1) * BLK] = pack_ref[rows, width:]


def mirror(s_ref):
    for i in range(1, 8):
        rows = slice(i * BLK, (i + 1) * BLK)
        left = s_ref[rows, :i * BLK].astype(F32)
        s_ref[:i * BLK, rows] = left.T.astype(BF16)


def pack_upper(pack_ref, f_ref):
    for p in range(4):
        rows = slice(p * BLK, (p + 1) * BLK)
        width = (8 - p) * BLK
        pack_ref[rows, :width] = f_ref[p * BLK:(p + 1) * BLK, p * BLK:]
        pack_ref[rows, width:] = f_ref[(7 - p) * BLK:(8 - p) * BLK, (7 - p) * BLK:]


def unpack_upper(f_ref, pack_ref):
    f_ref[...] = jnp.zeros_like(f_ref)
    for p in range(4):
        rows = slice(p * BLK, (p + 1) * BLK)
        width = (8 - p) * BLK
        f_ref[p * BLK:(p + 1) * BLK, p * BLK:] = pack_ref[rows, :width]
        f_ref[(7 - p) * BLK:(8 - p) * BLK, (7 - p) * BLK:] = pack_ref[rows, width:]


def lower(s_ref, f_ref, wt_ref, gt_ref):
    for i in range(4):
        cols = slice(0, (i + 1) * 256)
        gram = dot(f_ref[tile(i), i * 256:], f_ref[cols, i * 256:], NT)
        s_ref[tile(i), cols] = (gram + dot(wt_ref[tile(i), :], gt_ref[cols, :], NT)).astype(BF16)


def load_kernel(own_l, own_f, q0, e1, e2, e3, o1, o2, o3, gt_ref, f_ref, fpack_ref, spack_ref, l_ref, s_ref):
    x, parity, _ = here()
    f_ref[512:, :512] = jnp.zeros((512, 512), BF16)

    def place(at, piece, blocks):
        l_ref[block(at), :] = piece[:, :N]
        for b in range(blocks):
            f_ref[b * BLK:(b + 1) * BLK, block(at)] = piece[:, N + b * BLK:N + (b + 1) * BLK]

    at = parity * NX + x
    l_ref[block(at), :] = own_l[...]
    for b in range(8):
        f_ref[b * BLK:(b + 1) * BLK, block(at)] = own_f[:, b * BLK:(b + 1) * BLK]
    place((1 - parity) * NX + x, q0, 8)
    for dx, even, odd in ((1, e1, o1), (2, e2, o2), (3, e3, o3)):
        place(lax.rem(x + dx, NX), even, 4)
        place(NX + lax.rem(x + dx, NX), odd, 8)
    for i in range(4):
        gt_ref[tile(i), :] = dot(f_ref[tile(i), i * 256:], l_ref[:, i * 256:], NT).astype(BF16)
    lower(s_ref, f_ref, gt_ref, gt_ref)
    pack(spack_ref, s_ref)
    pack_upper(fpack_ref, f_ref)


def step_kernel(pack_in, gt_ref, f_ref, pack_out, s_ref, wt_ref):
    unpack(s_ref, pack_in)
    mirror(s_ref)
    for i in range(4):
        wt_ref[tile(i), :] = dot(gt_ref[tile(i), :], s_ref[...], NN).astype(BF16)
    lower(s_ref, f_ref, wt_ref, gt_ref)
    pack(pack_out, s_ref)


def rows_of(x, parity):
    far = 3 - x
    return (
        parity * NX + x, (1 - parity) * NX + x, parity * NX + far, (1 - parity) * NX + far
    )


def pick(out_ref, at, ref, places):
    for k, place in enumerate(places):
        out_ref[at + k * BLK:at + (k + 1) * BLK, :] = ref[block(place), :]


def gram_kernel(f_ref, out_ref, fm_ref):
    x, parity, _ = here()
    pick(fm_ref, 0, f_ref, rows_of(x, parity))
    for i in range(2):
        out_ref[tile(i), :] = dot(fm_ref[tile(i), :], f_ref[...], NT)


def prepare_kernel(gt_next, fpack_next, gt_ref, left_ref, base_ref, fn_ref, gm_ref, h_ref):
    x, parity, _ = here()
    places = rows_of(x, parity)
    unpack_upper(fn_ref, fpack_next)
    pick(gm_ref, 0, gt_ref, places)
    pick(left_ref, 512, gt_next, places)
    pick(h_ref, 512, fn_ref, places)
    for i in range(2):
        left_ref[tile(i), :] = dot(gm_ref[tile(i), :], gt_next[...], NN).astype(BF16)
        h_ref[tile(i), :] = dot(gm_ref[tile(i), :], fn_ref[...], NN).astype(BF16)
    for i in range(4):
        base_ref[tile(i), :] = dot(h_ref[tile(i), :], fn_ref[...], NT)


def final_kernel(
    to2, to1, to0, left_ref, base_ref, gt_next, gram_ref, gt_ref,
    own_ref, a1_ref, a2_ref, a3_ref, var_ref, s_ref, x_ref, w_ref,
):
    x, parity, group = here()
    places = rows_of(x, parity)
    for t, source in ((2, to2), (1, to1), (0, to0)):
        @pl.when(group == t)
        def _():
            unpack(s_ref, source)
            mirror(s_ref)

    @pl.when(group == TB - 1)
    def _():
        for i in range(8):
            row = lax.broadcasted_iota(jnp.int32, (BLK, N), 0) + i * BLK
            col = lax.broadcasted_iota(jnp.int32, (BLK, N), 1)
            s_ref[i * BLK:(i + 1) * BLK, :] = jnp.where(row == col, 1.0, 0.0).astype(BF16)

    @pl.when(group == 0)
    def _():
        for i in range(4):
            w_ref[tile(i), :] = dot(left_ref[tile(i), :], s_ref[...], NN).astype(BF16)
        for i in range(4):
            x_ref[tile(i), :] = (base_ref[tile(i), :] + dot(w_ref[tile(i), :], gt_next[...], NT)).astype(BF16)

    @pl.when(group != 0)
    def _():
        pick(w_ref, 0, gt_ref, places)
        for i in range(2):
            x_ref[tile(i), :] = dot(w_ref[tile(i), :], s_ref[...], NN).astype(BF16)
        pick(x_ref, 512, s_ref, places)

    outs = (own_ref, a1_ref, a2_ref, a3_ref)
    for i in range(2):
        strip = gram_ref[tile(i), :] + dot(x_ref[tile(i), :], gt_ref[...], NT)
        outs[2 * i][0] = strip[:BLK].astype(BF16)
        outs[2 * i + 1][0] = strip[BLK:].astype(BF16)
        off = -dot(x_ref[tile(i + 2), :], gt_ref[...], NT)
        outs[2 * i][1] = off[:BLK].astype(BF16)
        outs[2 * i + 1][1] = off[BLK:].astype(BF16)
    row = lax.broadcasted_iota(jnp.int32, (BLK, BLK), 0)
    col = lax.broadcasted_iota(jnp.int32, (BLK, BLK), 1)
    var_ref[...] = jnp.zeros_like(var_ref)
    for k, at in enumerate(places):
        square = outs[k][0, :, block(at)].astype(F32)
        var_ref[pl.ds(at, 1), :] = jnp.sum(jnp.where(row == col, square, 0.0), axis=0, keepdims=True)


def call(kernel, outs, scratch, flops, *args):
    vmem = pl.BlockSpec(memory_space=pltpu.VMEM)
    moved = sum(a.size * a.dtype.itemsize for a in args)
    return pl.pallas_call(
        kernel,
        out_shape=[jax.ShapeDtypeStruct(s, d) for s, d in outs],
        in_specs=[vmem] * len(args),
        out_specs=[vmem] * len(outs),
        scratch_shapes=[pltpu.VMEM(s, BF16) for s in scratch],
        cost_estimate=pl.CostEstimate(flops=flops, bytes_accessed=moved, transcendentals=0),
        compiler_params=pltpu.CompilerParams(vmem_limit_bytes=24 * 1024 * 1024),
    )(*args)


def sweep(linv, sub, owner):
    core = lax.rem(lax.axis_index("cfg"), 2)
    tm = lax.axis_index("tm")
    x, y = lax.rem(tm, NX), lax.div(tm, NX)
    flops = 2 * N * N * N
    square, packed, half = (N, N), (512, 1152), (512, N)

    turned = linv.reshape(BLK, 8, BLK).transpose(2, 1, 0).reshape(BLK, N)
    full = jnp.concatenate([sub, turned], 1)
    short = full[:, :N + 512]
    q0 = send(full, load_above)
    evens = [send(short, load_from(dx, 0)) for dx in (1, 2, 3)]
    odds = [send(full, load_from(dx, 1)) for dx in (1, 2, 3)]
    gt, ft, fpack, spack = call(
        load_kernel,
        [(square, BF16), (square, BF16), (packed, BF16), (packed, BF16)],
        [square, square], 3 * flops, sub, turned, q0, *evens, *odds,
    )
    to2 = send(spack, replica_to(3, 2))
    gt_next = send(gt, replica_to(1, 0))
    f_next = send(fpack, replica_to(1, 0))
    (second,) = call(step_kernel, [(packed, BF16)], [square, square], 2 * flops, to2, gt, ft)
    to0 = send(second, replica_to(2, 0))
    to1 = send(second, replica_to(2, 1))
    (gram,) = call(gram_kernel, [(half, F32)], [half], flops, ft)
    left, base = call(
        prepare_kernel, [(square, BF16), (square, F32)], [square, half, square],
        2 * flops, gt_next, f_next, gt,
    )
    strip = (2, BLK, N)
    own, a1, a2, a3, var = call(
        final_kernel,
        [(strip, BF16)] * 4 + [((8, BLK), F32)],
        [square, square, square],
        4 * flops, to2, to1, to0, left, base, gt_next, gram, gt,
    )
    b1 = send(a1, spread(False, True))
    b3 = send(a3, spread(True, True))
    b2 = send(a2, spread(True, False))

    n_tm = lax.axis_size("tm")
    every = lax.all_to_all(
        jnp.broadcast_to(var[None], (n_tm, 8, BLK)), "tm", 0, 0, tiled=True
    )
    every = every.reshape(2 * TB, NX, 8, BLK)
    pair = jnp.stack([
        jnp.where(core == 0, every[r0, 0] + every[r0, 1], every[r1, 2] + every[r1, 3])
        for r0, r1 in zip(*ROW_OF)
    ])
    variances = pair.reshape(TB, N)

    near = lax.div(x, 2) == core
    row_of = sum(
        jnp.where(lax.div(y, 2) == t, jnp.where(core == 0, ROW_OF[0][t], ROW_OF[1][t]), 0)
        for t in range(TB)
    )
    level = y == row_of
    rows = [
        jnp.where(near, jnp.where(level, own[i], b1[i]), jnp.where(level, b2[i], b3[i]))
        for i in range(2)
    ]

    positions = lax.broadcasted_iota(jnp.int32, (TB, TB), 1)
    current = lax.broadcasted_iota(jnp.int32, (TB, TB), 0)
    same_owner = owner[:, None] == owner[None, :]
    rank = jnp.sum(jnp.where(same_owner & (positions < current), 1, 0), axis=1)
    slot = lax.broadcasted_iota(jnp.int32, (SLOTS, TB), 0)
    chosen = (owner[None, :] == tm) & (rank[None, :] == slot)
    owned = jnp.sum(jnp.where(chosen[:, :, None], variances[None], 0.0), axis=1)
    return rows[0], rows[1], owned


def solution(mesh):
    spec = P(AXES, None)
    return jax.shard_map(
        sweep,
        mesh=mesh,
        in_specs=(spec, spec, P("cfg")),
        out_specs=(spec, spec, spec),
        check_vma=False,
    )
```

profile of v0, /device:TPU:20, one launch (start us, length us, event | category | flops | bytes accessed | tf_op | source)
XLA Modules:
  0.0 135.6 jit_solution(9332879934847998506)
XLA Ops:
  0.6 1.0 copy.8
  1.7 0.2 copy.7
  2.0 3.5 %collective-permute-start.1 = (bf16[128,1536]{1,0:T(8,128)(2,1)S(1)}, bf16[128,1536]{1,0:T(8,128)(2,1)S(1)}, u32[]{:S(2)}, u32[]{:S(2)}) collective-permute-start(bf16[128,1536]{1,0:T(8,128)(2,1)S(1)} %slice.100), channel_id=1, source_target_pairs={{1,0},{2,1},{9,12},{10,13},{17,20},{18,21},{25,24},{26,25},{32,35}... | collective-permute-start | bytes 1179656 | tf_op jit(solution)/shard_map/ppermute | solution.py:37
  5.5 1.3 collective-permute-start.2
  6.8 0.7 collective-permute-start
  7.5 0.7 collective-permute-start.4
  8.2 0.7 collective-permute-start.5
  8.9 2.3 %collective-permute-done.1.e1 = bf16[128,1536]{1,0:T(8,128)(2,1)S(1)} collective-permute-done((bf16[128,1536]{1,0:T(8,128)(2,1)S(1)}, bf16[128,1536]{1,0:T(8,128)(2,1)S(1)}, u32[]{:S(2)}, u32[]{:S(2)}) %collective-permute-start.1) | collective-permute-done | bytes 393248 | tf_op jit(solution)/shard_map/ppermute | solution.py:37
  11.2 0.7 collective-permute-start.6
  11.9 3.6 %collective-permute-done.2.e2 = bf16[128,1536]{1,0:T(8,128)(2,1)S(1)} collective-permute-done((bf16[128,1536]{1,0:T(8,128)(2,1)S(1)}, bf16[128,1536]{1,0:T(8,128)(2,1)S(1)}, u32[]{:S(2)}, u32[]{:S(2)}) %collective-permute-start.2) | collective-permute-done | bytes 393248 | tf_op jit(solution)/shard_map/ppermute | solution.py:37
  15.5 0.7 collective-permute-start.3
  16.2 0.0 collective-permute-done.3.e3
  16.3 0.0 collective-permute-done.q0
  16.3 0.0 collective-permute-done.4.o1
  16.3 0.0 collective-permute-done.5.o2
  16.3 0.0 collective-permute-done.6.o3
  16.3 5.0 %shard_map.58 = (bf16[1024,1024]{1,0:T(8,128)(2,1)S(1)}, bf16[1024,1024]{1,0:T(8,128)(2,1)S(1)}, bf16[512,1152]{1,0:T(8,128)(2,1)}, bf16[512,1152]{1,0:T(8,128)(2,1)S(1)}) custom-call(bf16[128,1024]{1,0:T(8,128)(2,1)S(1)} %copy-done, bf16[128,1024]{1,0:T(8,128)(2,1)S(1)} %bitcast.20, bf16[128,2048]{1,0:T(8,128)(2,1)S(1)} %collective-permute-done.q0, ...), custom_call_target="tpu_custom_call" | custom-call | flops 6442450944 | bytes 3801088 | tf_op jit(solution)/shard_map/pallas_call | solution.py:251
  21.3 0.7 collective-permute-start.7
  22.0 2.0 %collective-permute-start.10 = (bf16[1024,1024]{1,0:T(8,128)(2,1)S(1)}, bf16[1024,1024]{1,0:T(8,128)(2,1)}, u32[]{:S(2)}, u32[]{:S(2)}) collective-permute-start(bf16[1024,1024]{1,0:T(8,128)(2,1)S(1)} %get-tuple-element.15.gt_ref), channel_id=1, source_target_pairs={{12,0},{13,1},{42,34},{43,35},{76,64},{77,65},{106,98},{107,99},{1... | collective-permute-start | bytes 6291464 | tf_op jit(solution)/shard_map/ppermute | solution.py:37
  24.0 1.7 %collective-permute-start.11 = (bf16[512,1152]{1,0:T(8,128)(2,1)}, bf16[512,1152]{1,0:T(8,128)(2,1)}, u32[]{:S(2)}, u32[]{:S(2)}) collective-permute-start(bf16[512,1152]{1,0:T(8,128)(2,1)} %get-tuple-element.17), channel_id=1, source_target_pairs={{12,0},{13,1},{42,34},{43,35},{76,64},{77,65},{106,98},{107,99},{1... | collective-permute-start | bytes 3538952 | tf_op jit(solution)/shard_map/ppermute | solution.py:37
  25.7 0.0 collective-permute-done.7.pack_in.to2
  25.7 5.6 %shard_map.59 = bf16[512,1152]{1,0:T(8,128)(2,1)} custom-call(bf16[512,1152]{1,0:T(8,128)(2,1)S(1)} %collective-permute-done.7.pack_in.to2, bf16[1024,1024]{1,0:T(8,128)(2,1)S(1)} %get-tuple-element.15.gt_ref, bf16[1024,1024]{1,0:T(8,128)(2,1)S(1)} %get-tuple-element.16.f_ref), custom_call_target="tpu_custom_call" | custom-call | flops 4294967296 | bytes 5373952 | tf_op jit(solution)/shard_map/pallas_call | solution.py:251
  31.3 0.0 copy-done.1
  31.3 1.7 %collective-permute-start.8 = (bf16[512,1152]{1,0:T(8,128)(2,1)}, bf16[512,1152]{1,0:T(8,128)(2,1)}, u32[]{:S(2)}, u32[]{:S(2)}) collective-permute-start(bf16[512,1152]{1,0:T(8,128)(2,1)} %shard_map.59), channel_id=1, source_target_pairs={{20,12},{21,13},{54,42},{55,43},{84,76},{85,77},{118,106},{119,107... | collective-permute-start | bytes 3538952 | tf_op jit(solution)/shard_map/ppermute | solution.py:37
  33.0 1.7 %collective-permute-start.9 = (bf16[512,1152]{1,0:T(8,128)(2,1)}, bf16[512,1152]{1,0:T(8,128)(2,1)}, u32[]{:S(2)}, u32[]{:S(2)}) collective-permute-start(bf16[512,1152]{1,0:T(8,128)(2,1)} %shard_map.59), channel_id=1, source_target_pairs={{20,0},{21,1},{54,34},{55,35},{84,64},{85,65},{118,98},{119,99},{1... | collective-permute-start | bytes 3538952 | tf_op jit(solution)/shard_map/ppermute | solution.py:37
  34.8 1.6 %copy-done.6 = bf16[1024,1024]{1,0:T(8,128)(2,1)S(1)} copy-done((bf16[1024,1024]{1,0:T(8,128)(2,1)S(1)}, bf16[1024,1024]{1,0:T(8,128)(2,1)}, u32[]{:S(2)}) %copy-start.6) | copy-done | bytes 2097176
  36.4 1.3 shard_map.61.gram_ref
  37.6 0.0 collective-permute-done.11.fpack_next
  37.7 0.0 collective-permute-done.10.gt_next
  37.7 6.6 %shard_map.60 = (bf16[1024,1024]{1,0:T(8,128)(2,1)S(1)}, f32[1024,1024]{1,0:T(8,128)S(1)}) custom-call(bf16[1024,1024]{1,0:T(8,128)(2,1)} %collective-permute-done.10.gt_next, bf16[512,1152]{1,0:T(8,128)(2,1)} %collective-permute-done.11.fpack_next, bf16[1024,1024]{1,0:T(8,128)(2,1)S(1)} %get-tuple-element.15.gt_ref), custom_call_target="tpu_custom_call" | custom-call | flops 4294967296 | bytes 5373952 | tf_op jit(solution)/shard_map/pallas_call | solution.py:251
  44.3 0.0 collective-permute-done.8.to1
  44.3 0.0 collective-permute-done.9.to0
  44.3 0.0 copy-done.2
  44.3 6.6 %shard_map.62 = (bf16[2,128,1024]{2,1,0:T(8,128)(2,1)S(1)}, bf16[2,128,1024]{2,1,0:T(8,128)(2,1)S(1)}, bf16[2,128,1024]{2,1,0:T(8,128)(2,1)S(1)}, bf16[2,128,1024]{2,1,0:T(8,128)(2,1)S(1)}, f32[8,128]{1,0:T(8,128)S(1)}) custom-call(bf16[512,1152]{1,0:T(8,128)(2,1)S(1)} %copy-done.2, bf16[512,1152]{1,0:T(8,128)(2,1)} %collective-permute-done.8.to1, ...), custom_call_target="tpu_custom_call" | custom-call | flops 8589934592 | bytes 16121856 | tf_op jit(solution)/shard_map/pallas_call | solution.py:251
  50.9 0.8 copy-done.3
  51.7 0.8 copy-done.4
  52.5 0.7 broadcast_in_dim.44
  53.2 64.1 %all-to-all-start = ((f32[32,8,128]{2,1,0:T(8,128)}), f32[32,8,128]{2,1,0:T(8,128)S(1)}, u32[]{:S(2)}, u32[]{:S(2)}) async-start(f32[32,8,128]{2,1,0:T(8,128)} %broadcast_in_dim.44), calls=%async_computation | async-start | bytes 262144 | tf_op jit(solution)/shard_map/all_to_all | solution.py:303
  117.2 0.2 select_reduce_fusion.1
  117.4 0.7 collective-permute-start.12
  118.1 0.7 collective-permute-start.13
  118.8 1.3 collective-permute-start.14
  120.2 3.7 %all-to-all-done = f32[32,8,128]{2,1,0:T(8,128)S(1)} async-done(((f32[32,8,128]{2,1,0:T(8,128)}), f32[32,8,128]{2,1,0:T(8,128)S(1)}, u32[]{:S(2)}, u32[]{:S(2)}) %all-to-all-start) | async-done | bytes 131104 | tf_op jit(solution)/shard_map/all_to_all | solution.py:303
  123.9 0.7 select_reduce_fusion
  124.6 0.0 collective-permute-done.12
  124.6 0.0 collective-permute-done.13
  124.6 10.1 %collective-permute-done.14 = bf16[2,128,1024]{2,1,0:T(8,128)(2,1)S(1)} collective-permute-done((bf16[2,128,1024]{2,1,0:T(8,128)(2,1)S(1)}, bf16[2,128,1024]{2,1,0:T(8,128)(2,1)S(1)}, u32[]{:S(2)}, u32[]{:S(2)}) %collective-permute-start.14) | collective-permute-done | bytes 524320 | tf_op jit(solution)/shard_map/ppermute | solution.py:37
  134.7 0.9 fusion.1
  (19 shorter events, 0.2 us)
Async XLA Ops:
  0.6 1.3 copy-start
  2.0 9.2 %collective-permute-start.1 = (bf16[128,1536]{1,0:T(8,128)(2,1)S(1)}, bf16[128,1536]{1,0:T(8,128)(2,1)S(1)}, u32[]{:S(2)}, u32[]{:S(2)}) collective-permute-start(bf16[128,1536]{1,0:T(8,128)(2,1)S(1)} %slice.100), channel_id=1, source_target_pairs={{1,0},{2,1},{9,12},{10,13},{17,20},{18,21},{25,24},{26,25},{32,35}... | collective-permute-start | bytes 1179656 | tf_op jit(solution)/shard_map/ppermute | solution.py:37
  5.5 10.0 %collective-permute-start.2 = (bf16[128,1536]{1,0:T(8,128)(2,1)S(1)}, bf16[128,1536]{1,0:T(8,128)(2,1)S(1)}, u32[]{:S(2)}, u32[]{:S(2)}) collective-permute-start(bf16[128,1536]{1,0:T(8,128)(2,1)S(1)} %slice.100), channel_id=1, source_target_pairs={{2,0},{3,1},{10,12},{11,13},{18,20},{19,21},{26,24},{27,25},{32,34... | collective-permute-start | bytes 1179656 | tf_op jit(solution)/shard_map/ppermute | solution.py:37
  6.8 9.4 %collective-permute-start = (bf16[128,2048]{1,0:T(8,128)(2,1)S(1)}, bf16[128,2048]{1,0:T(8,128)(2,1)S(1)}, u32[]{:S(2)}, u32[]{:S(2)}) collective-permute-start(bf16[128,2048]{1,0:T(8,128)(2,1)S(1)} %constant_dynamic-update-slice_fusion), channel_id=1, source_target_pairs={{4,0},{5,1},{8,12},{9,13},{16,20},{17,21},{28,24},{29,25},{38,34},... | collective-permute-start | bytes 1572872 | tf_op jit(solution)/shard_map/ppermute | solution.py:37
  7.5 8.7 %collective-permute-start.4 = (bf16[128,2048]{1,0:T(8,128)(2,1)S(1)}, bf16[128,2048]{1,0:T(8,128)(2,1)S(1)}, u32[]{:S(2)}, u32[]{:S(2)}) collective-permute-start(bf16[128,2048]{1,0:T(8,128)(2,1)S(1)} %constant_dynamic-update-slice_fusion), channel_id=1, source_target_pairs={{5,0},{6,1},{13,12},{14,13},{21,20},{22,21},{29,24},{30,25},{36,35... | collective-permute-start | bytes 1572872 | tf_op jit(solution)/shard_map/ppermute | solution.py:37
  8.2 8.0 %collective-permute-start.5 = (bf16[128,2048]{1,0:T(8,128)(2,1)S(1)}, bf16[128,2048]{1,0:T(8,128)(2,1)S(1)}, u32[]{:S(2)}, u32[]{:S(2)}) collective-permute-start(bf16[128,2048]{1,0:T(8,128)(2,1)S(1)} %constant_dynamic-update-slice_fusion), channel_id=1, source_target_pairs={{6,0},{7,1},{14,12},{15,13},{22,20},{23,21},{30,24},{31,25},{36,34... | collective-permute-start | bytes 1572872 | tf_op jit(solution)/shard_map/ppermute | solution.py:37
  11.2 5.0 %collective-permute-start.6 = (bf16[128,2048]{1,0:T(8,128)(2,1)S(1)}, bf16[128,2048]{1,0:T(8,128)(2,1)S(1)}, u32[]{:S(2)}, u32[]{:S(2)}) collective-permute-start(bf16[128,2048]{1,0:T(8,128)(2,1)S(1)} %constant_dynamic-update-slice_fusion), channel_id=1, source_target_pairs={{4,1},{7,0},{12,13},{15,12},{20,21},{23,20},{28,25},{31,24},{37,34... | collective-permute-start | bytes 1572872 | tf_op jit(solution)/shard_map/ppermute | solution.py:37
  15.5 0.7 collective-permute-start.3
  21.3 10.0 %copy-start.5 = (bf16[1024,1024]{1,0:T(8,128)(2,1)}, bf16[1024,1024]{1,0:T(8,128)(2,1)S(1)}, u32[]{:S(2)}) copy-start(bf16[1024,1024]{1,0:T(8,128)(2,1)S(1)} %get-tuple-element.16.f_ref) | copy-start | bytes 6291460
  21.3 4.4 %collective-permute-start.7 = (bf16[512,1152]{1,0:T(8,128)(2,1)S(1)}, bf16[512,1152]{1,0:T(8,128)(2,1)S(1)}, u32[]{:S(2)}, u32[]{:S(2)}) collective-permute-start(bf16[512,1152]{1,0:T(8,128)(2,1)S(1)} %get-tuple-element.14), channel_id=1, source_target_pairs={{24,20},{25,21},{62,54},{63,55},{88,84},{89,85},{126,118},{127,119... | collective-permute-start | bytes 3538952 | tf_op jit(solution)/shard_map/ppermute | solution.py:37
  22.0 15.6 %collective-permute-start.10 = (bf16[1024,1024]{1,0:T(8,128)(2,1)S(1)}, bf16[1024,1024]{1,0:T(8,128)(2,1)}, u32[]{:S(2)}, u32[]{:S(2)}) collective-permute-start(bf16[1024,1024]{1,0:T(8,128)(2,1)S(1)} %get-tuple-element.15.gt_ref), channel_id=1, source_target_pairs={{12,0},{13,1},{42,34},{43,35},{76,64},{77,65},{106,98},{107,99},{1... | collective-permute-start | bytes 6291464 | tf_op jit(solution)/shard_map/ppermute | solution.py:37
  24.0 13.6 %collective-permute-start.11 = (bf16[512,1152]{1,0:T(8,128)(2,1)}, bf16[512,1152]{1,0:T(8,128)(2,1)}, u32[]{:S(2)}, u32[]{:S(2)}) collective-permute-start(bf16[512,1152]{1,0:T(8,128)(2,1)} %get-tuple-element.17), channel_id=1, source_target_pairs={{12,0},{13,1},{42,34},{43,35},{76,64},{77,65},{106,98},{107,99},{1... | collective-permute-start | bytes 3538952 | tf_op jit(solution)/shard_map/ppermute | solution.py:37
  25.7 5.6 %copy-start.1 = (bf16[512,1152]{1,0:T(8,128)(2,1)}, bf16[512,1152]{1,0:T(8,128)(2,1)S(1)}, u32[]{:S(2)}) copy-start(bf16[512,1152]{1,0:T(8,128)(2,1)S(1)} %collective-permute-done.7.pack_in.to2) | copy-start | bytes 3538948
  25.7 9.1 %copy-start.7 = (s32[4]{0:T(128)S(1)}, s32[4]{0:T(128)}, u32[]{:S(2)}) copy-start(s32[4]{0:T(128)} %param.5) | copy-start | bytes 52
  31.3 13.0 %collective-permute-start.8 = (bf16[512,1152]{1,0:T(8,128)(2,1)}, bf16[512,1152]{1,0:T(8,128)(2,1)}, u32[]{:S(2)}, u32[]{:S(2)}) collective-permute-start(bf16[512,1152]{1,0:T(8,128)(2,1)} %shard_map.59), channel_id=1, source_target_pairs={{20,12},{21,13},{54,42},{55,43},{84,76},{85,77},{118,106},{119,107... | collective-permute-start | bytes 3538952 | tf_op jit(solution)/shard_map/ppermute | solution.py:37
  33.0 11.3 %collective-permute-start.9 = (bf16[512,1152]{1,0:T(8,128)(2,1)}, bf16[512,1152]{1,0:T(8,128)(2,1)}, u32[]{:S(2)}, u32[]{:S(2)}) collective-permute-start(bf16[512,1152]{1,0:T(8,128)(2,1)} %shard_map.59), channel_id=1, source_target_pairs={{20,0},{21,1},{54,34},{55,35},{84,64},{85,65},{118,98},{119,99},{1... | collective-permute-start | bytes 3538952 | tf_op jit(solution)/shard_map/ppermute | solution.py:37
  34.8 1.6 %copy-start.6 = (bf16[1024,1024]{1,0:T(8,128)(2,1)S(1)}, bf16[1024,1024]{1,0:T(8,128)(2,1)}, u32[]{:S(2)}) copy-start(bf16[1024,1024]{1,0:T(8,128)(2,1)} %copy-done.5) | copy-start | bytes 6291460
  37.6 6.7 %copy-start.2 = (bf16[512,1152]{1,0:T(8,128)(2,1)S(1)}, bf16[512,1152]{1,0:T(8,128)(2,1)}, u32[]{:S(2)}) copy-start(bf16[512,1152]{1,0:T(8,128)(2,1)} %copy-done.1) | copy-start | bytes 3538948
  50.9 0.8 copy-start.3
  51.7 0.8 copy-start.4
  53.2 70.7 %all-to-all-start = ((f32[32,8,128]{2,1,0:T(8,128)}), f32[32,8,128]{2,1,0:T(8,128)S(1)}, u32[]{:S(2)}, u32[]{:S(2)}) async-start(f32[32,8,128]{2,1,0:T(8,128)} %broadcast_in_dim.44), calls=%async_computation | async-start | bytes 262144 | tf_op jit(solution)/shard_map/all_to_all | solution.py:303
  117.4 7.2 %collective-permute-start.12 = (bf16[2,128,1024]{2,1,0:T(8,128)(2,1)}, bf16[2,128,1024]{2,1,0:T(8,128)(2,1)S(1)}, u32[]{:S(2)}, u32[]{:S(2)}) collective-permute-start(bf16[2,128,1024]{2,1,0:T(8,128)(2,1)} %copy-done.4), channel_id=1, source_target_pairs={{0,4},{1,5},{12,8},{13,9},{20,16},{21,17},{24,28},{25,29},{34,38},... | collective-permute-start | bytes 1572872 | tf_op jit(solution)/shard_map/ppermute | solution.py:37
  118.1 6.5 %collective-permute-start.13 = (bf16[2,128,1024]{2,1,0:T(8,128)(2,1)}, bf16[2,128,1024]{2,1,0:T(8,128)(2,1)S(1)}, u32[]{:S(2)}, u32[]{:S(2)}) collective-permute-start(bf16[2,128,1024]{2,1,0:T(8,128)(2,1)} %copy-done.3), channel_id=1, source_target_pairs={{0,3},{1,2},{12,15},{13,14},{20,23},{21,22},{24,27},{25,26},{34,33... | collective-permute-start | bytes 1572872 | tf_op jit(solution)/shard_map/ppermute | solution.py:37
  118.8 15.9 %collective-permute-start.14 = (bf16[2,128,1024]{2,1,0:T(8,128)(2,1)S(1)}, bf16[2,128,1024]{2,1,0:T(8,128)(2,1)S(1)}, u32[]{:S(2)}, u32[]{:S(2)}) collective-permute-start(bf16[2,128,1024]{2,1,0:T(8,128)(2,1)S(1)} %get-tuple-element.23), channel_id=1, source_target_pairs={{0,7},{1,6},{12,11},{13,10},{20,19},{21,18},{24,31},{25,30},{34,37... | collective-permute-start | bytes 1572872 | tf_op jit(solution)/shard_map/ppermute | solution.py:37
where the time goes:
time: 136 us
  starting transfers between devices  82.8 us (61%)
  Pallas kernels  25 us (18%)
  waiting for transfers between devices  19.7 us (14%)
  local copies, waits for them, and re-layouts  5.28 us (4%)
  other arithmetic  1.81 us (1%)
    all_to_all x1, starting transfers between devices, sweep(): lax.all_to_all(jnp.broadcast_to(var[None], (n_tm, 8, BLK)), 'tm', 0, 0, t...  64.1 us
    pallas_call x5, Pallas kernels, call(): pl.pallas_call(kernel, out_shape=[jax.ShapeDtypeStruct(s, d) for s, d in...  25 us
    ppermute x15, starting transfers between devices, send(): return lax.ppermute(value, AXES, route)  18.7 us
    ppermute x15, waiting for transfers between devices, send(): return lax.ppermute(value, AXES, route)  16 us
    unnamed x19, local copies, waits for them, and re-layouts  4.32 us
    all_to_all x1, waiting for transfers between devices, sweep(): lax.all_to_all(jnp.broadcast_to(var[None], (n_tm, 8, BLK)), 'tm', 0, 0, t...  3.7 us
  transfers between devices with their start and end apart: 16, of which 4 were waited for; matrix products, arithmetic and copies ran while one was open for 1% of the time, Pallas kernels for 10%

commit v1 on v0

--- a/solution.py
+++ b/solution.py
@@ -130,7 +130,17 @@
         s_ref[tile(i), cols] = (gram + dot(wt_ref[tile(i), :], gt_ref[cols, :], NT)).astype(BF16)
 
 
-def load_kernel(own_l, own_f, q0, e1, e2, e3, o1, o2, o3, gt_ref, f_ref, fpack_ref, spack_ref, l_ref, s_ref):
+def pack_kernel(linv_ref, sub_ref, full_ref, short_ref):
+    full_ref[:, :N] = sub_ref[...]
+    short_ref[:, :N] = sub_ref[...]
+    for b in range(8):
+        turned = linv_ref[:, b * BLK:(b + 1) * BLK].astype(F32).T.astype(BF16)
+        full_ref[:, N + b * BLK:N + (b + 1) * BLK] = turned
+        if b < 4:
+            short_ref[:, N + b * BLK:N + (b + 1) * BLK] = turned
+
+
+def load_kernel(own, q0, e1, e2, e3, o1, o2, o3, gt_ref, f_ref, fpack_ref, spack_ref, l_ref, s_ref):
     x, parity, _ = here()
     f_ref[512:, :512] = jnp.zeros((512, 512), BF16)
 
@@ -139,10 +149,7 @@
         for b in range(blocks):
             f_ref[b * BLK:(b + 1) * BLK, block(at)] = piece[:, N + b * BLK:N + (b + 1) * BLK]
 
-    at = parity * NX + x
-    l_ref[block(at), :] = own_l[...]
-    for b in range(8):
-        f_ref[b * BLK:(b + 1) * BLK, block(at)] = own_f[:, b * BLK:(b + 1) * BLK]
+    place(parity * NX + x, own, 8)
     place((1 - parity) * NX + x, q0, 8)
     for dx, even, odd in ((1, e1, o1), (2, e2, o2), (3, e3, o3)):
         place(lax.rem(x + dx, NX), even, 4)
@@ -182,23 +189,30 @@
         out_ref[tile(i), :] = dot(fm_ref[tile(i), :], f_ref[...], NT)
 
 
-def prepare_kernel(gt_next, fpack_next, gt_ref, left_ref, base_ref, fn_ref, gm_ref, h_ref):
+def base_kernel(fpack_next, gt_ref, base_ref, fn_ref, gm_ref, h_ref):
     x, parity, _ = here()
     places = rows_of(x, parity)
     unpack_upper(fn_ref, fpack_next)
     pick(gm_ref, 0, gt_ref, places)
-    pick(left_ref, 512, gt_next, places)
     pick(h_ref, 512, fn_ref, places)
     for i in range(2):
-        left_ref[tile(i), :] = dot(gm_ref[tile(i), :], gt_next[...], NN).astype(BF16)
         h_ref[tile(i), :] = dot(gm_ref[tile(i), :], fn_ref[...], NN).astype(BF16)
     for i in range(4):
         base_ref[tile(i), :] = dot(h_ref[tile(i), :], fn_ref[...], NT)
 
 
-def final_kernel(
+def left_kernel(gt_next, gt_ref, left_ref, gm_ref):
+    x, parity, _ = here()
+    places = rows_of(x, parity)
+    pick(gm_ref, 0, gt_ref, places)
+    pick(left_ref, 512, gt_next, places)
+    for i in range(2):
+        left_ref[tile(i), :] = dot(gm_ref[tile(i), :], gt_next[...], NN).astype(BF16)
+
+
+def sweep_kernel(
     to2, to1, to0, left_ref, base_ref, gt_next, gram_ref, gt_ref,
-    own_ref, a1_ref, a2_ref, a3_ref, var_ref, s_ref, x_ref, w_ref,
+    own_ref, a1_ref, a2_ref, a3_ref, var_ref, s_ref, w_ref, x_ref, d_ref,
 ):
     x, parity, group = here()
     places = rows_of(x, parity)
@@ -229,6 +243,18 @@
             x_ref[tile(i), :] = dot(w_ref[tile(i), :], s_ref[...], NN).astype(BF16)
         pick(x_ref, 512, s_ref, places)
 
+    row = lax.broadcasted_iota(jnp.int32, (BLK, BLK), 0)
+    col = lax.broadcasted_iota(jnp.int32, (BLK, BLK), 1)
+    d_ref[...] = jnp.zeros_like(d_ref)
+    for k, at in enumerate(places):
+        rows = slice(k * BLK, (k + 1) * BLK)
+        terms = x_ref[rows, :].astype(F32) * gt_ref[block(at), :].astype(F32)
+        total = jnp.sum(terms, axis=1, keepdims=True) + gram_ref[rows, block(at)]
+        diag = jnp.sum(jnp.where(row == col, total, 0.0), axis=0, keepdims=True)
+        d_ref[pl.ds(at, 1), :] = diag.astype(BF16).astype(F32)
+    for k in range(var_ref.shape[0]):
+        var_ref[k] = d_ref[...]
+
     outs = (own_ref, a1_ref, a2_ref, a3_ref)
     for i in range(2):
         strip = gram_ref[tile(i), :] + dot(x_ref[tile(i), :], gt_ref[...], NT)
@@ -237,98 +263,95 @@
         off = -dot(x_ref[tile(i + 2), :], gt_ref[...], NT)
         outs[2 * i][1] = off[:BLK].astype(BF16)
         outs[2 * i + 1][1] = off[BLK:].astype(BF16)
-    row = lax.broadcasted_iota(jnp.int32, (BLK, BLK), 0)
-    col = lax.broadcasted_iota(jnp.int32, (BLK, BLK), 1)
-    var_ref[...] = jnp.zeros_like(var_ref)
-    for k, at in enumerate(places):
-        square = outs[k][0, :, block(at)].astype(F32)
-        var_ref[pl.ds(at, 1), :] = jnp.sum(jnp.where(row == col, square, 0.0), axis=0, keepdims=True)
-
-
-def call(kernel, outs, scratch, flops, *args):
+
+
+def deliver_kernel(owner_ref, every_ref, own_ref, b1_ref, b2_ref, b3_ref, diag_ref, off_ref, owned_ref):
+    x, parity, group = here()
+    core = lax.rem(lax.axis_index("cfg"), 2)
+    tm = lax.axis_index("tm")
+
+    def by_core(rows):
+        return jnp.where(core == 0, rows[0], rows[1])
+
+    level = jnp.int32(0)
+    for t in range(TB):
+        level = jnp.where(group == t, by_core((ROW_OF[0][t] % 2, ROW_OF[1][t] % 2)), level)
+    across = (lax.div(x, 2) != core).astype(jnp.int32)
+    way = 2 * across + (parity != level).astype(jnp.int32)
+    for k, source in enumerate((own_ref, b1_ref, b2_ref, b3_ref)):
+        @pl.when(way == k)
+        def _():
+            diag_ref[...] = source[0]
+            off_ref[...] = source[1]
+
+    total = [jnp.zeros((8, BLK), F32) for _ in range(SLOTS)]
+    for t in range(TB):
+        first = by_core((ROW_OF[0][t], ROW_OF[1][t])) * NX + 2 * core
+        row = every_ref[first] + every_ref[first + 1]
+        rank = sum(
+            ((owner_ref[u] == owner_ref[t]).astype(jnp.int32) for u in range(t)), jnp.int32(0)
+        )
+        for k in range(SLOTS):
+            hit = jnp.logical_and(owner_ref[t] == tm, rank == k)
+            total[k] = total[k] + jnp.where(hit, row, 0.0)
+    for k in range(SLOTS):
+        for b in range(8):
+            owned_ref[k:k + 1, b * BLK:(b + 1) * BLK] = total[k][b:b + 1, :]
+
+
+def call(kernel, outs, scratch, flops, *args, scalars=0):
     vmem = pl.BlockSpec(memory_space=pltpu.VMEM)
+    smem = pl.BlockSpec(memory_space=pltpu.SMEM)
     moved = sum(a.size * a.dtype.itemsize for a in args)
     return pl.pallas_call(
         kernel,
         out_shape=[jax.ShapeDtypeStruct(s, d) for s, d in outs],
-        in_specs=[vmem] * len(args),
+        in_specs=[smem] * scalars + [vmem] * (len(args) - scalars),
         out_specs=[vmem] * len(outs),
-        scratch_shapes=[pltpu.VMEM(s, BF16) for s in scratch],
+        scratch_shapes=[pltpu.VMEM(s, d) for s, d in scratch],
         cost_estimate=pl.CostEstimate(flops=flops, bytes_accessed=moved, transcendentals=0),
         compiler_params=pltpu.CompilerParams(vmem_limit_bytes=24 * 1024 * 1024),
     )(*args)
 
 
 def sweep(linv, sub, owner):
-    core = lax.rem(lax.axis_index("cfg"), 2)
-    tm = lax.axis_index("tm")
-    x, y = lax.rem(tm, NX), lax.div(tm, NX)
     flops = 2 * N * N * N
-    square, packed, half = (N, N), (512, 1152), (512, N)
-
-    turned = linv.reshape(BLK, 8, BLK).transpose(2, 1, 0).reshape(BLK, N)
-    full = jnp.concatenate([sub, turned], 1)
-    short = full[:, :N + 512]
+    square, packed, half, tall = ((N, N), BF16), ((512, 1152), BF16), ((512, N), F32), ((N, N), F32)
+    part, strip, rows = ((512, N), BF16), ((2, BLK, N), BF16), ((BLK, N), BF16)
+    n_tm = lax.axis_size("tm")
+
+    full, short = call(
+        pack_kernel, [((BLK, 2 * N), BF16), ((BLK, N + 512), BF16)], [], flops // 64, linv, sub
+    )
     q0 = send(full, load_above)
     evens = [send(short, load_from(dx, 0)) for dx in (1, 2, 3)]
     odds = [send(full, load_from(dx, 1)) for dx in (1, 2, 3)]
     gt, ft, fpack, spack = call(
-        load_kernel,
-        [(square, BF16), (square, BF16), (packed, BF16), (packed, BF16)],
-        [square, square], 3 * flops, sub, turned, q0, *evens, *odds,
+        load_kernel, [square, square, packed, packed], [square, square], 3 * flops,
+        full, q0, *evens, *odds,
     )
     to2 = send(spack, replica_to(3, 2))
     gt_next = send(gt, replica_to(1, 0))
     f_next = send(fpack, replica_to(1, 0))
-    (second,) = call(step_kernel, [(packed, BF16)], [square, square], 2 * flops, to2, gt, ft)
+    (second,) = call(step_kernel, [packed], [square, square], 2 * flops, to2, gt, ft)
     to0 = send(second, replica_to(2, 0))
     to1 = send(second, replica_to(2, 1))
-    (gram,) = call(gram_kernel, [(half, F32)], [half], flops, ft)
-    left, base = call(
-        prepare_kernel, [(square, BF16), (square, F32)], [square, half, square],
-        2 * flops, gt_next, f_next, gt,
-    )
-    strip = (2, BLK, N)
+    (gram,) = call(gram_kernel, [half], [part], flops, ft)
+    (base,) = call(base_kernel, [tall], [square, part, square], 3 * flops, f_next, gt)
+    (left,) = call(left_kernel, [square], [part], flops, gt_next, gt)
     own, a1, a2, a3, var = call(
-        final_kernel,
-        [(strip, BF16)] * 4 + [((8, BLK), F32)],
-        [square, square, square],
-        4 * flops, to2, to1, to0, left, base, gt_next, gram, gt,
-    )
+        sweep_kernel, [strip] * 4 + [((n_tm, 8, BLK), F32)],
+        [square, square, square, ((8, BLK), F32)],
+        6 * flops, to2, to1, to0, left, base, gt_next, gram, gt,
+    )
+    every = lax.all_to_all(var, "tm", 0, 0, tiled=True)
     b1 = send(a1, spread(False, True))
     b3 = send(a3, spread(True, True))
     b2 = send(a2, spread(True, False))
-
-    n_tm = lax.axis_size("tm")
-    every = lax.all_to_all(
-        jnp.broadcast_to(var[None], (n_tm, 8, BLK)), "tm", 0, 0, tiled=True
-    )
-    every = every.reshape(2 * TB, NX, 8, BLK)
-    pair = jnp.stack([
-        jnp.where(core == 0, every[r0, 0] + every[r0, 1], every[r1, 2] + every[r1, 3])
-        for r0, r1 in zip(*ROW_OF)
-    ])
-    variances = pair.reshape(TB, N)
-
-    near = lax.div(x, 2) == core
-    row_of = sum(
-        jnp.where(lax.div(y, 2) == t, jnp.where(core == 0, ROW_OF[0][t], ROW_OF[1][t]), 0)
-        for t in range(TB)
-    )
-    level = y == row_of
-    rows = [
-        jnp.where(near, jnp.where(level, own[i], b1[i]), jnp.where(level, b2[i], b3[i]))
-        for i in range(2)
-    ]
-
-    positions = lax.broadcasted_iota(jnp.int32, (TB, TB), 1)
-    current = lax.broadcasted_iota(jnp.int32, (TB, TB), 0)
-    same_owner = owner[:, None] == owner[None, :]
-    rank = jnp.sum(jnp.where(same_owner & (positions < current), 1, 0), axis=1)
-    slot = lax.broadcasted_iota(jnp.int32, (SLOTS, TB), 0)
-    chosen = (owner[None, :] == tm) & (rank[None, :] == slot)
-    owned = jnp.sum(jnp.where(chosen[:, :, None], variances[None], 0.0), axis=1)
-    return rows[0], rows[1], owned
+    return call(
+        deliver_kernel, [rows, rows, ((SLOTS, N), F32)], [], flops // 64,
+        owner, every, own, b1, b2, b3, scalars=1,
+    )
 
 
 def solution(mesh):

time: 136 us -> 125 us (0.919)
  the two profiles are of different devices: /device:TPU:20 before, /device:TPU:8 now
where the time goes in v1:
time: 125 us
  blocking collectives  50.2 us (40%)
  starting transfers between devices  41.3 us (33%)
  Pallas kernels  24.3 us (19%)
  waiting for transfers between devices  5.94 us (5%)
  local copies, waits for them, and re-layouts  1.9 us (2%)
    all_to_all x1, blocking collectives, sweep(): every = lax.all_to_all(var, 'tm', 0, 0, tiled=True)  50.2 us
    ppermute x15, starting transfers between devices, send(): return lax.ppermute(value, AXES, route)  41.3 us
    pallas_call x8, Pallas kernels, call(): pl.pallas_call(kernel, out_shape=[jax.ShapeDtypeStruct(s, d) for s, d in...  24.3 us
    ppermute x15, waiting for transfers between devices, send(): return lax.ppermute(value, AXES, route)  5.94 us
  transfers between devices with their start and end apart: 15, of which 1 were waited for; matrix products, arithmetic and copies ran while one was open for 0% of the time, Pallas kernels for 9%

profile of v1, /device:TPU:8, one launch (start us, length us, event | category | flops | bytes accessed | tf_op | source)
XLA Modules:
  0.0 124.5 jit_solution(16666546148640217440)
XLA Ops:
  0.6 0.0 copy-start
  0.6 0.9 copy-done
  1.6 0.0 copy-start.1
  1.6 0.9 copy-done.1
  2.5 0.1 shard_map.58
  2.7 0.7 collective-permute-start.3
  3.4 0.7 collective-permute-start.2
  4.1 4.5 %collective-permute-start.6 = (bf16[128,2048]{1,0:T(8,128)(2,1)S(1)}, bf16[128,2048]{1,0:T(8,128)(2,1)S(1)}, u32[]{:S(2)}, u32[]{:S(2)}) collective-permute-start(bf16[128,2048]{1,0:T(8,128)(2,1)S(1)} %get-tuple-element.14.own), channel_id=1, source_target_pairs={{4,1},{7,0},{12,13},{15,12},{20,21},{23,20},{28,25},{31,24},{37,34... | collective-permute-start | bytes 1572872 | tf_op jit(solution)/shard_map/ppermute | solution.py:37
  8.6 0.7 collective-permute-start.5
  9.3 0.7 collective-permute-start.4
  10.0 0.0 collective-permute-done.3.e3
  10.0 26.7 %collective-permute-start = (bf16[128,2048]{1,0:T(8,128)(2,1)S(1)}, bf16[128,2048]{1,0:T(8,128)(2,1)S(1)}, u32[]{:S(2)}, u32[]{:S(2)}) collective-permute-start(bf16[128,2048]{1,0:T(8,128)(2,1)S(1)} %get-tuple-element.14.own), channel_id=1, source_target_pairs={{4,0},{5,1},{8,12},{9,13},{16,20},{17,21},{28,24},{29,25},{38,34},... | collective-permute-start | bytes 1572872 | tf_op jit(solution)/shard_map/ppermute | solution.py:37
  36.7 0.0 collective-permute-done.2.e2
  36.7 0.7 collective-permute-start.1
  37.4 0.0 collective-permute-done.1.e1
  37.4 0.0 collective-permute-done.6.o3
  37.5 0.0 collective-permute-done.5.o2
  37.5 0.0 collective-permute-done.4.o1
  37.5 5.9 %collective-permute-done.q0 = bf16[128,2048]{1,0:T(8,128)(2,1)S(1)} collective-permute-done((bf16[128,2048]{1,0:T(8,128)(2,1)S(1)}, bf16[128,2048]{1,0:T(8,128)(2,1)S(1)}, u32[]{:S(2)}, u32[]{:S(2)}) %collective-permute-start) | collective-permute-done | bytes 524320 | tf_op jit(solution)/shard_map/ppermute | solution.py:37
  43.4 4.3 %shard_map.59 = (bf16[1024,1024]{1,0:T(8,128)(2,1)S(1)}, bf16[1024,1024]{1,0:T(8,128)(2,1)S(1)}, bf16[512,1152]{1,0:T(8,128)(2,1)S(1)}, bf16[512,1152]{1,0:T(8,128)(2,1)S(1)}) custom-call(bf16[128,2048]{1,0:T(8,128)(2,1)S(1)} %get-tuple-element.14.own, bf16[128,2048]{1,0:T(8,128)(2,1)S(1)} %collective-permute-done.q0, ...), custom_call_target="tpu_custom_call" | custom-call | flops 6442450944 | bytes 3801088 | tf_op jit(solution)/shard_map/pallas_call | solution.py:306
  47.7 0.7 collective-permute-start.7
  48.4 0.8 collective-permute-start.10
  49.2 0.7 collective-permute-start.11
  50.0 0.0 collective-permute-done.7.pack_in.to2
  50.0 4.6 %shard_map.60 = bf16[512,1152]{1,0:T(8,128)(2,1)S(1)} custom-call(bf16[512,1152]{1,0:T(8,128)(2,1)S(1)} %collective-permute-done.7.pack_in.to2, bf16[1024,1024]{1,0:T(8,128)(2,1)S(1)} %get-tuple-element.17.gt_ref, bf16[1024,1024]{1,0:T(8,128)(2,1)S(1)} %get-tuple-element.18.f_ref), custom_call_target="tpu_custom_call" | custom-call | flops 4294967296 | bytes 5373952 | tf_op jit(solution)/shard_map/pallas_call | solution.py:306
  54.6 0.7 collective-permute-start.9
  55.4 0.9 collective-permute-start.8
  56.3 1.3 %shard_map.63.gram_ref = f32[512,1024]{1,0:T(8,128)S(1)} custom-call(bf16[1024,1024]{1,0:T(8,128)(2,1)S(1)} %get-tuple-element.18.f_ref), custom_call_target="tpu_custom_call" | custom-call | flops 2147483648 | bytes 2097152 | tf_op jit(solution)/shard_map/pallas_call | solution.py:306
  57.6 0.0 collective-permute-done.11.fpack_next
  57.6 3.5 %shard_map.62.base_ref = f32[1024,1024]{1,0:T(8,128)S(1)} custom-call(bf16[512,1152]{1,0:T(8,128)(2,1)S(1)} %collective-permute-done.11.fpack_next, bf16[1024,1024]{1,0:T(8,128)(2,1)S(1)} %get-tuple-element.17.gt_ref), custom_call_target="tpu_custom_call" | custom-call | flops 6442450944 | bytes 3276800 | tf_op jit(solution)/shard_map/pallas_call | solution.py:306
  61.1 0.0 collective-permute-done.10.gt_next
  61.1 1.3 %shard_map.61.left_ref = bf16[1024,1024]{1,0:T(8,128)(2,1)S(1)} custom-call(bf16[1024,1024]{1,0:T(8,128)(2,1)S(1)} %collective-permute-done.10.gt_next, bf16[1024,1024]{1,0:T(8,128)(2,1)S(1)} %get-tuple-element.17.gt_ref), custom_call_target="tpu_custom_call" | custom-call | flops 2147483648 | bytes 4194304 | tf_op jit(solution)/shard_map/pallas_call | solution.py:306
  62.4 0.0 copy-start.2
  62.4 0.0 collective-permute-done.9.to0
  62.4 0.0 collective-permute-done.8.to1
  62.5 7.7 %shard_map.64 = (bf16[2,128,1024]{2,1,0:T(8,128)(2,1)S(1)}, bf16[2,128,1024]{2,1,0:T(8,128)(2,1)S(1)}, bf16[2,128,1024]{2,1,0:T(8,128)(2,1)S(1)}, bf16[2,128,1024]{2,1,0:T(8,128)(2,1)S(1)}, f32[32,8,128]{2,1,0:T(8,128)S(1)}) custom-call(bf16[512,1152]{1,0:T(8,128)(2,1)S(1)} %collective-permute-done.7.pack_in.to2, ...), custom_call_target="tpu_custom_call" | custom-call | flops 12884901888 | bytes 16121856 | tf_op jit(solution)/shard_map/pallas_call | solution.py:306
  70.2 1.3 %collective-permute-start.12 = (bf16[2,128,1024]{2,1,0:T(8,128)(2,1)S(1)}, bf16[2,128,1024]{2,1,0:T(8,128)(2,1)S(1)}, u32[]{:S(2)}, u32[]{:S(2)}) collective-permute-start(bf16[2,128,1024]{2,1,0:T(8,128)(2,1)S(1)} %get-tuple-element.22), channel_id=1, source_target_pairs={{0,4},{1,5},{12,8},{13,9},{20,16},{21,17},{24,28},{25,29},{34,38},... | collective-permute-start | bytes 1572872 | tf_op jit(solution)/shard_map/ppermute | solution.py:37
  71.5 0.7 collective-permute-start.13
  72.2 0.7 collective-permute-start.14
  72.9 50.2 %all_to_all.5.every_ref = f32[32,8,128]{2,1,0:T(8,128)S(1)} all-to-all(f32[32,8,128]{2,1,0:T(8,128)S(1)} %get-tuple-element.20), channel_id=1, replica_groups=mesh['cfg'=16,'tm'=32] {'tm'}, dimensions={0} | all-to-all | bytes 262144 | tf_op jit(solution)/shard_map/all_to_all | solution.py:347
  123.1 0.0 collective-permute-done.12.b1_ref
  123.1 0.0 collective-permute-done.13.b2_ref
  123.1 0.0 collective-permute-done.14.b3_ref
  123.1 0.0 copy-done.2
  123.1 1.4 %shard_map.65 = (bf16[128,1024]{1,0:T(8,128)(2,1)}, bf16[128,1024]{1,0:T(8,128)(2,1)}, f32[2,1024]{1,0:T(2,128)}) custom-call(s32[4]{0:T(128)S(1)} %copy-done.2, f32[32,8,128]{2,1,0:T(8,128)S(1)} %all_to_all.5.every_ref, bf16[2,128,1024]{2,1,0:T(8,128)(2,1)S(1)} %get-tuple-element.21.own_ref, bf16[2,128,1024]{2,1,0:T(8,128)(2,1)S(1)} %collective-permute-done.12.b1_ref, ...), custom_call_target="tpu_custom_call" | custom-call | flops 33554432 | bytes 2228240 | tf_op jit(solution)/shard_map/pallas_call | solution.py:306
Async XLA Ops:
  0.6 1.0 copy-start
  1.6 0.9 copy-start.1
  2.7 7.3 %collective-permute-start.3 = (bf16[128,1536]{1,0:T(8,128)(2,1)S(1)}, bf16[128,1536]{1,0:T(8,128)(2,1)S(1)}, u32[]{:S(2)}, u32[]{:S(2)}) collective-permute-start(bf16[128,1536]{1,0:T(8,128)(2,1)S(1)} %get-tuple-element.15), channel_id=1, source_target_pairs={{0,1},{3,0},{8,13},{11,12},{16,21},{19,20},{24,25},{27,24},{33,34}... | collective-permute-start | bytes 1179656 | tf_op jit(solution)/shard_map/ppermute | solution.py:37
  3.4 33.4 %collective-permute-start.2 = (bf16[128,1536]{1,0:T(8,128)(2,1)S(1)}, bf16[128,1536]{1,0:T(8,128)(2,1)S(1)}, u32[]{:S(2)}, u32[]{:S(2)}) collective-permute-start(bf16[128,1536]{1,0:T(8,128)(2,1)S(1)} %get-tuple-element.15), channel_id=1, source_target_pairs={{2,0},{3,1},{10,12},{11,13},{18,20},{19,21},{26,24},{27,25},{32,34... | collective-permute-start | bytes 1179656 | tf_op jit(solution)/shard_map/ppermute | solution.py:37
  4.1 33.4 %collective-permute-start.6 = (bf16[128,2048]{1,0:T(8,128)(2,1)S(1)}, bf16[128,2048]{1,0:T(8,128)(2,1)S(1)}, u32[]{:S(2)}, u32[]{:S(2)}) collective-permute-start(bf16[128,2048]{1,0:T(8,128)(2,1)S(1)} %get-tuple-element.14.own), channel_id=1, source_target_pairs={{4,1},{7,0},{12,13},{15,12},{20,21},{23,20},{28,25},{31,24},{37,34... | collective-permute-start | bytes 1572872 | tf_op jit(solution)/shard_map/ppermute | solution.py:37
  8.6 28.9 %collective-permute-start.5 = (bf16[128,2048]{1,0:T(8,128)(2,1)S(1)}, bf16[128,2048]{1,0:T(8,128)(2,1)S(1)}, u32[]{:S(2)}, u32[]{:S(2)}) collective-permute-start(bf16[128,2048]{1,0:T(8,128)(2,1)S(1)} %get-tuple-element.14.own), channel_id=1, source_target_pairs={{6,0},{7,1},{14,12},{15,13},{22,20},{23,21},{30,24},{31,25},{36,34... | collective-permute-start | bytes 1572872 | tf_op jit(solution)/shard_map/ppermute | solution.py:37
  9.3 28.2 %collective-permute-start.4 = (bf16[128,2048]{1,0:T(8,128)(2,1)S(1)}, bf16[128,2048]{1,0:T(8,128)(2,1)S(1)}, u32[]{:S(2)}, u32[]{:S(2)}) collective-permute-start(bf16[128,2048]{1,0:T(8,128)(2,1)S(1)} %get-tuple-element.14.own), channel_id=1, source_target_pairs={{5,0},{6,1},{13,12},{14,13},{21,20},{22,21},{29,24},{30,25},{36,35... | collective-permute-start | bytes 1572872 | tf_op jit(solution)/shard_map/ppermute | solution.py:37
  10.0 33.4 %collective-permute-start = (bf16[128,2048]{1,0:T(8,128)(2,1)S(1)}, bf16[128,2048]{1,0:T(8,128)(2,1)S(1)}, u32[]{:S(2)}, u32[]{:S(2)}) collective-permute-start(bf16[128,2048]{1,0:T(8,128)(2,1)S(1)} %get-tuple-element.14.own), channel_id=1, source_target_pairs={{4,0},{5,1},{8,12},{9,13},{16,20},{17,21},{28,24},{29,25},{38,34},... | collective-permute-start | bytes 1572872 | tf_op jit(solution)/shard_map/ppermute | solution.py:37
  36.7 0.7 collective-permute-start.1
  47.7 2.3 %collective-permute-start.7 = (bf16[512,1152]{1,0:T(8,128)(2,1)S(1)}, bf16[512,1152]{1,0:T(8,128)(2,1)S(1)}, u32[]{:S(2)}, u32[]{:S(2)}) collective-permute-start(bf16[512,1152]{1,0:T(8,128)(2,1)S(1)} %get-tuple-element.16), channel_id=1, source_target_pairs={{24,20},{25,21},{62,54},{63,55},{88,84},{89,85},{126,118},{127,119... | collective-permute-start | bytes 3538952 | tf_op jit(solution)/shard_map/ppermute | solution.py:37
  48.4 12.7 %collective-permute-start.10 = (bf16[1024,1024]{1,0:T(8,128)(2,1)S(1)}, bf16[1024,1024]{1,0:T(8,128)(2,1)S(1)}, u32[]{:S(2)}, u32[]{:S(2)}) collective-permute-start(bf16[1024,1024]{1,0:T(8,128)(2,1)S(1)} %get-tuple-element.17.gt_ref), channel_id=1, source_target_pairs={{12,0},{13,1},{42,34},{43,35},{76,64},{77,65},{106,98},{107,99},{1... | collective-permute-start | bytes 6291464 | tf_op jit(solution)/shard_map/ppermute | solution.py:37
  49.2 8.4 %collective-permute-start.11 = (bf16[512,1152]{1,0:T(8,128)(2,1)S(1)}, bf16[512,1152]{1,0:T(8,128)(2,1)S(1)}, u32[]{:S(2)}, u32[]{:S(2)}) collective-permute-start(bf16[512,1152]{1,0:T(8,128)(2,1)S(1)} %get-tuple-element.19), channel_id=1, source_target_pairs={{12,0},{13,1},{42,34},{43,35},{76,64},{77,65},{106,98},{107,99},{1... | collective-permute-start | bytes 3538952 | tf_op jit(solution)/shard_map/ppermute | solution.py:37
  54.6 7.8 %collective-permute-start.9 = (bf16[512,1152]{1,0:T(8,128)(2,1)S(1)}, bf16[512,1152]{1,0:T(8,128)(2,1)S(1)}, u32[]{:S(2)}, u32[]{:S(2)}) collective-permute-start(bf16[512,1152]{1,0:T(8,128)(2,1)S(1)} %shard_map.60), channel_id=1, source_target_pairs={{20,0},{21,1},{54,34},{55,35},{84,64},{85,65},{118,98},{119,99},{1... | collective-permute-start | bytes 3538952 | tf_op jit(solution)/shard_map/ppermute | solution.py:37
  55.4 7.1 %collective-permute-start.8 = (bf16[512,1152]{1,0:T(8,128)(2,1)S(1)}, bf16[512,1152]{1,0:T(8,128)(2,1)S(1)}, u32[]{:S(2)}, u32[]{:S(2)}) collective-permute-start(bf16[512,1152]{1,0:T(8,128)(2,1)S(1)} %shard_map.60), channel_id=1, source_target_pairs={{20,12},{21,13},{54,42},{55,43},{84,76},{85,77},{118,106},{119,107... | collective-permute-start | bytes 3538952 | tf_op jit(solution)/shard_map/ppermute | solution.py:37
  62.4 60.7 %copy-start.2 = (s32[4]{0:T(128)S(1)}, s32[4]{0:T(128)}, u32[]{:S(2)}) copy-start(s32[4]{0:T(128)} %owner_ref.1) | copy-start | bytes 52
  70.2 52.9 %collective-permute-start.12 = (bf16[2,128,1024]{2,1,0:T(8,128)(2,1)S(1)}, bf16[2,128,1024]{2,1,0:T(8,128)(2,1)S(1)}, u32[]{:S(2)}, u32[]{:S(2)}) collective-permute-start(bf16[2,128,1024]{2,1,0:T(8,128)(2,1)S(1)} %get-tuple-element.22), channel_id=1, source_target_pairs={{0,4},{1,5},{12,8},{13,9},{20,16},{21,17},{24,28},{25,29},{34,38},... | collective-permute-start | bytes 1572872 | tf_op jit(solution)/shard_map/ppermute | solution.py:37
  71.5 51.6 %collective-permute-start.13 = (bf16[2,128,1024]{2,1,0:T(8,128)(2,1)S(1)}, bf16[2,128,1024]{2,1,0:T(8,128)(2,1)S(1)}, u32[]{:S(2)}, u32[]{:S(2)}) collective-permute-start(bf16[2,128,1024]{2,1,0:T(8,128)(2,1)S(1)} %get-tuple-element.23), channel_id=1, source_target_pairs={{0,3},{1,2},{12,15},{13,14},{20,23},{21,22},{24,27},{25,26},{34,33... | collective-permute-start | bytes 1572872 | tf_op jit(solution)/shard_map/ppermute | solution.py:37
  72.2 50.9 %collective-permute-start.14 = (bf16[2,128,1024]{2,1,0:T(8,128)(2,1)S(1)}, bf16[2,128,1024]{2,1,0:T(8,128)(2,1)S(1)}, u32[]{:S(2)}, u32[]{:S(2)}) collective-permute-start(bf16[2,128,1024]{2,1,0:T(8,128)(2,1)S(1)} %get-tuple-element.24), channel_id=1, source_target_pairs={{0,7},{1,6},{12,11},{13,10},{20,19},{21,18},{24,31},{25,30},{34,37... | collective-permute-start | bytes 1572872 | tf_op jit(solution)/shard_map/ppermute | solution.py:37

commit v2 on v1

--- a/solution.py
+++ b/solution.py
@@ -12,7 +12,7 @@
 N = 1024
 BLK = 128
 AXES = ("cfg", "tm")
-ROW_OF = ((0, 3, 5, 6), (0, 2, 5, 7))
+ROW_OF = ((0, 3, 5, 6), (0, 2, 4, 7))
 
 
 NN = (((1,), (0,)), ((), ()))
@@ -37,16 +37,23 @@
     return lax.ppermute(value, AXES, route)
 
 
-def load_from(dx, parity):
+def load_from(dx, parity, groups):
     def fn(x, y, core):
         to = (x - dx) % NX
-        return (to, ROW_OF[core][y // 2]) if y % 2 == parity and mine(to, core) else None
+        if y // 2 in groups and y % 2 == parity and mine(to, core):
+            return (to, ROW_OF[core][y // 2])
+        return None
 
     return fn
 
 
-def load_above(x, y, core):
-    return (x, y ^ 1) if mine(x, core) and y ^ 1 == ROW_OF[core][y // 2] else None
+def load_above(groups):
+    def fn(x, y, core):
+        if y // 2 in groups and mine(x, core) and y ^ 1 == ROW_OF[core][y // 2]:
+            return (x, y ^ 1)
+        return None
+
+    return fn
 
 
 def replica_to(t, u):
@@ -130,7 +137,15 @@
         s_ref[tile(i), cols] = (gram + dot(wt_ref[tile(i), :], gt_ref[cols, :], NT)).astype(BF16)
 
 
-def pack_kernel(linv_ref, sub_ref, full_ref, short_ref):
+def pack_kernel(linv_hbm, sub_hbm, full_ref, short_ref, linv_ref, sub_ref, sems):
+    copies = [
+        pltpu.make_async_copy(linv_hbm, linv_ref, sems.at[0]),
+        pltpu.make_async_copy(sub_hbm, sub_ref, sems.at[1]),
+    ]
+    for copy in copies:
+        copy.start()
+    for copy in copies:
+        copy.wait()
     full_ref[:, :N] = sub_ref[...]
     short_ref[:, :N] = sub_ref[...]
     for b in range(8):
@@ -140,7 +155,7 @@
             short_ref[:, N + b * BLK:N + (b + 1) * BLK] = turned
 
 
-def load_kernel(own, q0, e1, e2, e3, o1, o2, o3, gt_ref, f_ref, fpack_ref, spack_ref, l_ref, s_ref):
+def assemble(own, q0, e1, e2, e3, o1, o2, o3, f_ref, l_ref):
     x, parity, _ = here()
     f_ref[512:, :512] = jnp.zeros((512, 512), BF16)
 
@@ -154,11 +169,33 @@
     for dx, even, odd in ((1, e1, o1), (2, e2, o2), (3, e3, o3)):
         place(lax.rem(x + dx, NX), even, 4)
         place(NX + lax.rem(x + dx, NX), odd, 8)
+
+
+def couple(gt_ref, f_ref, l_ref):
     for i in range(4):
         gt_ref[tile(i), :] = dot(f_ref[tile(i), i * 256:], l_ref[:, i * 256:], NT).astype(BF16)
+
+
+def load_kernel(own, q0, e1, e2, e3, o1, o2, o3, gt_ref, f_ref, fpack_ref, spack_ref, l_ref, s_ref):
+    assemble(own, q0, e1, e2, e3, o1, o2, o3, f_ref, l_ref)
+    couple(gt_ref, f_ref, l_ref)
     lower(s_ref, f_ref, gt_ref, gt_ref)
     pack(spack_ref, s_ref)
     pack_upper(fpack_ref, f_ref)
+
+
+def late_kernel(own, q0, e1, e2, e3, o1, o2, o3, gt_in, f_in, gt_ref, f_ref, l_ref):
+    _, _, group = here()
+
+    @pl.when(group == 0)
+    def _():
+        assemble(own, q0, e1, e2, e3, o1, o2, o3, f_ref, l_ref)
+        couple(gt_ref, f_ref, l_ref)
+
+    @pl.when(group != 0)
+    def _():
+        gt_ref[...] = gt_in[...]
+        f_ref[...] = f_in[...]
 
 
 def step_kernel(pack_in, gt_ref, f_ref, pack_out, s_ref, wt_ref):
@@ -299,16 +336,15 @@
             owned_ref[k:k + 1, b * BLK:(b + 1) * BLK] = total[k][b:b + 1, :]
 
 
-def call(kernel, outs, scratch, flops, *args, scalars=0):
+def call(kernel, outs, scratch, flops, *args, first=pltpu.VMEM, special=0):
     vmem = pl.BlockSpec(memory_space=pltpu.VMEM)
-    smem = pl.BlockSpec(memory_space=pltpu.SMEM)
     moved = sum(a.size * a.dtype.itemsize for a in args)
     return pl.pallas_call(
         kernel,
         out_shape=[jax.ShapeDtypeStruct(s, d) for s, d in outs],
-        in_specs=[smem] * scalars + [vmem] * (len(args) - scalars),
+        in_specs=[pl.BlockSpec(memory_space=first)] * special + [vmem] * (len(args) - special),
         out_specs=[vmem] * len(outs),
-        scratch_shapes=[pltpu.VMEM(s, d) for s, d in scratch],
+        scratch_shapes=[pltpu.VMEM(*s) if isinstance(s, tuple) else s for s in scratch],
         cost_estimate=pl.CostEstimate(flops=flops, bytes_accessed=moved, transcendentals=0),
         compiler_params=pltpu.CompilerParams(vmem_limit_bytes=24 * 1024 * 1024),
     )(*args)
@@ -321,19 +357,27 @@
     n_tm = lax.axis_size("tm")
 
     full, short = call(
-        pack_kernel, [((BLK, 2 * N), BF16), ((BLK, N + 512), BF16)], [], flops // 64, linv, sub
-    )
-    q0 = send(full, load_above)
-    evens = [send(short, load_from(dx, 0)) for dx in (1, 2, 3)]
-    odds = [send(full, load_from(dx, 1)) for dx in (1, 2, 3)]
-    gt, ft, fpack, spack = call(
-        load_kernel, [square, square, packed, packed], [square, square], 3 * flops,
-        full, q0, *evens, *odds,
+        pack_kernel, [((BLK, 2 * N), BF16), ((BLK, N + 512), BF16)],
+        [rows, rows, pltpu.SemaphoreType.DMA((2,))], flops // 64, linv, sub,
+        first=pltpu.HBM, special=2,
+    )
+
+    def load(groups):
+        q0 = send(full, load_above(groups))
+        odds = [send(full, load_from(dx, 1, groups)) for dx in (1, 2, 3)]
+        evens = [send(short, load_from(dx, 0, groups)) for dx in (1, 2, 3)]
+        return (full, q0, *evens, *odds)
+
+    pieces = load((1, 2, 3))
+    gt_first, ft_first, fpack, spack = call(
+        load_kernel, [square, square, packed, packed], [square, square], 3 * flops, *pieces
     )
     to2 = send(spack, replica_to(3, 2))
-    gt_next = send(gt, replica_to(1, 0))
+    gt_next = send(gt_first, replica_to(1, 0))
     f_next = send(fpack, replica_to(1, 0))
-    (second,) = call(step_kernel, [packed], [square, square], 2 * flops, to2, gt, ft)
+    (second,) = call(step_kernel, [packed], [square, square], 2 * flops, to2, gt_first, ft_first)
+    pieces = load((0,))
+    gt, ft = call(late_kernel, [square, square], [square], flops, *pieces, gt_first, ft_first)
     to0 = send(second, replica_to(2, 0))
     to1 = send(second, replica_to(2, 1))
     (gram,) = call(gram_kernel, [half], [part], flops, ft)
@@ -350,7 +394,7 @@
     b2 = send(a2, spread(True, False))
     return call(
         deliver_kernel, [rows, rows, ((SLOTS, N), F32)], [], flops // 64,
-        owner, every, own, b1, b2, b3, scalars=1,
+        owner, every, own, b1, b2, b3, first=pltpu.SMEM, special=1,
     )
 
 

time: 125 us -> 146 us (1.17)
  waiting for transfers between devices: 5.94 us -> 32.5 us
  blocking collectives: 50.2 us -> 38.6 us
  starting transfers between devices: 41.3 us -> 45.6 us
  Pallas kernels: 24.3 us -> 26.3 us
    ppermute x15 -> x22, waiting for transfers between devices: 5.94 us -> 32.5 us  [send(): return lax.ppermute(value, AXES, route)]
    all_to_all x1, blocking collectives: 50.2 us -> 38.6 us  [sweep(): every = lax.all_to_all(var, 'tm', 0, 0, tiled=True)]
    ppermute x15 -> x22, starting transfers between devices: 41.3 us -> 45.6 us  [send(): return lax.ppermute(value, AXES, route)]
    pallas_call x8 -> x9, Pallas kernels: 24.3 us -> 26.3 us  [call(): pl.pallas_call(kernel, out_shape=[jax.ShapeDtypeStruct(s, d) for s, d in...]
  transfers between devices with their start and end apart: 15 -> 22, of which waited for: 1 -> 2; matrix products, arithmetic and copies ran while one was open for 0% -> 0% of each run, Pallas kernels for 9% -> 9%
where the time goes in v2:
time: 146 us
  starting transfers between devices  45.6 us (31%)
  blocking collectives  38.6 us (26%)
  waiting for transfers between devices  32.5 us (22%)
  Pallas kernels  26.3 us (18%)
  local copies, waits for them, and re-layouts  1.9 us (1%)
    ppermute x22, starting transfers between devices, send(): return lax.ppermute(value, AXES, route)  45.6 us
    all_to_all x1, blocking collectives, sweep(): every = lax.all_to_all(var, 'tm', 0, 0, tiled=True)  38.6 us
    ppermute x22, waiting for transfers between devices, send(): return lax.ppermute(value, AXES, route)  32.5 us
    pallas_call x9, Pallas kernels, call(): pl.pallas_call(kernel, out_shape=[jax.ShapeDtypeStruct(s, d) for s, d in...  26.3 us
  transfers between devices with their start and end apart: 22, of which 2 were waited for; matrix products, arithmetic and copies ran while one was open for 0% of the time, Pallas kernels for 9%

profile of v2, /device:TPU:8, one launch (start us, length us, event | category | flops | bytes accessed | tf_op | source)
XLA Modules:
  0.0 145.9 jit_solution(11704457525931362302)
XLA Ops:
  0.6 0.9 copy-done
  1.6 0.9 copy-done.1
  2.5 0.2 shard_map.58
  2.8 0.7 collective-permute-start.3
  3.4 0.7 collective-permute-start.2
  4.1 0.7 collective-permute-start.6
  4.8 0.7 collective-permute-start.5
  5.5 0.7 collective-permute-start.4
  6.3 0.7 collective-permute-start
  7.0 0.0 collective-permute-done.2.e2
  7.0 0.7 collective-permute-start.1
  7.7 0.0 collective-permute-done.6.o3
  7.7 0.0 collective-permute-done.5.o2
  7.7 4.3 %shard_map.59 = (bf16[1024,1024]{1,0:T(8,128)(2,1)S(1)}, bf16[1024,1024]{1,0:T(8,128)(2,1)S(1)}, bf16[512,1152]{1,0:T(8,128)(2,1)S(1)}, bf16[512,1152]{1,0:T(8,128)(2,1)S(1)}) custom-call(bf16[128,2048]{1,0:T(8,128)(2,1)S(1)} %get-tuple-element.16.own, bf16[128,2048]{1,0:T(8,128)(2,1)S(1)} %collective-permute-done.q0, ...), custom_call_target="tpu_custom_call" | custom-call | flops 6442450944 | bytes 3801088 | tf_op jit(solution)/shard_map/pallas_call | solution.py:342
  12.0 0.7 collective-permute-start.7
  12.7 0.7 collective-permute-start.14
  13.4 0.7 collective-permute-start.13
  14.1 0.8 collective-permute-start.10
  14.9 5.1 %collective-permute-start.17 = (bf16[128,2048]{1,0:T(8,128)(2,1)S(1)}, bf16[128,2048]{1,0:T(8,128)(2,1)S(1)}, u32[]{:S(2)}, u32[]{:S(2)}) collective-permute-start(bf16[128,2048]{1,0:T(8,128)(2,1)S(1)} %get-tuple-element.16.own), channel_id=1, source_target_pairs={{4,1},{7,0},{37,34},{38,35},{68,65},{71,64},{101,98},{102,99},{132... | collective-permute-start | bytes 1572872 | tf_op jit(solution)/shard_map/ppermute | solution.py:37
  20.0 0.0 collective-permute-done.14.e3
  20.0 0.7 collective-permute-start.12
  20.7 0.7 collective-permute-start.18
  21.5 0.7 collective-permute-start.16
  22.2 4.5 %collective-permute-done.17.o3 = bf16[128,2048]{1,0:T(8,128)(2,1)S(1)} collective-permute-done((bf16[128,2048]{1,0:T(8,128)(2,1)S(1)}, bf16[128,2048]{1,0:T(8,128)(2,1)S(1)}, u32[]{:S(2)}, u32[]{:S(2)}) %collective-permute-start.17) | collective-permute-done | bytes 524320 | tf_op jit(solution)/shard_map/ppermute | solution.py:37
  26.7 0.7 collective-permute-start.15
  27.4 0.0 collective-permute-done.7.pack_in.to2
  27.4 25.8 %collective-permute-start.11 = (bf16[128,2048]{1,0:T(8,128)(2,1)S(1)}, bf16[128,2048]{1,0:T(8,128)(2,1)S(1)}, u32[]{:S(2)}, u32[]{:S(2)}) collective-permute-start(bf16[128,2048]{1,0:T(8,128)(2,1)S(1)} %get-tuple-element.16.own), channel_id=1, source_target_pairs={{4,0},{5,1},{38,34},{39,35},{68,64},{69,65},{102,98},{103,99},{132... | collective-permute-start | bytes 1572872 | tf_op jit(solution)/shard_map/ppermute | solution.py:37
  53.2 4.6 %shard_map.60 = bf16[512,1152]{1,0:T(8,128)(2,1)S(1)} custom-call(bf16[512,1152]{1,0:T(8,128)(2,1)S(1)} %collective-permute-done.7.pack_in.to2, bf16[1024,1024]{1,0:T(8,128)(2,1)S(1)} %get-tuple-element.19.gt_ref.gt_in, bf16[1024,1024]{1,0:T(8,128)(2,1)S(1)} %get-tuple-element.20.f_ref.f_in), custom_call_target="tpu_custom_call" | custom-call | flops 4294967296 | bytes 5373952 | tf_op jit(solution)/shard_map/pallas_call | solution.py:342
  57.8 0.0 collective-permute-done.16.o2
  57.8 0.7 collective-permute-start.9
  58.6 0.0 collective-permute-done.15.o1
  58.6 0.7 collective-permute-start.8
  59.3 27.9 %collective-permute-done.11.q0 = bf16[128,2048]{1,0:T(8,128)(2,1)S(1)} collective-permute-done((bf16[128,2048]{1,0:T(8,128)(2,1)S(1)}, bf16[128,2048]{1,0:T(8,128)(2,1)S(1)}, u32[]{:S(2)}, u32[]{:S(2)}) %collective-permute-start.11) | collective-permute-done | bytes 524320 | tf_op jit(solution)/shard_map/ppermute | solution.py:37
  87.2 2.0 %shard_map.61 = (bf16[1024,1024]{1,0:T(8,128)(2,1)S(1)}, bf16[1024,1024]{1,0:T(8,128)(2,1)S(1)}) custom-call(bf16[128,2048]{1,0:T(8,128)(2,1)S(1)} %get-tuple-element.16.own, bf16[128,2048]{1,0:T(8,128)(2,1)S(1)} %collective-permute-done.11.q0, bf16[128,1536]{1,0:T(8,128)(2,1)S(1)} %collective-permute-done.12.e1, ...), custom_call_target="tpu_custom_call" | custom-call | flops 2147483648 | bytes 7995392 | tf_op jit(solution)/shard_map/pallas_call | solution.py:342
  89.2 1.3 shard_map.64.gram_ref
  90.5 0.0 collective-permute-done.18.fpack_next
  90.5 3.5 %shard_map.63.base_ref = f32[1024,1024]{1,0:T(8,128)S(1)} custom-call(bf16[512,1152]{1,0:T(8,128)(2,1)S(1)} %collective-permute-done.18.fpack_next, bf16[1024,1024]{1,0:T(8,128)(2,1)S(1)} %get-tuple-element.21.gt_ref), custom_call_target="tpu_custom_call" | custom-call | flops 6442450944 | bytes 3276800 | tf_op jit(solution)/shard_map/pallas_call | solution.py:342
  94.1 1.3 shard_map.62.left_ref
  95.3 0.0 copy-start.2
  95.4 0.0 collective-permute-done.9.to0
  95.4 7.7 %shard_map.65 = (bf16[2,128,1024]{2,1,0:T(8,128)(2,1)S(1)}, bf16[2,128,1024]{2,1,0:T(8,128)(2,1)S(1)}, bf16[2,128,1024]{2,1,0:T(8,128)(2,1)S(1)}, bf16[2,128,1024]{2,1,0:T(8,128)(2,1)S(1)}, f32[32,8,128]{2,1,0:T(8,128)S(1)}) custom-call(bf16[512,1152]{1,0:T(8,128)(2,1)S(1)} %collective-permute-done.7.pack_in.to2, ...), custom_call_target="tpu_custom_call" | custom-call | flops 12884901888 | bytes 16121856 | tf_op jit(solution)/shard_map/pallas_call | solution.py:342
  103.1 1.3 collective-permute-start.19
  104.4 0.7 collective-permute-start.20
  105.1 0.7 collective-permute-start.21
  105.8 38.6 %all_to_all.5.every_ref = f32[32,8,128]{2,1,0:T(8,128)S(1)} all-to-all(f32[32,8,128]{2,1,0:T(8,128)S(1)} %get-tuple-element.24), channel_id=1, replica_groups=mesh['cfg'=16,'tm'=32] {'tm'}, dimensions={0} | all-to-all | bytes 262144 | tf_op jit(solution)/shard_map/all_to_all | solution.py:391
  144.4 0.0 collective-permute-done.19.b1_ref
  144.5 0.0 collective-permute-done.20.b2_ref
  144.5 1.4 shard_map.66
  (12 shorter events, 0.0 us)
Async XLA Ops:
  0.6 1.0 copy-start
  1.6 0.9 copy-start.1
  2.8 3.5 %collective-permute-start.3 = (bf16[128,1536]{1,0:T(8,128)(2,1)S(1)}, bf16[128,1536]{1,0:T(8,128)(2,1)S(1)}, u32[]{:S(2)}, u32[]{:S(2)}) collective-permute-start(bf16[128,1536]{1,0:T(8,128)(2,1)S(1)} %get-tuple-element.17), channel_id=1, source_target_pairs={{8,13},{11,12},{16,21},{19,20},{24,25},{27,24},{41,42},{42,43},{49... | collective-permute-start | bytes 1179656 | tf_op jit(solution)/shard_map/ppermute | solution.py:37
  3.4 3.5 %collective-permute-start.2 = (bf16[128,1536]{1,0:T(8,128)(2,1)S(1)}, bf16[128,1536]{1,0:T(8,128)(2,1)S(1)}, u32[]{:S(2)}, u32[]{:S(2)}) collective-permute-start(bf16[128,1536]{1,0:T(8,128)(2,1)S(1)} %get-tuple-element.17), channel_id=1, source_target_pairs={{10,12},{11,13},{18,20},{19,21},{26,24},{27,25},{40,42},{41,43},{4... | collective-permute-start | bytes 1179656 | tf_op jit(solution)/shard_map/ppermute | solution.py:37
  4.1 3.5 %collective-permute-start.6 = (bf16[128,2048]{1,0:T(8,128)(2,1)S(1)}, bf16[128,2048]{1,0:T(8,128)(2,1)S(1)}, u32[]{:S(2)}, u32[]{:S(2)}) collective-permute-start(bf16[128,2048]{1,0:T(8,128)(2,1)S(1)} %get-tuple-element.16.own), channel_id=1, source_target_pairs={{12,13},{15,12},{20,21},{23,20},{28,25},{31,24},{45,42},{46,43},{5... | collective-permute-start | bytes 1572872 | tf_op jit(solution)/shard_map/ppermute | solution.py:37
  4.8 2.8 %collective-permute-start.5 = (bf16[128,2048]{1,0:T(8,128)(2,1)S(1)}, bf16[128,2048]{1,0:T(8,128)(2,1)S(1)}, u32[]{:S(2)}, u32[]{:S(2)}) collective-permute-start(bf16[128,2048]{1,0:T(8,128)(2,1)S(1)} %get-tuple-element.16.own), channel_id=1, source_target_pairs={{14,12},{15,13},{22,20},{23,21},{30,24},{31,25},{44,42},{45,43},{5... | collective-permute-start | bytes 1572872 | tf_op jit(solution)/shard_map/ppermute | solution.py:37
  5.5 2.2 %collective-permute-start.4 = (bf16[128,2048]{1,0:T(8,128)(2,1)S(1)}, bf16[128,2048]{1,0:T(8,128)(2,1)S(1)}, u32[]{:S(2)}, u32[]{:S(2)}) collective-permute-start(bf16[128,2048]{1,0:T(8,128)(2,1)S(1)} %get-tuple-element.16.own), channel_id=1, source_target_pairs={{13,12},{14,13},{21,20},{22,21},{29,24},{30,25},{44,43},{47,42},{5... | collective-permute-start | bytes 1572872 | tf_op jit(solution)/shard_map/ppermute | solution.py:37
  6.3 1.5 collective-permute-start
  7.0 0.7 collective-permute-start.1
  12.0 15.4 %collective-permute-start.7 = (bf16[512,1152]{1,0:T(8,128)(2,1)S(1)}, bf16[512,1152]{1,0:T(8,128)(2,1)S(1)}, u32[]{:S(2)}, u32[]{:S(2)}) collective-permute-start(bf16[512,1152]{1,0:T(8,128)(2,1)S(1)} %get-tuple-element.18), channel_id=1, source_target_pairs={{24,20},{25,21},{62,50},{63,51},{88,84},{89,85},{126,114},{127,115... | collective-permute-start | bytes 3538952 | tf_op jit(solution)/shard_map/ppermute | solution.py:37
  12.7 7.3 %collective-permute-start.14 = (bf16[128,1536]{1,0:T(8,128)(2,1)S(1)}, bf16[128,1536]{1,0:T(8,128)(2,1)S(1)}, u32[]{:S(2)}, u32[]{:S(2)}) collective-permute-start(bf16[128,1536]{1,0:T(8,128)(2,1)S(1)} %get-tuple-element.17), channel_id=1, source_target_pairs={{0,1},{3,0},{33,34},{34,35},{64,65},{67,64},{97,98},{98,99},{128,1... | collective-permute-start | bytes 1179656 | tf_op jit(solution)/shard_map/ppermute | solution.py:37
  13.4 7.3 %collective-permute-start.13 = (bf16[128,1536]{1,0:T(8,128)(2,1)S(1)}, bf16[128,1536]{1,0:T(8,128)(2,1)S(1)}, u32[]{:S(2)}, u32[]{:S(2)}) collective-permute-start(bf16[128,1536]{1,0:T(8,128)(2,1)S(1)} %get-tuple-element.17), channel_id=1, source_target_pairs={{2,0},{3,1},{32,34},{33,35},{66,64},{67,65},{96,98},{97,99},{130,1... | collective-permute-start | bytes 1179656 | tf_op jit(solution)/shard_map/ppermute | solution.py:37
  14.1 79.9 %collective-permute-start.10 = (bf16[1024,1024]{1,0:T(8,128)(2,1)S(1)}, bf16[1024,1024]{1,0:T(8,128)(2,1)S(1)}, u32[]{:S(2)}, u32[]{:S(2)}) collective-permute-start(bf16[1024,1024]{1,0:T(8,128)(2,1)S(1)} %get-tuple-element.19.gt_ref.gt_in), channel_id=1, source_target_pairs={{12,0},{13,1},{42,34},{43,35},{76,64},{77,65},{106,98},{107,99},{1... | collective-permute-start | bytes 6291464 | tf_op jit(solution)/shard_map/ppermute | solution.py:37
  14.9 11.8 %collective-permute-start.17 = (bf16[128,2048]{1,0:T(8,128)(2,1)S(1)}, bf16[128,2048]{1,0:T(8,128)(2,1)S(1)}, u32[]{:S(2)}, u32[]{:S(2)}) collective-permute-start(bf16[128,2048]{1,0:T(8,128)(2,1)S(1)} %get-tuple-element.16.own), channel_id=1, source_target_pairs={{4,1},{7,0},{37,34},{38,35},{68,65},{71,64},{101,98},{102,99},{132... | collective-permute-start | bytes 1572872 | tf_op jit(solution)/shard_map/ppermute | solution.py:37
  20.0 1.5 collective-permute-start.12
  20.7 69.8 %collective-permute-start.18 = (bf16[512,1152]{1,0:T(8,128)(2,1)S(1)}, bf16[512,1152]{1,0:T(8,128)(2,1)S(1)}, u32[]{:S(2)}, u32[]{:S(2)}) collective-permute-start(bf16[512,1152]{1,0:T(8,128)(2,1)S(1)} %get-tuple-element.22), channel_id=1, source_target_pairs={{12,0},{13,1},{42,34},{43,35},{76,64},{77,65},{106,98},{107,99},{1... | collective-permute-start | bytes 3538952 | tf_op jit(solution)/shard_map/ppermute | solution.py:37
  21.5 36.4 %collective-permute-start.16 = (bf16[128,2048]{1,0:T(8,128)(2,1)S(1)}, bf16[128,2048]{1,0:T(8,128)(2,1)S(1)}, u32[]{:S(2)}, u32[]{:S(2)}) collective-permute-start(bf16[128,2048]{1,0:T(8,128)(2,1)S(1)} %get-tuple-element.16.own), channel_id=1, source_target_pairs={{6,0},{7,1},{36,34},{37,35},{70,64},{71,65},{100,98},{101,99},{134... | collective-permute-start | bytes 1572872 | tf_op jit(solution)/shard_map/ppermute | solution.py:37
  26.7 31.9 %collective-permute-start.15 = (bf16[128,2048]{1,0:T(8,128)(2,1)S(1)}, bf16[128,2048]{1,0:T(8,128)(2,1)S(1)}, u32[]{:S(2)}, u32[]{:S(2)}) collective-permute-start(bf16[128,2048]{1,0:T(8,128)(2,1)S(1)} %get-tuple-element.16.own), channel_id=1, source_target_pairs={{5,0},{6,1},{36,35},{39,34},{69,64},{70,65},{100,99},{103,98},{133... | collective-permute-start | bytes 1572872 | tf_op jit(solution)/shard_map/ppermute | solution.py:37
  27.4 59.8 %collective-permute-start.11 = (bf16[128,2048]{1,0:T(8,128)(2,1)S(1)}, bf16[128,2048]{1,0:T(8,128)(2,1)S(1)}, u32[]{:S(2)}, u32[]{:S(2)}) collective-permute-start(bf16[128,2048]{1,0:T(8,128)(2,1)S(1)} %get-tuple-element.16.own), channel_id=1, source_target_pairs={{4,0},{5,1},{38,34},{39,35},{68,64},{69,65},{102,98},{103,99},{132... | collective-permute-start | bytes 1572872 | tf_op jit(solution)/shard_map/ppermute | solution.py:37
  57.8 37.5 %collective-permute-start.9 = (bf16[512,1152]{1,0:T(8,128)(2,1)S(1)}, bf16[512,1152]{1,0:T(8,128)(2,1)S(1)}, u32[]{:S(2)}, u32[]{:S(2)}) collective-permute-start(bf16[512,1152]{1,0:T(8,128)(2,1)S(1)} %shard_map.60), channel_id=1, source_target_pairs={{20,0},{21,1},{50,34},{51,35},{84,64},{85,65},{114,98},{115,99},{1... | collective-permute-start | bytes 3538952 | tf_op jit(solution)/shard_map/ppermute | solution.py:37
  58.6 36.8 %collective-permute-start.8 = (bf16[512,1152]{1,0:T(8,128)(2,1)S(1)}, bf16[512,1152]{1,0:T(8,128)(2,1)S(1)}, u32[]{:S(2)}, u32[]{:S(2)}) collective-permute-start(bf16[512,1152]{1,0:T(8,128)(2,1)S(1)} %shard_map.60), channel_id=1, source_target_pairs={{20,12},{21,13},{50,42},{51,43},{84,76},{85,77},{114,106},{115,107... | collective-permute-start | bytes 3538952 | tf_op jit(solution)/shard_map/ppermute | solution.py:37
  95.3 49.1 %copy-start.2 = (s32[4]{0:T(128)S(1)}, s32[4]{0:T(128)}, u32[]{:S(2)}) copy-start(s32[4]{0:T(128)} %owner_ref.1) | copy-start | bytes 52
  103.1 41.3 %collective-permute-start.19 = (bf16[2,128,1024]{2,1,0:T(8,128)(2,1)S(1)}, bf16[2,128,1024]{2,1,0:T(8,128)(2,1)S(1)}, u32[]{:S(2)}, u32[]{:S(2)}) collective-permute-start(bf16[2,128,1024]{2,1,0:T(8,128)(2,1)S(1)} %get-tuple-element.26), channel_id=1, source_target_pairs={{0,4},{1,5},{12,8},{13,9},{20,16},{21,17},{24,28},{25,29},{34,38},... | collective-permute-start | bytes 1572872 | tf_op jit(solution)/shard_map/ppermute | solution.py:37
  104.4 40.0 %collective-permute-start.20 = (bf16[2,128,1024]{2,1,0:T(8,128)(2,1)S(1)}, bf16[2,128,1024]{2,1,0:T(8,128)(2,1)S(1)}, u32[]{:S(2)}, u32[]{:S(2)}) collective-permute-start(bf16[2,128,1024]{2,1,0:T(8,128)(2,1)S(1)} %get-tuple-element.27), channel_id=1, source_target_pairs={{0,3},{1,2},{12,15},{13,14},{20,23},{21,22},{24,27},{25,26},{34,33... | collective-permute-start | bytes 1572872 | tf_op jit(solution)/shard_map/ppermute | solution.py:37
  105.1 39.3 %collective-permute-start.21 = (bf16[2,128,1024]{2,1,0:T(8,128)(2,1)S(1)}, bf16[2,128,1024]{2,1,0:T(8,128)(2,1)S(1)}, u32[]{:S(2)}, u32[]{:S(2)}) collective-permute-start(bf16[2,128,1024]{2,1,0:T(8,128)(2,1)S(1)} %get-tuple-element.28), channel_id=1, source_target_pairs={{0,7},{1,6},{12,11},{13,10},{20,19},{21,18},{24,31},{25,30},{34,37... | collective-permute-start | bytes 1572872 | tf_op jit(solution)/shard_map/ppermute | solution.py:37

commit v3 on v2

--- a/solution.py
+++ b/solution.py
@@ -43,6 +43,18 @@
         if y // 2 in groups and y % 2 == parity and mine(to, core):
             return (to, ROW_OF[core][y // 2])
         return None
+
+    return fn
+
+
+def late_above(x, y, core):
+    return (x, 0) if y == 1 else None
+
+
+def late_from(dx):
+    def fn(x, y, core):
+        to = (x - dx) % NX
+        return (to, 0) if y == 0 and mine(to, core) else None
 
     return fn
 
@@ -155,25 +167,31 @@
             short_ref[:, N + b * BLK:N + (b + 1) * BLK] = turned
 
 
+def place(at, piece, blocks, f_ref, l_ref):
+    l_ref[block(at), :] = piece[:, :N]
+    for b in range(blocks):
+        f_ref[b * BLK:(b + 1) * BLK, block(at)] = piece[:, N + b * BLK:N + (b + 1) * BLK]
+
+
 def assemble(own, q0, e1, e2, e3, o1, o2, o3, f_ref, l_ref):
     x, parity, _ = here()
     f_ref[512:, :512] = jnp.zeros((512, 512), BF16)
 
-    def place(at, piece, blocks):
-        l_ref[block(at), :] = piece[:, :N]
-        for b in range(blocks):
-            f_ref[b * BLK:(b + 1) * BLK, block(at)] = piece[:, N + b * BLK:N + (b + 1) * BLK]
-
-    place(parity * NX + x, own, 8)
-    place((1 - parity) * NX + x, q0, 8)
+    place(parity * NX + x, own, 8, f_ref, l_ref)
+    place((1 - parity) * NX + x, q0, 8, f_ref, l_ref)
     for dx, even, odd in ((1, e1, o1), (2, e2, o2), (3, e3, o3)):
-        place(lax.rem(x + dx, NX), even, 4)
-        place(NX + lax.rem(x + dx, NX), odd, 8)
+        place(lax.rem(x + dx, NX), even, 4, f_ref, l_ref)
+        place(NX + lax.rem(x + dx, NX), odd, 8, f_ref, l_ref)
 
 
 def couple(gt_ref, f_ref, l_ref):
     for i in range(4):
         gt_ref[tile(i), :] = dot(f_ref[tile(i), i * 256:], l_ref[:, i * 256:], NT).astype(BF16)
+
+
+def join_kernel(short_ref, full_ref, out_ref):
+    out_ref[:, :N + 512] = short_ref[...]
+    out_ref[:, N + 512:] = full_ref[...]
 
 
 def load_kernel(own, q0, e1, e2, e3, o1, o2, o3, gt_ref, f_ref, fpack_ref, spack_ref, l_ref, s_ref):
@@ -184,12 +202,16 @@
     pack_upper(fpack_ref, f_ref)
 
 
-def late_kernel(own, q0, e1, e2, e3, o1, o2, o3, gt_in, f_in, gt_ref, f_ref, l_ref):
-    _, _, group = here()
+def late_kernel(j0, j1, j2, j3, gt_in, f_in, gt_ref, f_ref, l_ref):
+    x, _, group = here()
 
     @pl.when(group == 0)
     def _():
-        assemble(own, q0, e1, e2, e3, o1, o2, o3, f_ref, l_ref)
+        f_ref[512:, :512] = jnp.zeros((512, 512), BF16)
+        for dx, piece in enumerate((j0, j1, j2, j3)):
+            at = lax.rem(x + dx, NX)
+            place(at, piece[:, :N + 512], 4, f_ref, l_ref)
+            place(NX + at, piece[:, N + 512:], 8, f_ref, l_ref)
         couple(gt_ref, f_ref, l_ref)
 
     @pl.when(group != 0)
@@ -369,6 +391,7 @@
         return (full, q0, *evens, *odds)
 
     pieces = load((1, 2, 3))
+    above = send(full, late_above)
     gt_first, ft_first, fpack, spack = call(
         load_kernel, [square, square, packed, packed], [square, square], 3 * flops, *pieces
     )
@@ -376,7 +399,8 @@
     gt_next = send(gt_first, replica_to(1, 0))
     f_next = send(fpack, replica_to(1, 0))
     (second,) = call(step_kernel, [packed], [square, square], 2 * flops, to2, gt_first, ft_first)
-    pieces = load((0,))
+    (joined,) = call(join_kernel, [((BLK, 3 * N + 512), BF16)], [], flops // 64, short, above)
+    pieces = [joined] + [send(joined, late_from(dx)) for dx in (1, 2, 3)]
     gt, ft = call(late_kernel, [square, square], [square], flops, *pieces, gt_first, ft_first)
     to0 = send(second, replica_to(2, 0))
     to1 = send(second, replica_to(2, 1))

time: 146 us -> 118 us (0.81)
  the two profiles are of different devices: /device:TPU:8 before, /device:TPU:401 now
where the time goes in v3:
time: 118 us; the launch traced here: 117 us
  blocking collectives  47.7 us (40%)
  waiting for transfers between devices  24.4 us (21%)
  Pallas kernels  21.6 us (18%)
  starting transfers between devices  20.9 us (18%)
  local copies, waits for them, and re-layouts  1.9 us (2%)
    all_to_all x1, blocking collectives, sweep(): every = lax.all_to_all(var, 'tm', 0, 0, tiled=True)  47.7 us
    ppermute x19, waiting for transfers between devices, send(): return lax.ppermute(value, AXES, route)  24.4 us
    pallas_call x10, Pallas kernels, call(): pl.pallas_call(kernel, out_shape=[jax.ShapeDtypeStruct(s, d) for s, d in...  21.6 us
    ppermute x19, starting transfers between devices, send(): return lax.ppermute(value, AXES, route)  20.9 us
  transfers between devices with their start and end apart: 19, of which 2 were waited for; matrix products, arithmetic and copies ran while one was open for 0% of the time, Pallas kernels for 10%

profile of v3, /device:TPU:401, one launch (start us, length us, event | category | flops | bytes accessed | tf_op | source)
XLA Modules:
  0.0 117.4 jit_solution(15995902766707719093)
XLA Ops:
  0.6 0.9 copy-done
  1.6 0.9 copy-done.1
  2.5 0.2 shard_map.58
  2.8 0.7 collective-permute-start.3
  3.4 6.8 %collective-permute-start.2 = (bf16[128,1536]{1,0:T(8,128)(2,1)S(1)}, bf16[128,1536]{1,0:T(8,128)(2,1)S(1)}, u32[]{:S(2)}, u32[]{:S(2)}) collective-permute-start(bf16[128,1536]{1,0:T(8,128)(2,1)S(1)} %get-tuple-element.17.short_ref), channel_id=1, source_target_pairs={{10,12},{11,13},{18,20},{19,21},{26,24},{27,25},{40,42},{41,43},{4... | collective-permute-start | bytes 1179656 | tf_op jit(solution)/shard_map/ppermute | solution.py:37
  10.3 0.7 collective-permute-start.6
  11.0 0.7 collective-permute-start.5
  11.7 0.7 collective-permute-start.4
  12.4 0.0 collective-permute-done.3.e3
  12.4 0.7 collective-permute-start
  13.1 13.0 %collective-permute-done.2.e2 = bf16[128,1536]{1,0:T(8,128)(2,1)S(1)} collective-permute-done((bf16[128,1536]{1,0:T(8,128)(2,1)S(1)}, bf16[128,1536]{1,0:T(8,128)(2,1)S(1)}, u32[]{:S(2)}, u32[]{:S(2)}) %collective-permute-start.2) | collective-permute-done | bytes 393248 | tf_op jit(solution)/shard_map/ppermute | solution.py:37
  26.1 1.3 %collective-permute-start.1 = (bf16[128,1536]{1,0:T(8,128)(2,1)S(1)}, bf16[128,1536]{1,0:T(8,128)(2,1)S(1)}, u32[]{:S(2)}, u32[]{:S(2)}) collective-permute-start(bf16[128,1536]{1,0:T(8,128)(2,1)S(1)} %get-tuple-element.17.short_ref), channel_id=1, source_target_pairs={{9,12},{10,13},{17,20},{18,21},{25,24},{26,25},{40,43},{43,42},{48... | collective-permute-start | bytes 1179656 | tf_op jit(solution)/shard_map/ppermute | solution.py:37
  27.4 11.3 %collective-permute-done.1.e1 = bf16[128,1536]{1,0:T(8,128)(2,1)S(1)} collective-permute-done((bf16[128,1536]{1,0:T(8,128)(2,1)S(1)}, bf16[128,1536]{1,0:T(8,128)(2,1)S(1)}, u32[]{:S(2)}, u32[]{:S(2)}) %collective-permute-start.1) | collective-permute-done | bytes 393248 | tf_op jit(solution)/shard_map/ppermute | solution.py:37
  38.7 0.0 collective-permute-done.6.o3
  38.7 0.0 collective-permute-done.5.o2
  38.7 0.0 collective-permute-done.4.o1
  38.7 0.0 collective-permute-done.q0
  38.7 4.3 %shard_map.59 = (bf16[1024,1024]{1,0:T(8,128)(2,1)S(1)}, bf16[1024,1024]{1,0:T(8,128)(2,1)S(1)}, bf16[512,1152]{1,0:T(8,128)(2,1)S(1)}, bf16[512,1152]{1,0:T(8,128)(2,1)S(1)}) custom-call(bf16[128,2048]{1,0:T(8,128)(2,1)S(1)} %get-tuple-element.16.own, bf16[128,2048]{1,0:T(8,128)(2,1)S(1)} %collective-permute-done.q0, ...), custom_call_target="tpu_custom_call" | custom-call | flops 6442450944 | bytes 3801088 | tf_op jit(solution)/shard_map/pallas_call | solution.py:364
  43.0 0.7 collective-permute-start.7
  43.8 0.7 collective-permute-start.11
  44.5 0.8 collective-permute-start.10
  45.3 0.0 collective-permute-done.11.full_ref
  45.3 0.1 shard_map.61.j0
  45.4 0.7 collective-permute-start.14
  46.1 0.7 collective-permute-start.13
  46.8 0.7 collective-permute-start.12
  47.6 0.0 collective-permute-done.7.pack_in.to2
  47.6 0.7 collective-permute-start.15
  48.3 4.6 %shard_map.60 = bf16[512,1152]{1,0:T(8,128)(2,1)S(1)} custom-call(bf16[512,1152]{1,0:T(8,128)(2,1)S(1)} %collective-permute-done.7.pack_in.to2, bf16[1024,1024]{1,0:T(8,128)(2,1)S(1)} %get-tuple-element.19.gt_ref.gt_in, bf16[1024,1024]{1,0:T(8,128)(2,1)S(1)} %get-tuple-element.20.f_ref.f_in), custom_call_target="tpu_custom_call" | custom-call | flops 4294967296 | bytes 5373952 | tf_op jit(solution)/shard_map/pallas_call | solution.py:364
  52.9 0.0 collective-permute-done.14.j3
  52.9 0.7 collective-permute-start.9
  53.7 0.0 collective-permute-done.13.j2
  53.7 0.7 collective-permute-start.8
  54.4 0.5 shard_map.62
  54.9 1.3 %shard_map.65.gram_ref = f32[512,1024]{1,0:T(8,128)S(1)} custom-call(bf16[1024,1024]{1,0:T(8,128)(2,1)S(1)} %get-tuple-element.23.f_ref), custom_call_target="tpu_custom_call" | custom-call | flops 2147483648 | bytes 2097152 | tf_op jit(solution)/shard_map/pallas_call | solution.py:364
  56.2 3.5 %shard_map.64.base_ref = f32[1024,1024]{1,0:T(8,128)S(1)} custom-call(bf16[512,1152]{1,0:T(8,128)(2,1)S(1)} %collective-permute-done.15.fpack_next, bf16[1024,1024]{1,0:T(8,128)(2,1)S(1)} %get-tuple-element.21.gt_ref), custom_call_target="tpu_custom_call" | custom-call | flops 6442450944 | bytes 3276800 | tf_op jit(solution)/shard_map/pallas_call | solution.py:364
  59.8 1.3 %shard_map.63.left_ref = bf16[1024,1024]{1,0:T(8,128)(2,1)S(1)} custom-call(bf16[1024,1024]{1,0:T(8,128)(2,1)S(1)} %collective-permute-done.10.gt_next, bf16[1024,1024]{1,0:T(8,128)(2,1)S(1)} %get-tuple-element.21.gt_ref), custom_call_target="tpu_custom_call" | custom-call | flops 2147483648 | bytes 4194304 | tf_op jit(solution)/shard_map/pallas_call | solution.py:364
  61.1 0.0 copy-start.2
  61.1 0.0 collective-permute-done.8.to1
  61.1 4.5 %shard_map.66 = (bf16[2,128,1024]{2,1,0:T(8,128)(2,1)S(1)}, bf16[2,128,1024]{2,1,0:T(8,128)(2,1)S(1)}, bf16[2,128,1024]{2,1,0:T(8,128)(2,1)S(1)}, bf16[2,128,1024]{2,1,0:T(8,128)(2,1)S(1)}, f32[32,8,128]{2,1,0:T(8,128)S(1)}) custom-call(bf16[512,1152]{1,0:T(8,128)(2,1)S(1)} %collective-permute-done.7.pack_in.to2, ...), custom_call_target="tpu_custom_call" | custom-call | flops 12884901888 | bytes 16121856 | tf_op jit(solution)/shard_map/pallas_call | solution.py:364
  65.6 0.7 collective-permute-start.16
  66.3 1.3 %collective-permute-start.17 = (bf16[2,128,1024]{2,1,0:T(8,128)(2,1)S(1)}, bf16[2,128,1024]{2,1,0:T(8,128)(2,1)S(1)}, u32[]{:S(2)}, u32[]{:S(2)}) collective-permute-start(bf16[2,128,1024]{2,1,0:T(8,128)(2,1)S(1)} %get-tuple-element.27), channel_id=1, source_target_pairs={{0,3},{1,2},{12,15},{13,14},{20,23},{21,22},{24,27},{25,26},{34,33... | collective-permute-start | bytes 1572872 | tf_op jit(solution)/shard_map/ppermute | solution.py:37
  67.6 0.7 collective-permute-start.18
  68.3 47.7 %all_to_all.5.every_ref = f32[32,8,128]{2,1,0:T(8,128)S(1)} all-to-all(f32[32,8,128]{2,1,0:T(8,128)S(1)} %get-tuple-element.24), channel_id=1, replica_groups=mesh['cfg'=16,'tm'=32] {'tm'}, dimensions={0} | all-to-all | bytes 262144 | tf_op jit(solution)/shard_map/all_to_all | solution.py:415
  115.9 0.0 collective-permute-done.16.b1_ref
  116.0 0.0 collective-permute-done.17.b2_ref
  116.0 0.0 collective-permute-done.18.b3_ref
  116.0 1.4 %shard_map.67 = (bf16[128,1024]{1,0:T(8,128)(2,1)}, bf16[128,1024]{1,0:T(8,128)(2,1)}, f32[2,1024]{1,0:T(2,128)}) custom-call(s32[4]{0:T(128)S(1)} %copy-done.2, f32[32,8,128]{2,1,0:T(8,128)S(1)} %all_to_all.5.every_ref, bf16[2,128,1024]{2,1,0:T(8,128)(2,1)S(1)} %get-tuple-element.25.own_ref, bf16[2,128,1024]{2,1,0:T(8,128)(2,1)S(1)} %collective-permute-done.16.b1_ref, ...), custom_call_target="tpu_custom_call" | custom-call | flops 33554432 | bytes 2228240 | tf_op jit(solution)/shard_map/pallas_call | solution.py:364
  (7 shorter events, 0.0 us)
Async XLA Ops:
  0.6 1.0 copy-start
  1.6 0.9 copy-start.1
  2.8 9.6 %collective-permute-start.3 = (bf16[128,1536]{1,0:T(8,128)(2,1)S(1)}, bf16[128,1536]{1,0:T(8,128)(2,1)S(1)}, u32[]{:S(2)}, u32[]{:S(2)}) collective-permute-start(bf16[128,1536]{1,0:T(8,128)(2,1)S(1)} %get-tuple-element.17.short_ref), channel_id=1, source_target_pairs={{8,13},{11,12},{16,21},{19,20},{24,25},{27,24},{41,42},{42,43},{49... | collective-permute-start | bytes 1179656 | tf_op jit(solution)/shard_map/ppermute | solution.py:37
  3.4 22.7 %collective-permute-start.2 = (bf16[128,1536]{1,0:T(8,128)(2,1)S(1)}, bf16[128,1536]{1,0:T(8,128)(2,1)S(1)}, u32[]{:S(2)}, u32[]{:S(2)}) collective-permute-start(bf16[128,1536]{1,0:T(8,128)(2,1)S(1)} %get-tuple-element.17.short_ref), channel_id=1, source_target_pairs={{10,12},{11,13},{18,20},{19,21},{26,24},{27,25},{40,42},{41,43},{4... | collective-permute-start | bytes 1179656 | tf_op jit(solution)/shard_map/ppermute | solution.py:37
  10.3 28.5 %collective-permute-start.6 = (bf16[128,2048]{1,0:T(8,128)(2,1)S(1)}, bf16[128,2048]{1,0:T(8,128)(2,1)S(1)}, u32[]{:S(2)}, u32[]{:S(2)}) collective-permute-start(bf16[128,2048]{1,0:T(8,128)(2,1)S(1)} %get-tuple-element.16.own), channel_id=1, source_target_pairs={{12,13},{15,12},{20,21},{23,20},{28,25},{31,24},{45,42},{46,43},{5... | collective-permute-start | bytes 1572872 | tf_op jit(solution)/shard_map/ppermute | solution.py:37
  11.0 27.8 %collective-permute-start.5 = (bf16[128,2048]{1,0:T(8,128)(2,1)S(1)}, bf16[128,2048]{1,0:T(8,128)(2,1)S(1)}, u32[]{:S(2)}, u32[]{:S(2)}) collective-permute-start(bf16[128,2048]{1,0:T(8,128)(2,1)S(1)} %get-tuple-element.16.own), channel_id=1, source_target_pairs={{14,12},{15,13},{22,20},{23,21},{30,24},{31,25},{44,42},{45,43},{5... | collective-permute-start | bytes 1572872 | tf_op jit(solution)/shard_map/ppermute | solution.py:37
  11.7 27.1 %collective-permute-start.4 = (bf16[128,2048]{1,0:T(8,128)(2,1)S(1)}, bf16[128,2048]{1,0:T(8,128)(2,1)S(1)}, u32[]{:S(2)}, u32[]{:S(2)}) collective-permute-start(bf16[128,2048]{1,0:T(8,128)(2,1)S(1)} %get-tuple-element.16.own), channel_id=1, source_target_pairs={{13,12},{14,13},{21,20},{22,21},{29,24},{30,25},{44,43},{47,42},{5... | collective-permute-start | bytes 1572872 | tf_op jit(solution)/shard_map/ppermute | solution.py:37
  12.4 26.3 %collective-permute-start = (bf16[128,2048]{1,0:T(8,128)(2,1)S(1)}, bf16[128,2048]{1,0:T(8,128)(2,1)S(1)}, u32[]{:S(2)}, u32[]{:S(2)}) collective-permute-start(bf16[128,2048]{1,0:T(8,128)(2,1)S(1)} %get-tuple-element.16.own), channel_id=1, source_target_pairs={{8,12},{9,13},{16,20},{17,21},{28,24},{29,25},{46,42},{47,43},{54,... | collective-permute-start | bytes 1572872 | tf_op jit(solution)/shard_map/ppermute | solution.py:37
  26.1 12.6 %collective-permute-start.1 = (bf16[128,1536]{1,0:T(8,128)(2,1)S(1)}, bf16[128,1536]{1,0:T(8,128)(2,1)S(1)}, u32[]{:S(2)}, u32[]{:S(2)}) collective-permute-start(bf16[128,1536]{1,0:T(8,128)(2,1)S(1)} %get-tuple-element.17.short_ref), channel_id=1, source_target_pairs={{9,12},{10,13},{17,20},{18,21},{25,24},{26,25},{40,43},{43,42},{48... | collective-permute-start | bytes 1179656 | tf_op jit(solution)/shard_map/ppermute | solution.py:37
  43.0 4.5 %collective-permute-start.7 = (bf16[512,1152]{1,0:T(8,128)(2,1)S(1)}, bf16[512,1152]{1,0:T(8,128)(2,1)S(1)}, u32[]{:S(2)}, u32[]{:S(2)}) collective-permute-start(bf16[512,1152]{1,0:T(8,128)(2,1)S(1)} %get-tuple-element.18), channel_id=1, source_target_pairs={{24,20},{25,21},{62,50},{63,51},{88,84},{89,85},{126,114},{127,115... | collective-permute-start | bytes 3538952 | tf_op jit(solution)/shard_map/ppermute | solution.py:37
  43.8 1.5 %collective-permute-start.11 = (bf16[128,2048]{1,0:T(8,128)(2,1)S(1)}, bf16[128,2048]{1,0:T(8,128)(2,1)S(1)}, u32[]{:S(2)}, u32[]{:S(2)}) collective-permute-start(bf16[128,2048]{1,0:T(8,128)(2,1)S(1)} %get-tuple-element.16.own), channel_id=1, source_target_pairs={{4,0},{5,1},{6,2},{7,3},{36,32},{37,33},{38,34},{39,35},{68,64},{6... | collective-permute-start | bytes 1572872 | tf_op jit(solution)/shard_map/ppermute | solution.py:37
  44.5 15.3 %collective-permute-start.10 = (bf16[1024,1024]{1,0:T(8,128)(2,1)S(1)}, bf16[1024,1024]{1,0:T(8,128)(2,1)S(1)}, u32[]{:S(2)}, u32[]{:S(2)}) collective-permute-start(bf16[1024,1024]{1,0:T(8,128)(2,1)S(1)} %get-tuple-element.19.gt_ref.gt_in), channel_id=1, source_target_pairs={{12,0},{13,1},{42,34},{43,35},{76,64},{77,65},{106,98},{107,99},{1... | collective-permute-start | bytes 6291464 | tf_op jit(solution)/shard_map/ppermute | solution.py:37
  45.4 7.5 %collective-permute-start.14 = (bf16[128,3584]{1,0:T(8,128)(2,1)S(1)}, bf16[128,3584]{1,0:T(8,128)(2,1)S(1)}, u32[]{:S(2)}, u32[]{:S(2)}) collective-permute-start(bf16[128,3584]{1,0:T(8,128)(2,1)S(1)} %shard_map.61.j0), channel_id=1, source_target_pairs={{0,1},{3,0},{33,34},{34,35},{64,65},{67,64},{97,98},{98,99},{128,1... | collective-permute-start | bytes 2752520 | tf_op jit(solution)/shard_map/ppermute | solution.py:37
  46.1 7.6 %collective-permute-start.13 = (bf16[128,3584]{1,0:T(8,128)(2,1)S(1)}, bf16[128,3584]{1,0:T(8,128)(2,1)S(1)}, u32[]{:S(2)}, u32[]{:S(2)}) collective-permute-start(bf16[128,3584]{1,0:T(8,128)(2,1)S(1)} %shard_map.61.j0), channel_id=1, source_target_pairs={{2,0},{3,1},{32,34},{33,35},{66,64},{67,65},{96,98},{97,99},{130,1... | collective-permute-start | bytes 2752520 | tf_op jit(solution)/shard_map/ppermute | solution.py:37
  46.8 7.6 %collective-permute-start.12 = (bf16[128,3584]{1,0:T(8,128)(2,1)S(1)}, bf16[128,3584]{1,0:T(8,128)(2,1)S(1)}, u32[]{:S(2)}, u32[]{:S(2)}) collective-permute-start(bf16[128,3584]{1,0:T(8,128)(2,1)S(1)} %shard_map.61.j0), channel_id=1, source_target_pairs={{1,0},{2,1},{32,35},{35,34},{65,64},{66,65},{96,99},{99,98},{129,1... | collective-permute-start | bytes 2752520 | tf_op jit(solution)/shard_map/ppermute | solution.py:37
  47.6 8.6 %collective-permute-start.15 = (bf16[512,1152]{1,0:T(8,128)(2,1)S(1)}, bf16[512,1152]{1,0:T(8,128)(2,1)S(1)}, u32[]{:S(2)}, u32[]{:S(2)}) collective-permute-start(bf16[512,1152]{1,0:T(8,128)(2,1)S(1)} %get-tuple-element.22), channel_id=1, source_target_pairs={{12,0},{13,1},{42,34},{43,35},{76,64},{77,65},{106,98},{107,99},{1... | collective-permute-start | bytes 3538952 | tf_op jit(solution)/shard_map/ppermute | solution.py:37
  52.9 8.2 %collective-permute-start.9 = (bf16[512,1152]{1,0:T(8,128)(2,1)S(1)}, bf16[512,1152]{1,0:T(8,128)(2,1)S(1)}, u32[]{:S(2)}, u32[]{:S(2)}) collective-permute-start(bf16[512,1152]{1,0:T(8,128)(2,1)S(1)} %shard_map.60), channel_id=1, source_target_pairs={{20,0},{21,1},{50,34},{51,35},{84,64},{85,65},{114,98},{115,99},{1... | collective-permute-start | bytes 3538952 | tf_op jit(solution)/shard_map/ppermute | solution.py:37
  53.7 7.4 %collective-permute-start.8 = (bf16[512,1152]{1,0:T(8,128)(2,1)S(1)}, bf16[512,1152]{1,0:T(8,128)(2,1)S(1)}, u32[]{:S(2)}, u32[]{:S(2)}) collective-permute-start(bf16[512,1152]{1,0:T(8,128)(2,1)S(1)} %shard_map.60), channel_id=1, source_target_pairs={{20,12},{21,13},{50,42},{51,43},{84,76},{85,77},{114,106},{115,107... | collective-permute-start | bytes 3538952 | tf_op jit(solution)/shard_map/ppermute | solution.py:37
  61.1 54.9 %copy-start.2 = (s32[4]{0:T(128)S(1)}, s32[4]{0:T(128)}, u32[]{:S(2)}) copy-start(s32[4]{0:T(128)} %owner_ref.1) | copy-start | bytes 52
  65.6 50.4 %collective-permute-start.16 = (bf16[2,128,1024]{2,1,0:T(8,128)(2,1)S(1)}, bf16[2,128,1024]{2,1,0:T(8,128)(2,1)S(1)}, u32[]{:S(2)}, u32[]{:S(2)}) collective-permute-start(bf16[2,128,1024]{2,1,0:T(8,128)(2,1)S(1)} %get-tuple-element.26), channel_id=1, source_target_pairs={{0,4},{1,5},{12,8},{13,9},{20,16},{21,17},{24,28},{25,29},{34,38},... | collective-permute-start | bytes 1572872 | tf_op jit(solution)/shard_map/ppermute | solution.py:37
  66.3 49.7 %collective-permute-start.17 = (bf16[2,128,1024]{2,1,0:T(8,128)(2,1)S(1)}, bf16[2,128,1024]{2,1,0:T(8,128)(2,1)S(1)}, u32[]{:S(2)}, u32[]{:S(2)}) collective-permute-start(bf16[2,128,1024]{2,1,0:T(8,128)(2,1)S(1)} %get-tuple-element.27), channel_id=1, source_target_pairs={{0,3},{1,2},{12,15},{13,14},{20,23},{21,22},{24,27},{25,26},{34,33... | collective-permute-start | bytes 1572872 | tf_op jit(solution)/shard_map/ppermute | solution.py:37
  67.6 48.4 %collective-permute-start.18 = (bf16[2,128,1024]{2,1,0:T(8,128)(2,1)S(1)}, bf16[2,128,1024]{2,1,0:T(8,128)(2,1)S(1)}, u32[]{:S(2)}, u32[]{:S(2)}) collective-permute-start(bf16[2,128,1024]{2,1,0:T(8,128)(2,1)S(1)} %get-tuple-element.28), channel_id=1, source_target_pairs={{0,7},{1,6},{12,11},{13,10},{20,19},{21,18},{24,31},{25,30},{34,37... | collective-permute-start | bytes 1572872 | tf_op jit(solution)/shard_map/ppermute | solution.py:37

commit v4 on v3

--- a/solution.py
+++ b/solution.py
@@ -142,11 +142,12 @@
         f_ref[(7 - p) * BLK:(8 - p) * BLK, (7 - p) * BLK:] = pack_ref[rows, width:]
 
 
-def lower(s_ref, f_ref, wt_ref, gt_ref):
-    for i in range(4):
-        cols = slice(0, (i + 1) * 256)
-        gram = dot(f_ref[tile(i), i * 256:], f_ref[cols, i * 256:], NT)
-        s_ref[tile(i), cols] = (gram + dot(wt_ref[tile(i), :], gt_ref[cols, :], NT)).astype(BF16)
+def gram_tile(f_ref, i):
+    return dot(f_ref[tile(i), i * 256:], f_ref[:(i + 1) * 256, i * 256:], NT)
+
+
+def sweep_tile(wt_ref, gt_ref, i):
+    return dot(wt_ref[tile(i), :], gt_ref[:(i + 1) * 256, :], NT)
 
 
 def pack_kernel(linv_hbm, sub_hbm, full_ref, short_ref, linv_ref, sub_ref, sems):
@@ -195,11 +196,21 @@
 
 
 def load_kernel(own, q0, e1, e2, e3, o1, o2, o3, gt_ref, f_ref, fpack_ref, spack_ref, l_ref, s_ref):
+    _, _, group = here()
     assemble(own, q0, e1, e2, e3, o1, o2, o3, f_ref, l_ref)
     couple(gt_ref, f_ref, l_ref)
-    lower(s_ref, f_ref, gt_ref, gt_ref)
-    pack(spack_ref, s_ref)
-    pack_upper(fpack_ref, f_ref)
+
+    @pl.when(group == TB - 1)
+    def _():
+        for i in range(4):
+            s_ref[tile(i), :(i + 1) * 256] = (
+                gram_tile(f_ref, i) + sweep_tile(gt_ref, gt_ref, i)
+            ).astype(BF16)
+        pack(spack_ref, s_ref)
+
+    @pl.when(group != TB - 1)
+    def _():
+        pack_upper(fpack_ref, f_ref)
 
 
 def late_kernel(j0, j1, j2, j3, gt_in, f_in, gt_ref, f_ref, l_ref):
@@ -220,12 +231,20 @@
         f_ref[...] = f_in[...]
 
 
-def step_kernel(pack_in, gt_ref, f_ref, pack_out, s_ref, wt_ref):
+def lower_kernel(f_ref, low_ref):
+    for i in range(4):
+        low_ref[tile(i), :(i + 1) * 256] = gram_tile(f_ref, i)
+
+
+def step_kernel(pack_in, gt_ref, low_ref, pack_out, s_ref, wt_ref):
     unpack(s_ref, pack_in)
     mirror(s_ref)
     for i in range(4):
         wt_ref[tile(i), :] = dot(gt_ref[tile(i), :], s_ref[...], NN).astype(BF16)
-    lower(s_ref, f_ref, wt_ref, gt_ref)
+    for i in range(4):
+        s_ref[tile(i), :(i + 1) * 256] = (
+            low_ref[tile(i), :(i + 1) * 256] + sweep_tile(wt_ref, gt_ref, i)
+        ).astype(BF16)
     pack(pack_out, s_ref)
 
 
@@ -358,7 +377,7 @@
             owned_ref[k:k + 1, b * BLK:(b + 1) * BLK] = total[k][b:b + 1, :]
 
 
-def call(kernel, outs, scratch, flops, *args, first=pltpu.VMEM, special=0):
+def call(kernel, outs, scratch, flops, *args, first=pltpu.VMEM, special=0, grant=24 << 20):
     vmem = pl.BlockSpec(memory_space=pltpu.VMEM)
     moved = sum(a.size * a.dtype.itemsize for a in args)
     return pl.pallas_call(
@@ -368,7 +387,7 @@
         out_specs=[vmem] * len(outs),
         scratch_shapes=[pltpu.VMEM(*s) if isinstance(s, tuple) else s for s in scratch],
         cost_estimate=pl.CostEstimate(flops=flops, bytes_accessed=moved, transcendentals=0),
-        compiler_params=pltpu.CompilerParams(vmem_limit_bytes=24 * 1024 * 1024),
+        compiler_params=pltpu.CompilerParams(vmem_limit_bytes=grant),
     )(*args)
 
 
@@ -381,7 +400,7 @@
     full, short = call(
         pack_kernel, [((BLK, 2 * N), BF16), ((BLK, N + 512), BF16)],
         [rows, rows, pltpu.SemaphoreType.DMA((2,))], flops // 64, linv, sub,
-        first=pltpu.HBM, special=2,
+        first=pltpu.HBM, special=2, grant=24 << 20,
     )
 
     def load(groups):
@@ -398,7 +417,8 @@
     to2 = send(spack, replica_to(3, 2))
     gt_next = send(gt_first, replica_to(1, 0))
     f_next = send(fpack, replica_to(1, 0))
-    (second,) = call(step_kernel, [packed], [square, square], 2 * flops, to2, gt_first, ft_first)
+    (low,) = call(lower_kernel, [tall], [], flops // 2, ft_first)
+    (second,) = call(step_kernel, [packed], [square, square], 2 * flops, to2, gt_first, low)
     (joined,) = call(join_kernel, [((BLK, 3 * N + 512), BF16)], [], flops // 64, short, above)
     pieces = [joined] + [send(joined, late_from(dx)) for dx in (1, 2, 3)]
     gt, ft = call(late_kernel, [square, square], [square], flops, *pieces, gt_first, ft_first)

time: 118 us -> 116 us (0.983)
  the two profiles are of different devices: /device:TPU:401 before, /device:TPU:1 now
where the time goes in v4:
time: 116 us
  blocking collectives  43.5 us (38%)
  starting transfers between devices  27 us (23%)
  Pallas kernels  24.4 us (21%)
  waiting for transfers between devices  18.1 us (16%)
  local copies, waits for them, and re-layouts  1.9 us (2%)
    all_to_all x1, blocking collectives, sweep(): every = lax.all_to_all(var, 'tm', 0, 0, tiled=True)  43.5 us
    ppermute x19, starting transfers between devices, send(): return lax.ppermute(value, AXES, route)  27 us
    pallas_call x11, Pallas kernels, call(): pl.pallas_call(kernel, out_shape=[jax.ShapeDtypeStruct(s, d) for s, d in...  24.4 us
    ppermute x19, waiting for transfers between devices, send(): return lax.ppermute(value, AXES, route)  18.1 us
  transfers between devices with their start and end apart: 19, of which 3 were waited for; matrix products, arithmetic and copies ran while one was open for 0% of the time, Pallas kernels for 11%

profile of v4, /device:TPU:1, one launch (start us, length us, event | category | flops | bytes accessed | tf_op | source)
XLA Modules:
  0.0 115.8 jit_solution(14773990675762851978)
XLA Ops:
  0.6 0.9 copy-done
  1.6 0.9 copy-done.1
  2.5 0.2 shard_map.58
  2.8 0.7 collective-permute-start.3
  3.4 0.7 collective-permute-start.2
  4.1 0.7 collective-permute-start.6
  4.8 0.7 collective-permute-start.5
  5.5 0.7 collective-permute-start.4
  6.2 0.0 collective-permute-done.3.e3
  6.3 0.7 collective-permute-start
  7.0 0.0 collective-permute-done.2.e2
  7.0 0.7 collective-permute-start.1
  7.7 0.0 collective-permute-done.1.e1
  7.7 0.0 collective-permute-done.6.o3
  7.7 0.0 collective-permute-done.5.o2
  7.7 0.0 collective-permute-done.4.o1
  7.7 0.0 collective-permute-done.q0
  7.7 2.1 %shard_map.59 = (bf16[1024,1024]{1,0:T(8,128)(2,1)S(1)}, bf16[1024,1024]{1,0:T(8,128)(2,1)S(1)}, bf16[512,1152]{1,0:T(8,128)(2,1)S(1)}, bf16[512,1152]{1,0:T(8,128)(2,1)S(1)}) custom-call(bf16[128,2048]{1,0:T(8,128)(2,1)S(1)} %get-tuple-element.16.own, bf16[128,2048]{1,0:T(8,128)(2,1)S(1)} %collective-permute-done.q0, ...), custom_call_target="tpu_custom_call" | custom-call | flops 6442450944 | bytes 3801088 | tf_op jit(solution)/shard_map/pallas_call | solution.py:383
  9.8 0.7 collective-permute-start.7
  10.6 1.3 %collective-permute-start.11 = (bf16[128,2048]{1,0:T(8,128)(2,1)S(1)}, bf16[128,2048]{1,0:T(8,128)(2,1)S(1)}, u32[]{:S(2)}, u32[]{:S(2)}) collective-permute-start(bf16[128,2048]{1,0:T(8,128)(2,1)S(1)} %get-tuple-element.16.own), channel_id=1, source_target_pairs={{4,0},{5,1},{6,2},{7,3},{36,32},{37,33},{38,34},{39,35},{68,64},{6... | collective-permute-start | bytes 1572872 | tf_op jit(solution)/shard_map/ppermute | solution.py:37
  11.9 0.8 collective-permute-start.10
  12.7 7.8 %collective-permute-done.11.full_ref = bf16[128,2048]{1,0:T(8,128)(2,1)S(1)} collective-permute-done((bf16[128,2048]{1,0:T(8,128)(2,1)S(1)}, bf16[128,2048]{1,0:T(8,128)(2,1)S(1)}, u32[]{:S(2)}, u32[]{:S(2)}) %collective-permute-start.11) | collective-permute-done | bytes 524320 | tf_op jit(solution)/shard_map/ppermute | solution.py:37
  20.5 0.1 shard_map.62.j0
  20.6 0.7 collective-permute-start.14
  21.3 12.4 %collective-permute-start.13 = (bf16[128,3584]{1,0:T(8,128)(2,1)S(1)}, bf16[128,3584]{1,0:T(8,128)(2,1)S(1)}, u32[]{:S(2)}, u32[]{:S(2)}) collective-permute-start(bf16[128,3584]{1,0:T(8,128)(2,1)S(1)} %shard_map.62.j0), channel_id=1, source_target_pairs={{2,0},{3,1},{32,34},{33,35},{66,64},{67,65},{96,98},{97,99},{130,1... | collective-permute-start | bytes 2752520 | tf_op jit(solution)/shard_map/ppermute | solution.py:37
  33.7 1.3 %collective-permute-start.12 = (bf16[128,3584]{1,0:T(8,128)(2,1)S(1)}, bf16[128,3584]{1,0:T(8,128)(2,1)S(1)}, u32[]{:S(2)}, u32[]{:S(2)}) collective-permute-start(bf16[128,3584]{1,0:T(8,128)(2,1)S(1)} %shard_map.62.j0), channel_id=1, source_target_pairs={{1,0},{2,1},{32,35},{35,34},{65,64},{66,65},{96,99},{99,98},{129,1... | collective-permute-start | bytes 2752520 | tf_op jit(solution)/shard_map/ppermute | solution.py:37
  35.0 0.0 collective-permute-done.7.pack_in.to2
  35.0 0.7 collective-permute-start.15
  35.8 0.9 shard_map.60.low_ref
  36.7 3.9 %shard_map.61 = bf16[512,1152]{1,0:T(8,128)(2,1)S(1)} custom-call(bf16[512,1152]{1,0:T(8,128)(2,1)S(1)} %collective-permute-done.7.pack_in.to2, bf16[1024,1024]{1,0:T(8,128)(2,1)S(1)} %get-tuple-element.19.gt_ref.gt_in, f32[1024,1024]{1,0:T(8,128)S(1)} %shard_map.60.low_ref), custom_call_target="tpu_custom_call" | custom-call | flops 4294967296 | bytes 7471104 | tf_op jit(solution)/shard_map/pallas_call | solution.py:383
  40.6 0.0 collective-permute-done.14.j3
  40.6 0.7 collective-permute-start.9
  41.3 10.1 %collective-permute-done.13.j2 = bf16[128,3584]{1,0:T(8,128)(2,1)S(1)} collective-permute-done((bf16[128,3584]{1,0:T(8,128)(2,1)S(1)}, bf16[128,3584]{1,0:T(8,128)(2,1)S(1)}, u32[]{:S(2)}, u32[]{:S(2)}) %collective-permute-start.13) | collective-permute-done | bytes 917536 | tf_op jit(solution)/shard_map/ppermute | solution.py:37
  51.4 0.7 collective-permute-start.8
  52.1 0.1 collective-permute-done.12.j1
  52.2 2.0 %shard_map.63 = (bf16[1024,1024]{1,0:T(8,128)(2,1)S(1)}, bf16[1024,1024]{1,0:T(8,128)(2,1)S(1)}) custom-call(bf16[128,3584]{1,0:T(8,128)(2,1)S(1)} %shard_map.62.j0, bf16[128,3584]{1,0:T(8,128)(2,1)S(1)} %collective-permute-done.12.j1, bf16[128,3584]{1,0:T(8,128)(2,1)S(1)} %collective-permute-done.13.j2, bf16[128,3584]{1,0:T(8,128)(2,1)S(1)} %collective-permute-done.14.j3, ...), custom_call_target="tpu_custom_call" | custom-call | flops 2147483648 | bytes 7864320 | tf_op jit(solution)/shard_map/pallas_call | solution.py:383
  54.3 1.3 %shard_map.66.gram_ref = f32[512,1024]{1,0:T(8,128)S(1)} custom-call(bf16[1024,1024]{1,0:T(8,128)(2,1)S(1)} %get-tuple-element.23.f_ref), custom_call_target="tpu_custom_call" | custom-call | flops 2147483648 | bytes 2097152 | tf_op jit(solution)/shard_map/pallas_call | solution.py:383
  55.6 3.5 %shard_map.65.base_ref = f32[1024,1024]{1,0:T(8,128)S(1)} custom-call(bf16[512,1152]{1,0:T(8,128)(2,1)S(1)} %collective-permute-done.15.fpack_next, bf16[1024,1024]{1,0:T(8,128)(2,1)S(1)} %get-tuple-element.21.gt_ref), custom_call_target="tpu_custom_call" | custom-call | flops 6442450944 | bytes 3276800 | tf_op jit(solution)/shard_map/pallas_call | solution.py:383
  59.1 1.3 %shard_map.64.left_ref = bf16[1024,1024]{1,0:T(8,128)(2,1)S(1)} custom-call(bf16[1024,1024]{1,0:T(8,128)(2,1)S(1)} %collective-permute-done.10.gt_next, bf16[1024,1024]{1,0:T(8,128)(2,1)S(1)} %get-tuple-element.21.gt_ref), custom_call_target="tpu_custom_call" | custom-call | flops 2147483648 | bytes 4194304 | tf_op jit(solution)/shard_map/pallas_call | solution.py:383
  60.4 0.0 copy-start.2
  60.4 0.0 collective-permute-done.9.to0
  60.4 0.0 collective-permute-done.8.to1
  60.4 7.7 %shard_map.67 = (bf16[2,128,1024]{2,1,0:T(8,128)(2,1)S(1)}, bf16[2,128,1024]{2,1,0:T(8,128)(2,1)S(1)}, bf16[2,128,1024]{2,1,0:T(8,128)(2,1)S(1)}, bf16[2,128,1024]{2,1,0:T(8,128)(2,1)S(1)}, f32[32,8,128]{2,1,0:T(8,128)S(1)}) custom-call(bf16[512,1152]{1,0:T(8,128)(2,1)S(1)} %collective-permute-done.7.pack_in.to2, ...), custom_call_target="tpu_custom_call" | custom-call | flops 12884901888 | bytes 16121856 | tf_op jit(solution)/shard_map/pallas_call | solution.py:383
  68.2 0.7 collective-permute-start.16
  68.9 1.3 %collective-permute-start.17 = (bf16[2,128,1024]{2,1,0:T(8,128)(2,1)S(1)}, bf16[2,128,1024]{2,1,0:T(8,128)(2,1)S(1)}, u32[]{:S(2)}, u32[]{:S(2)}) collective-permute-start(bf16[2,128,1024]{2,1,0:T(8,128)(2,1)S(1)} %get-tuple-element.27), channel_id=1, source_target_pairs={{0,3},{1,2},{12,15},{13,14},{20,23},{21,22},{24,27},{25,26},{34,33... | collective-permute-start | bytes 1572872 | tf_op jit(solution)/shard_map/ppermute | solution.py:37
  70.2 0.7 collective-permute-start.18
  70.9 43.5 %all_to_all.5.every_ref = f32[32,8,128]{2,1,0:T(8,128)S(1)} all-to-all(f32[32,8,128]{2,1,0:T(8,128)S(1)} %get-tuple-element.24), channel_id=1, replica_groups=mesh['cfg'=16,'tm'=32] {'tm'}, dimensions={0} | all-to-all | bytes 262144 | tf_op jit(solution)/shard_map/all_to_all | solution.py:435
  114.4 1.4 %shard_map.68 = (bf16[128,1024]{1,0:T(8,128)(2,1)}, bf16[128,1024]{1,0:T(8,128)(2,1)}, f32[2,1024]{1,0:T(2,128)}) custom-call(s32[4]{0:T(128)S(1)} %copy-done.2, f32[32,8,128]{2,1,0:T(8,128)S(1)} %all_to_all.5.every_ref, bf16[2,128,1024]{2,1,0:T(8,128)(2,1)S(1)} %get-tuple-element.25.own_ref, bf16[2,128,1024]{2,1,0:T(8,128)(2,1)S(1)} %collective-permute-done.16.b1_ref, ...), custom_call_target="tpu_custom_call" | custom-call | flops 33554432 | bytes 2228240 | tf_op jit(solution)/shard_map/pallas_call | solution.py:383
  (8 shorter events, 0.0 us)
Async XLA Ops:
  0.6 1.0 copy-start
  1.6 0.9 copy-start.1
  2.8 3.5 %collective-permute-start.3 = (bf16[128,1536]{1,0:T(8,128)(2,1)S(1)}, bf16[128,1536]{1,0:T(8,128)(2,1)S(1)}, u32[]{:S(2)}, u32[]{:S(2)}) collective-permute-start(bf16[128,1536]{1,0:T(8,128)(2,1)S(1)} %get-tuple-element.17.short_ref), channel_id=1, source_target_pairs={{8,13},{11,12},{16,21},{19,20},{24,25},{27,24},{41,42},{42,43},{49... | collective-permute-start | bytes 1179656 | tf_op jit(solution)/shard_map/ppermute | solution.py:37
  3.4 3.5 %collective-permute-start.2 = (bf16[128,1536]{1,0:T(8,128)(2,1)S(1)}, bf16[128,1536]{1,0:T(8,128)(2,1)S(1)}, u32[]{:S(2)}, u32[]{:S(2)}) collective-permute-start(bf16[128,1536]{1,0:T(8,128)(2,1)S(1)} %get-tuple-element.17.short_ref), channel_id=1, source_target_pairs={{10,12},{11,13},{18,20},{19,21},{26,24},{27,25},{40,42},{41,43},{4... | collective-permute-start | bytes 1179656 | tf_op jit(solution)/shard_map/ppermute | solution.py:37
  4.1 3.5 %collective-permute-start.6 = (bf16[128,2048]{1,0:T(8,128)(2,1)S(1)}, bf16[128,2048]{1,0:T(8,128)(2,1)S(1)}, u32[]{:S(2)}, u32[]{:S(2)}) collective-permute-start(bf16[128,2048]{1,0:T(8,128)(2,1)S(1)} %get-tuple-element.16.own), channel_id=1, source_target_pairs={{12,13},{15,12},{20,21},{23,20},{28,25},{31,24},{45,42},{46,43},{5... | collective-permute-start | bytes 1572872 | tf_op jit(solution)/shard_map/ppermute | solution.py:37
  4.8 2.8 %collective-permute-start.5 = (bf16[128,2048]{1,0:T(8,128)(2,1)S(1)}, bf16[128,2048]{1,0:T(8,128)(2,1)S(1)}, u32[]{:S(2)}, u32[]{:S(2)}) collective-permute-start(bf16[128,2048]{1,0:T(8,128)(2,1)S(1)} %get-tuple-element.16.own), channel_id=1, source_target_pairs={{14,12},{15,13},{22,20},{23,21},{30,24},{31,25},{44,42},{45,43},{5... | collective-permute-start | bytes 1572872 | tf_op jit(solution)/shard_map/ppermute | solution.py:37
  5.5 2.2 %collective-permute-start.4 = (bf16[128,2048]{1,0:T(8,128)(2,1)S(1)}, bf16[128,2048]{1,0:T(8,128)(2,1)S(1)}, u32[]{:S(2)}, u32[]{:S(2)}) collective-permute-start(bf16[128,2048]{1,0:T(8,128)(2,1)S(1)} %get-tuple-element.16.own), channel_id=1, source_target_pairs={{13,12},{14,13},{21,20},{22,21},{29,24},{30,25},{44,43},{47,42},{5... | collective-permute-start | bytes 1572872 | tf_op jit(solution)/shard_map/ppermute | solution.py:37
  6.3 1.5 %collective-permute-start = (bf16[128,2048]{1,0:T(8,128)(2,1)S(1)}, bf16[128,2048]{1,0:T(8,128)(2,1)S(1)}, u32[]{:S(2)}, u32[]{:S(2)}) collective-permute-start(bf16[128,2048]{1,0:T(8,128)(2,1)S(1)} %get-tuple-element.16.own), channel_id=1, source_target_pairs={{8,12},{9,13},{16,20},{17,21},{28,24},{29,25},{46,42},{47,43},{54,... | collective-permute-start | bytes 1572872 | tf_op jit(solution)/shard_map/ppermute | solution.py:37
  7.0 0.7 collective-permute-start.1
  9.8 25.2 %collective-permute-start.7 = (bf16[512,1152]{1,0:T(8,128)(2,1)S(1)}, bf16[512,1152]{1,0:T(8,128)(2,1)S(1)}, u32[]{:S(2)}, u32[]{:S(2)}) collective-permute-start(bf16[512,1152]{1,0:T(8,128)(2,1)S(1)} %get-tuple-element.18), channel_id=1, source_target_pairs={{24,20},{25,21},{62,50},{63,51},{88,84},{89,85},{126,114},{127,115... | collective-permute-start | bytes 3538952 | tf_op jit(solution)/shard_map/ppermute | solution.py:37
  10.6 9.9 %collective-permute-start.11 = (bf16[128,2048]{1,0:T(8,128)(2,1)S(1)}, bf16[128,2048]{1,0:T(8,128)(2,1)S(1)}, u32[]{:S(2)}, u32[]{:S(2)}) collective-permute-start(bf16[128,2048]{1,0:T(8,128)(2,1)S(1)} %get-tuple-element.16.own), channel_id=1, source_target_pairs={{4,0},{5,1},{6,2},{7,3},{36,32},{37,33},{38,34},{39,35},{68,64},{6... | collective-permute-start | bytes 1572872 | tf_op jit(solution)/shard_map/ppermute | solution.py:37
  11.9 47.3 %collective-permute-start.10 = (bf16[1024,1024]{1,0:T(8,128)(2,1)S(1)}, bf16[1024,1024]{1,0:T(8,128)(2,1)S(1)}, u32[]{:S(2)}, u32[]{:S(2)}) collective-permute-start(bf16[1024,1024]{1,0:T(8,128)(2,1)S(1)} %get-tuple-element.19.gt_ref.gt_in), channel_id=1, source_target_pairs={{12,0},{13,1},{42,34},{43,35},{76,64},{77,65},{106,98},{107,99},{1... | collective-permute-start | bytes 6291464 | tf_op jit(solution)/shard_map/ppermute | solution.py:37
  20.6 20.0 %collective-permute-start.14 = (bf16[128,3584]{1,0:T(8,128)(2,1)S(1)}, bf16[128,3584]{1,0:T(8,128)(2,1)S(1)}, u32[]{:S(2)}, u32[]{:S(2)}) collective-permute-start(bf16[128,3584]{1,0:T(8,128)(2,1)S(1)} %shard_map.62.j0), channel_id=1, source_target_pairs={{0,1},{3,0},{33,34},{34,35},{64,65},{67,64},{97,98},{98,99},{128,1... | collective-permute-start | bytes 2752520 | tf_op jit(solution)/shard_map/ppermute | solution.py:37
  21.3 30.1 %collective-permute-start.13 = (bf16[128,3584]{1,0:T(8,128)(2,1)S(1)}, bf16[128,3584]{1,0:T(8,128)(2,1)S(1)}, u32[]{:S(2)}, u32[]{:S(2)}) collective-permute-start(bf16[128,3584]{1,0:T(8,128)(2,1)S(1)} %shard_map.62.j0), channel_id=1, source_target_pairs={{2,0},{3,1},{32,34},{33,35},{66,64},{67,65},{96,98},{97,99},{130,1... | collective-permute-start | bytes 2752520 | tf_op jit(solution)/shard_map/ppermute | solution.py:37
  33.7 18.6 %collective-permute-start.12 = (bf16[128,3584]{1,0:T(8,128)(2,1)S(1)}, bf16[128,3584]{1,0:T(8,128)(2,1)S(1)}, u32[]{:S(2)}, u32[]{:S(2)}) collective-permute-start(bf16[128,3584]{1,0:T(8,128)(2,1)S(1)} %shard_map.62.j0), channel_id=1, source_target_pairs={{1,0},{2,1},{32,35},{35,34},{65,64},{66,65},{96,99},{99,98},{129,1... | collective-permute-start | bytes 2752520 | tf_op jit(solution)/shard_map/ppermute | solution.py:37
  35.0 20.5 %collective-permute-start.15 = (bf16[512,1152]{1,0:T(8,128)(2,1)S(1)}, bf16[512,1152]{1,0:T(8,128)(2,1)S(1)}, u32[]{:S(2)}, u32[]{:S(2)}) collective-permute-start(bf16[512,1152]{1,0:T(8,128)(2,1)S(1)} %get-tuple-element.22), channel_id=1, source_target_pairs={{12,0},{13,1},{42,34},{43,35},{76,64},{77,65},{106,98},{107,99},{1... | collective-permute-start | bytes 3538952 | tf_op jit(solution)/shard_map/ppermute | solution.py:37
  40.6 19.8 %collective-permute-start.9 = (bf16[512,1152]{1,0:T(8,128)(2,1)S(1)}, bf16[512,1152]{1,0:T(8,128)(2,1)S(1)}, u32[]{:S(2)}, u32[]{:S(2)}) collective-permute-start(bf16[512,1152]{1,0:T(8,128)(2,1)S(1)} %shard_map.61), channel_id=1, source_target_pairs={{20,0},{21,1},{50,34},{51,35},{84,64},{85,65},{114,98},{115,99},{1... | collective-permute-start | bytes 3538952 | tf_op jit(solution)/shard_map/ppermute | solution.py:37
  51.4 9.0 %collective-permute-start.8 = (bf16[512,1152]{1,0:T(8,128)(2,1)S(1)}, bf16[512,1152]{1,0:T(8,128)(2,1)S(1)}, u32[]{:S(2)}, u32[]{:S(2)}) collective-permute-start(bf16[512,1152]{1,0:T(8,128)(2,1)S(1)} %shard_map.61), channel_id=1, source_target_pairs={{20,12},{21,13},{50,42},{51,43},{84,76},{85,77},{114,106},{115,107... | collective-permute-start | bytes 3538952 | tf_op jit(solution)/shard_map/ppermute | solution.py:37
  60.4 54.0 %copy-start.2 = (s32[4]{0:T(128)S(1)}, s32[4]{0:T(128)}, u32[]{:S(2)}) copy-start(s32[4]{0:T(128)} %owner_ref.1) | copy-start | bytes 52
  68.2 46.2 %collective-permute-start.16 = (bf16[2,128,1024]{2,1,0:T(8,128)(2,1)S(1)}, bf16[2,128,1024]{2,1,0:T(8,128)(2,1)S(1)}, u32[]{:S(2)}, u32[]{:S(2)}) collective-permute-start(bf16[2,128,1024]{2,1,0:T(8,128)(2,1)S(1)} %get-tuple-element.26), channel_id=1, source_target_pairs={{0,4},{1,5},{12,8},{13,9},{20,16},{21,17},{24,28},{25,29},{34,38},... | collective-permute-start | bytes 1572872 | tf_op jit(solution)/shard_map/ppermute | solution.py:37
  68.9 45.5 %collective-permute-start.17 = (bf16[2,128,1024]{2,1,0:T(8,128)(2,1)S(1)}, bf16[2,128,1024]{2,1,0:T(8,128)(2,1)S(1)}, u32[]{:S(2)}, u32[]{:S(2)}) collective-permute-start(bf16[2,128,1024]{2,1,0:T(8,128)(2,1)S(1)} %get-tuple-element.27), channel_id=1, source_target_pairs={{0,3},{1,2},{12,15},{13,14},{20,23},{21,22},{24,27},{25,26},{34,33... | collective-permute-start | bytes 1572872 | tf_op jit(solution)/shard_map/ppermute | solution.py:37
  70.2 44.2 %collective-permute-start.18 = (bf16[2,128,1024]{2,1,0:T(8,128)(2,1)S(1)}, bf16[2,128,1024]{2,1,0:T(8,128)(2,1)S(1)}, u32[]{:S(2)}, u32[]{:S(2)}) collective-permute-start(bf16[2,128,1024]{2,1,0:T(8,128)(2,1)S(1)} %get-tuple-element.28), channel_id=1, source_target_pairs={{0,7},{1,6},{12,11},{13,10},{20,19},{21,18},{24,31},{25,30},{34,37... | collective-permute-start | bytes 1572872 | tf_op jit(solution)/shard_map/ppermute | solution.py:37

commit v5 on v4

--- a/solution.py
+++ b/solution.py
@@ -405,8 +405,10 @@
 
     def load(groups):
         q0 = send(full, load_above(groups))
-        odds = [send(full, load_from(dx, 1, groups)) for dx in (1, 2, 3)]
-        evens = [send(short, load_from(dx, 0, groups)) for dx in (1, 2, 3)]
+        odds, evens = [], []
+        for dx in (1, 2, 3):
+            odds.append(send(full, load_from(dx, 1, groups)))
+            evens.append(send(short, load_from(dx, 0, groups)))
         return (full, q0, *evens, *odds)
 
     pieces = load((1, 2, 3))

time: 116 us -> 116 us (level)
  no operation moved by 1% of the time
where the time goes in v5:
time: 116 us
  blocking collectives  43.5 us (38%)
  starting transfers between devices  27 us (23%)
  Pallas kernels  24.4 us (21%)
  waiting for transfers between devices  18.1 us (16%)
  local copies, waits for them, and re-layouts  1.9 us (2%)
    all_to_all x1, blocking collectives, sweep(): every = lax.all_to_all(var, 'tm', 0, 0, tiled=True)  43.5 us
    ppermute x19, starting transfers between devices, send(): return lax.ppermute(value, AXES, route)  27 us
    pallas_call x11, Pallas kernels, call(): pl.pallas_call(kernel, out_shape=[jax.ShapeDtypeStruct(s, d) for s, d in...  24.4 us
    ppermute x19, waiting for transfers between devices, send(): return lax.ppermute(value, AXES, route)  18.1 us
  transfers between devices with their start and end apart: 19, of which 3 were waited for; matrix products, arithmetic and copies ran while one was open for 0% of the time, Pallas kernels for 11%

profile of v5, /device:TPU:1, one launch (start us, length us, event | category | flops | bytes accessed | tf_op | source)
XLA Modules:
  0.0 115.8 jit_solution(14773990675762851978)
XLA Ops:
  0.6 0.9 copy-done
  1.6 0.9 copy-done.1
  2.5 0.2 shard_map.58
  2.8 0.7 collective-permute-start.3
  3.4 0.7 collective-permute-start.2
  4.1 0.7 collective-permute-start.6
  4.8 0.7 collective-permute-start.5
  5.5 0.7 collective-permute-start.4
  6.2 0.0 collective-permute-done.3.e3
  6.3 0.7 collective-permute-start
  7.0 0.0 collective-permute-done.2.e2
  7.0 0.7 collective-permute-start.1
  7.7 0.0 collective-permute-done.1.e1
  7.7 0.0 collective-permute-done.6.o3
  7.7 0.0 collective-permute-done.5.o2
  7.7 0.0 collective-permute-done.4.o1
  7.7 0.0 collective-permute-done.q0
  7.7 2.1 %shard_map.59 = (bf16[1024,1024]{1,0:T(8,128)(2,1)S(1)}, bf16[1024,1024]{1,0:T(8,128)(2,1)S(1)}, bf16[512,1152]{1,0:T(8,128)(2,1)S(1)}, bf16[512,1152]{1,0:T(8,128)(2,1)S(1)}) custom-call(bf16[128,2048]{1,0:T(8,128)(2,1)S(1)} %get-tuple-element.16.own, bf16[128,2048]{1,0:T(8,128)(2,1)S(1)} %collective-permute-done.q0, ...), custom_call_target="tpu_custom_call" | custom-call | flops 6442450944 | bytes 3801088 | tf_op jit(solution)/shard_map/pallas_call | solution.py:383
  9.8 0.7 collective-permute-start.7
  10.6 1.3 %collective-permute-start.11 = (bf16[128,2048]{1,0:T(8,128)(2,1)S(1)}, bf16[128,2048]{1,0:T(8,128)(2,1)S(1)}, u32[]{:S(2)}, u32[]{:S(2)}) collective-permute-start(bf16[128,2048]{1,0:T(8,128)(2,1)S(1)} %get-tuple-element.16.own), channel_id=1, source_target_pairs={{4,0},{5,1},{6,2},{7,3},{36,32},{37,33},{38,34},{39,35},{68,64},{6... | collective-permute-start | bytes 1572872 | tf_op jit(solution)/shard_map/ppermute | solution.py:37
  11.9 0.8 collective-permute-start.10
  12.7 7.8 %collective-permute-done.11.full_ref = bf16[128,2048]{1,0:T(8,128)(2,1)S(1)} collective-permute-done((bf16[128,2048]{1,0:T(8,128)(2,1)S(1)}, bf16[128,2048]{1,0:T(8,128)(2,1)S(1)}, u32[]{:S(2)}, u32[]{:S(2)}) %collective-permute-start.11) | collective-permute-done | bytes 524320 | tf_op jit(solution)/shard_map/ppermute | solution.py:37
  20.5 0.1 shard_map.62.j0
  20.6 0.7 collective-permute-start.14
  21.3 12.4 %collective-permute-start.13 = (bf16[128,3584]{1,0:T(8,128)(2,1)S(1)}, bf16[128,3584]{1,0:T(8,128)(2,1)S(1)}, u32[]{:S(2)}, u32[]{:S(2)}) collective-permute-start(bf16[128,3584]{1,0:T(8,128)(2,1)S(1)} %shard_map.62.j0), channel_id=1, source_target_pairs={{2,0},{3,1},{32,34},{33,35},{66,64},{67,65},{96,98},{97,99},{130,1... | collective-permute-start | bytes 2752520 | tf_op jit(solution)/shard_map/ppermute | solution.py:37
  33.7 1.3 %collective-permute-start.12 = (bf16[128,3584]{1,0:T(8,128)(2,1)S(1)}, bf16[128,3584]{1,0:T(8,128)(2,1)S(1)}, u32[]{:S(2)}, u32[]{:S(2)}) collective-permute-start(bf16[128,3584]{1,0:T(8,128)(2,1)S(1)} %shard_map.62.j0), channel_id=1, source_target_pairs={{1,0},{2,1},{32,35},{35,34},{65,64},{66,65},{96,99},{99,98},{129,1... | collective-permute-start | bytes 2752520 | tf_op jit(solution)/shard_map/ppermute | solution.py:37
  35.0 0.0 collective-permute-done.7.pack_in.to2
  35.0 0.7 collective-permute-start.15
  35.8 0.9 shard_map.60.low_ref
  36.7 3.9 %shard_map.61 = bf16[512,1152]{1,0:T(8,128)(2,1)S(1)} custom-call(bf16[512,1152]{1,0:T(8,128)(2,1)S(1)} %collective-permute-done.7.pack_in.to2, bf16[1024,1024]{1,0:T(8,128)(2,1)S(1)} %get-tuple-element.19.gt_ref.gt_in, f32[1024,1024]{1,0:T(8,128)S(1)} %shard_map.60.low_ref), custom_call_target="tpu_custom_call" | custom-call | flops 4294967296 | bytes 7471104 | tf_op jit(solution)/shard_map/pallas_call | solution.py:383
  40.6 0.0 collective-permute-done.14.j3
  40.6 0.7 collective-permute-start.9
  41.3 10.1 %collective-permute-done.13.j2 = bf16[128,3584]{1,0:T(8,128)(2,1)S(1)} collective-permute-done((bf16[128,3584]{1,0:T(8,128)(2,1)S(1)}, bf16[128,3584]{1,0:T(8,128)(2,1)S(1)}, u32[]{:S(2)}, u32[]{:S(2)}) %collective-permute-start.13) | collective-permute-done | bytes 917536 | tf_op jit(solution)/shard_map/ppermute | solution.py:37
  51.4 0.7 collective-permute-start.8
  52.1 0.1 collective-permute-done.12.j1
  52.2 2.0 %shard_map.63 = (bf16[1024,1024]{1,0:T(8,128)(2,1)S(1)}, bf16[1024,1024]{1,0:T(8,128)(2,1)S(1)}) custom-call(bf16[128,3584]{1,0:T(8,128)(2,1)S(1)} %shard_map.62.j0, bf16[128,3584]{1,0:T(8,128)(2,1)S(1)} %collective-permute-done.12.j1, bf16[128,3584]{1,0:T(8,128)(2,1)S(1)} %collective-permute-done.13.j2, bf16[128,3584]{1,0:T(8,128)(2,1)S(1)} %collective-permute-done.14.j3, ...), custom_call_target="tpu_custom_call" | custom-call | flops 2147483648 | bytes 7864320 | tf_op jit(solution)/shard_map/pallas_call | solution.py:383
  54.3 1.3 %shard_map.66.gram_ref = f32[512,1024]{1,0:T(8,128)S(1)} custom-call(bf16[1024,1024]{1,0:T(8,128)(2,1)S(1)} %get-tuple-element.23.f_ref), custom_call_target="tpu_custom_call" | custom-call | flops 2147483648 | bytes 2097152 | tf_op jit(solution)/shard_map/pallas_call | solution.py:383
  55.6 3.5 %shard_map.65.base_ref = f32[1024,1024]{1,0:T(8,128)S(1)} custom-call(bf16[512,1152]{1,0:T(8,128)(2,1)S(1)} %collective-permute-done.15.fpack_next, bf16[1024,1024]{1,0:T(8,128)(2,1)S(1)} %get-tuple-element.21.gt_ref), custom_call_target="tpu_custom_call" | custom-call | flops 6442450944 | bytes 3276800 | tf_op jit(solution)/shard_map/pallas_call | solution.py:383
  59.1 1.3 %shard_map.64.left_ref = bf16[1024,1024]{1,0:T(8,128)(2,1)S(1)} custom-call(bf16[1024,1024]{1,0:T(8,128)(2,1)S(1)} %collective-permute-done.10.gt_next, bf16[1024,1024]{1,0:T(8,128)(2,1)S(1)} %get-tuple-element.21.gt_ref), custom_call_target="tpu_custom_call" | custom-call | flops 2147483648 | bytes 4194304 | tf_op jit(solution)/shard_map/pallas_call | solution.py:383
  60.4 0.0 copy-start.2
  60.4 0.0 collective-permute-done.9.to0
  60.4 0.0 collective-permute-done.8.to1
  60.4 7.7 %shard_map.67 = (bf16[2,128,1024]{2,1,0:T(8,128)(2,1)S(1)}, bf16[2,128,1024]{2,1,0:T(8,128)(2,1)S(1)}, bf16[2,128,1024]{2,1,0:T(8,128)(2,1)S(1)}, bf16[2,128,1024]{2,1,0:T(8,128)(2,1)S(1)}, f32[32,8,128]{2,1,0:T(8,128)S(1)}) custom-call(bf16[512,1152]{1,0:T(8,128)(2,1)S(1)} %collective-permute-done.7.pack_in.to2, ...), custom_call_target="tpu_custom_call" | custom-call | flops 12884901888 | bytes 16121856 | tf_op jit(solution)/shard_map/pallas_call | solution.py:383
  68.2 0.7 collective-permute-start.16
  68.9 1.3 %collective-permute-start.17 = (bf16[2,128,1024]{2,1,0:T(8,128)(2,1)S(1)}, bf16[2,128,1024]{2,1,0:T(8,128)(2,1)S(1)}, u32[]{:S(2)}, u32[]{:S(2)}) collective-permute-start(bf16[2,128,1024]{2,1,0:T(8,128)(2,1)S(1)} %get-tuple-element.27), channel_id=1, source_target_pairs={{0,3},{1,2},{12,15},{13,14},{20,23},{21,22},{24,27},{25,26},{34,33... | collective-permute-start | bytes 1572872 | tf_op jit(solution)/shard_map/ppermute | solution.py:37
  70.2 0.7 collective-permute-start.18
  70.9 43.5 %all_to_all.5.every_ref = f32[32,8,128]{2,1,0:T(8,128)S(1)} all-to-all(f32[32,8,128]{2,1,0:T(8,128)S(1)} %get-tuple-element.24), channel_id=1, replica_groups=mesh['cfg'=16,'tm'=32] {'tm'}, dimensions={0} | all-to-all | bytes 262144 | tf_op jit(solution)/shard_map/all_to_all | solution.py:437
  114.4 1.4 %shard_map.68 = (bf16[128,1024]{1,0:T(8,128)(2,1)}, bf16[128,1024]{1,0:T(8,128)(2,1)}, f32[2,1024]{1,0:T(2,128)}) custom-call(s32[4]{0:T(128)S(1)} %copy-done.2, f32[32,8,128]{2,1,0:T(8,128)S(1)} %all_to_all.5.every_ref, bf16[2,128,1024]{2,1,0:T(8,128)(2,1)S(1)} %get-tuple-element.25.own_ref, bf16[2,128,1024]{2,1,0:T(8,128)(2,1)S(1)} %collective-permute-done.16.b1_ref, ...), custom_call_target="tpu_custom_call" | custom-call | flops 33554432 | bytes 2228240 | tf_op jit(solution)/shard_map/pallas_call | solution.py:383
  (8 shorter events, 0.0 us)
Async XLA Ops:
  0.6 1.0 copy-start
  1.6 0.9 copy-start.1
  2.8 3.5 %collective-permute-start.3 = (bf16[128,1536]{1,0:T(8,128)(2,1)S(1)}, bf16[128,1536]{1,0:T(8,128)(2,1)S(1)}, u32[]{:S(2)}, u32[]{:S(2)}) collective-permute-start(bf16[128,1536]{1,0:T(8,128)(2,1)S(1)} %get-tuple-element.17.short_ref), channel_id=1, source_target_pairs={{8,13},{11,12},{16,21},{19,20},{24,25},{27,24},{41,42},{42,43},{49... | collective-permute-start | bytes 1179656 | tf_op jit(solution)/shard_map/ppermute | solution.py:37
  3.4 3.5 %collective-permute-start.2 = (bf16[128,1536]{1,0:T(8,128)(2,1)S(1)}, bf16[128,1536]{1,0:T(8,128)(2,1)S(1)}, u32[]{:S(2)}, u32[]{:S(2)}) collective-permute-start(bf16[128,1536]{1,0:T(8,128)(2,1)S(1)} %get-tuple-element.17.short_ref), channel_id=1, source_target_pairs={{10,12},{11,13},{18,20},{19,21},{26,24},{27,25},{40,42},{41,43},{4... | collective-permute-start | bytes 1179656 | tf_op jit(solution)/shard_map/ppermute | solution.py:37
  4.1 3.5 %collective-permute-start.6 = (bf16[128,2048]{1,0:T(8,128)(2,1)S(1)}, bf16[128,2048]{1,0:T(8,128)(2,1)S(1)}, u32[]{:S(2)}, u32[]{:S(2)}) collective-permute-start(bf16[128,2048]{1,0:T(8,128)(2,1)S(1)} %get-tuple-element.16.own), channel_id=1, source_target_pairs={{12,13},{15,12},{20,21},{23,20},{28,25},{31,24},{45,42},{46,43},{5... | collective-permute-start | bytes 1572872 | tf_op jit(solution)/shard_map/ppermute | solution.py:37
  4.8 2.8 %collective-permute-start.5 = (bf16[128,2048]{1,0:T(8,128)(2,1)S(1)}, bf16[128,2048]{1,0:T(8,128)(2,1)S(1)}, u32[]{:S(2)}, u32[]{:S(2)}) collective-permute-start(bf16[128,2048]{1,0:T(8,128)(2,1)S(1)} %get-tuple-element.16.own), channel_id=1, source_target_pairs={{14,12},{15,13},{22,20},{23,21},{30,24},{31,25},{44,42},{45,43},{5... | collective-permute-start | bytes 1572872 | tf_op jit(solution)/shard_map/ppermute | solution.py:37
  5.5 2.2 %collective-permute-start.4 = (bf16[128,2048]{1,0:T(8,128)(2,1)S(1)}, bf16[128,2048]{1,0:T(8,128)(2,1)S(1)}, u32[]{:S(2)}, u32[]{:S(2)}) collective-permute-start(bf16[128,2048]{1,0:T(8,128)(2,1)S(1)} %get-tuple-element.16.own), channel_id=1, source_target_pairs={{13,12},{14,13},{21,20},{22,21},{29,24},{30,25},{44,43},{47,42},{5... | collective-permute-start | bytes 1572872 | tf_op jit(solution)/shard_map/ppermute | solution.py:37
  6.3 1.5 %collective-permute-start = (bf16[128,2048]{1,0:T(8,128)(2,1)S(1)}, bf16[128,2048]{1,0:T(8,128)(2,1)S(1)}, u32[]{:S(2)}, u32[]{:S(2)}) collective-permute-start(bf16[128,2048]{1,0:T(8,128)(2,1)S(1)} %get-tuple-element.16.own), channel_id=1, source_target_pairs={{8,12},{9,13},{16,20},{17,21},{28,24},{29,25},{46,42},{47,43},{54,... | collective-permute-start | bytes 1572872 | tf_op jit(solution)/shard_map/ppermute | solution.py:37
  7.0 0.7 collective-permute-start.1
  9.8 25.2 %collective-permute-start.7 = (bf16[512,1152]{1,0:T(8,128)(2,1)S(1)}, bf16[512,1152]{1,0:T(8,128)(2,1)S(1)}, u32[]{:S(2)}, u32[]{:S(2)}) collective-permute-start(bf16[512,1152]{1,0:T(8,128)(2,1)S(1)} %get-tuple-element.18), channel_id=1, source_target_pairs={{24,20},{25,21},{62,50},{63,51},{88,84},{89,85},{126,114},{127,115... | collective-permute-start | bytes 3538952 | tf_op jit(solution)/shard_map/ppermute | solution.py:37
  10.6 9.9 %collective-permute-start.11 = (bf16[128,2048]{1,0:T(8,128)(2,1)S(1)}, bf16[128,2048]{1,0:T(8,128)(2,1)S(1)}, u32[]{:S(2)}, u32[]{:S(2)}) collective-permute-start(bf16[128,2048]{1,0:T(8,128)(2,1)S(1)} %get-tuple-element.16.own), channel_id=1, source_target_pairs={{4,0},{5,1},{6,2},{7,3},{36,32},{37,33},{38,34},{39,35},{68,64},{6... | collective-permute-start | bytes 1572872 | tf_op jit(solution)/shard_map/ppermute | solution.py:37
  11.9 47.3 %collective-permute-start.10 = (bf16[1024,1024]{1,0:T(8,128)(2,1)S(1)}, bf16[1024,1024]{1,0:T(8,128)(2,1)S(1)}, u32[]{:S(2)}, u32[]{:S(2)}) collective-permute-start(bf16[1024,1024]{1,0:T(8,128)(2,1)S(1)} %get-tuple-element.19.gt_ref.gt_in), channel_id=1, source_target_pairs={{12,0},{13,1},{42,34},{43,35},{76,64},{77,65},{106,98},{107,99},{1... | collective-permute-start | bytes 6291464 | tf_op jit(solution)/shard_map/ppermute | solution.py:37
  20.6 20.0 %collective-permute-start.14 = (bf16[128,3584]{1,0:T(8,128)(2,1)S(1)}, bf16[128,3584]{1,0:T(8,128)(2,1)S(1)}, u32[]{:S(2)}, u32[]{:S(2)}) collective-permute-start(bf16[128,3584]{1,0:T(8,128)(2,1)S(1)} %shard_map.62.j0), channel_id=1, source_target_pairs={{0,1},{3,0},{33,34},{34,35},{64,65},{67,64},{97,98},{98,99},{128,1... | collective-permute-start | bytes 2752520 | tf_op jit(solution)/shard_map/ppermute | solution.py:37
  21.3 30.1 %collective-permute-start.13 = (bf16[128,3584]{1,0:T(8,128)(2,1)S(1)}, bf16[128,3584]{1,0:T(8,128)(2,1)S(1)}, u32[]{:S(2)}, u32[]{:S(2)}) collective-permute-start(bf16[128,3584]{1,0:T(8,128)(2,1)S(1)} %shard_map.62.j0), channel_id=1, source_target_pairs={{2,0},{3,1},{32,34},{33,35},{66,64},{67,65},{96,98},{97,99},{130,1... | collective-permute-start | bytes 2752520 | tf_op jit(solution)/shard_map/ppermute | solution.py:37
  33.7 18.6 %collective-permute-start.12 = (bf16[128,3584]{1,0:T(8,128)(2,1)S(1)}, bf16[128,3584]{1,0:T(8,128)(2,1)S(1)}, u32[]{:S(2)}, u32[]{:S(2)}) collective-permute-start(bf16[128,3584]{1,0:T(8,128)(2,1)S(1)} %shard_map.62.j0), channel_id=1, source_target_pairs={{1,0},{2,1},{32,35},{35,34},{65,64},{66,65},{96,99},{99,98},{129,1... | collective-permute-start | bytes 2752520 | tf_op jit(solution)/shard_map/ppermute | solution.py:37
  35.0 20.5 %collective-permute-start.15 = (bf16[512,1152]{1,0:T(8,128)(2,1)S(1)}, bf16[512,1152]{1,0:T(8,128)(2,1)S(1)}, u32[]{:S(2)}, u32[]{:S(2)}) collective-permute-start(bf16[512,1152]{1,0:T(8,128)(2,1)S(1)} %get-tuple-element.22), channel_id=1, source_target_pairs={{12,0},{13,1},{42,34},{43,35},{76,64},{77,65},{106,98},{107,99},{1... | collective-permute-start | bytes 3538952 | tf_op jit(solution)/shard_map/ppermute | solution.py:37
  40.6 19.8 %collective-permute-start.9 = (bf16[512,1152]{1,0:T(8,128)(2,1)S(1)}, bf16[512,1152]{1,0:T(8,128)(2,1)S(1)}, u32[]{:S(2)}, u32[]{:S(2)}) collective-permute-start(bf16[512,1152]{1,0:T(8,128)(2,1)S(1)} %shard_map.61), channel_id=1, source_target_pairs={{20,0},{21,1},{50,34},{51,35},{84,64},{85,65},{114,98},{115,99},{1... | collective-permute-start | bytes 3538952 | tf_op jit(solution)/shard_map/ppermute | solution.py:37
  51.4 9.0 %collective-permute-start.8 = (bf16[512,1152]{1,0:T(8,128)(2,1)S(1)}, bf16[512,1152]{1,0:T(8,128)(2,1)S(1)}, u32[]{:S(2)}, u32[]{:S(2)}) collective-permute-start(bf16[512,1152]{1,0:T(8,128)(2,1)S(1)} %shard_map.61), channel_id=1, source_target_pairs={{20,12},{21,13},{50,42},{51,43},{84,76},{85,77},{114,106},{115,107... | collective-permute-start | bytes 3538952 | tf_op jit(solution)/shard_map/ppermute | solution.py:37
  60.4 54.0 %copy-start.2 = (s32[4]{0:T(128)S(1)}, s32[4]{0:T(128)}, u32[]{:S(2)}) copy-start(s32[4]{0:T(128)} %owner_ref.1) | copy-start | bytes 52
  68.2 46.2 %collective-permute-start.16 = (bf16[2,128,1024]{2,1,0:T(8,128)(2,1)S(1)}, bf16[2,128,1024]{2,1,0:T(8,128)(2,1)S(1)}, u32[]{:S(2)}, u32[]{:S(2)}) collective-permute-start(bf16[2,128,1024]{2,1,0:T(8,128)(2,1)S(1)} %get-tuple-element.26), channel_id=1, source_target_pairs={{0,4},{1,5},{12,8},{13,9},{20,16},{21,17},{24,28},{25,29},{34,38},... | collective-permute-start | bytes 1572872 | tf_op jit(solution)/shard_map/ppermute | solution.py:37
  68.9 45.5 %collective-permute-start.17 = (bf16[2,128,1024]{2,1,0:T(8,128)(2,1)S(1)}, bf16[2,128,1024]{2,1,0:T(8,128)(2,1)S(1)}, u32[]{:S(2)}, u32[]{:S(2)}) collective-permute-start(bf16[2,128,1024]{2,1,0:T(8,128)(2,1)S(1)} %get-tuple-element.27), channel_id=1, source_target_pairs={{0,3},{1,2},{12,15},{13,14},{20,23},{21,22},{24,27},{25,26},{34,33... | collective-permute-start | bytes 1572872 | tf_op jit(solution)/shard_map/ppermute | solution.py:37
  70.2 44.2 %collective-permute-start.18 = (bf16[2,128,1024]{2,1,0:T(8,128)(2,1)S(1)}, bf16[2,128,1024]{2,1,0:T(8,128)(2,1)S(1)}, u32[]{:S(2)}, u32[]{:S(2)}) collective-permute-start(bf16[2,128,1024]{2,1,0:T(8,128)(2,1)S(1)} %get-tuple-element.28), channel_id=1, source_target_pairs={{0,7},{1,6},{12,11},{13,10},{20,19},{21,18},{24,31},{25,30},{34,37... | collective-permute-start | bytes 1572872 | tf_op jit(solution)/shard_map/ppermute | solution.py:37

commit v6 on v5

--- a/solution.py
+++ b/solution.py
@@ -331,7 +331,7 @@
         diag = jnp.sum(jnp.where(row == col, total, 0.0), axis=0, keepdims=True)
         d_ref[pl.ds(at, 1), :] = diag.astype(BF16).astype(F32)
     for k in range(var_ref.shape[0]):
-        var_ref[k] = d_ref[...]
+        var_ref[k] = d_ref[...].astype(BF16)
 
     outs = (own_ref, a1_ref, a2_ref, a3_ref)
     for i in range(2):
@@ -365,7 +365,7 @@
     total = [jnp.zeros((8, BLK), F32) for _ in range(SLOTS)]
     for t in range(TB):
         first = by_core((ROW_OF[0][t], ROW_OF[1][t])) * NX + 2 * core
-        row = every_ref[first] + every_ref[first + 1]
+        row = every_ref[first].astype(F32) + every_ref[first + 1].astype(F32)
         rank = sum(
             ((owner_ref[u] == owner_ref[t]).astype(jnp.int32) for u in range(t)), jnp.int32(0)
         )
@@ -430,7 +430,7 @@
     (base,) = call(base_kernel, [tall], [square, part, square], 3 * flops, f_next, gt)
     (left,) = call(left_kernel, [square], [part], flops, gt_next, gt)
     own, a1, a2, a3, var = call(
-        sweep_kernel, [strip] * 4 + [((n_tm, 8, BLK), F32)],
+        sweep_kernel, [strip] * 4 + [((n_tm, 8, BLK), BF16)],
         [square, square, square, ((8, BLK), F32)],
         6 * flops, to2, to1, to0, left, base, gt_next, gram, gt,
     )

time: 116 us -> 115 us (level)
  blocking collectives: 43.5 us -> 42.1 us
    all_to_all x1, blocking collectives: 43.5 us -> 42.1 us  [sweep(): every = lax.all_to_all(var, 'tm', 0, 0, tiled=True)]
where the time goes in v6:
time: 115 us; the launch traced here: 114 us
  blocking collectives  42.1 us (37%)
  starting transfers between devices  27 us (23%)
  Pallas kernels  24.4 us (21%)
  waiting for transfers between devices  18.1 us (16%)
  local copies, waits for them, and re-layouts  1.9 us (2%)
    all_to_all x1, blocking collectives, sweep(): every = lax.all_to_all(var, 'tm', 0, 0, tiled=True)  42.1 us
    ppermute x19, starting transfers between devices, send(): return lax.ppermute(value, AXES, route)  27 us
    pallas_call x11, Pallas kernels, call(): pl.pallas_call(kernel, out_shape=[jax.ShapeDtypeStruct(s, d) for s, d in...  24.4 us
    ppermute x19, waiting for transfers between devices, send(): return lax.ppermute(value, AXES, route)  18.1 us
  transfers between devices with their start and end apart: 19, of which 3 were waited for; matrix products, arithmetic and copies ran while one was open for 0% of the time, Pallas kernels for 11%

profile of v6, /device:TPU:1, one launch (start us, length us, event | category | flops | bytes accessed | tf_op | source)
XLA Modules:
  0.0 114.5 jit_solution(3809381936985880697)
XLA Ops:
  0.6 0.9 copy-done
  1.6 0.9 copy-done.1
  2.5 0.2 shard_map.58
  2.8 0.7 collective-permute-start.3
  3.4 0.7 collective-permute-start.2
  4.1 0.7 collective-permute-start.6
  4.8 0.7 collective-permute-start.5
  5.5 0.7 collective-permute-start.4
  6.2 0.0 collective-permute-done.3.e3
  6.3 0.7 collective-permute-start
  7.0 0.0 collective-permute-done.2.e2
  7.0 0.7 collective-permute-start.1
  7.7 0.0 collective-permute-done.1.e1
  7.7 0.0 collective-permute-done.6.o3
  7.7 0.0 collective-permute-done.5.o2
  7.7 0.0 collective-permute-done.4.o1
  7.7 0.0 collective-permute-done.q0
  7.7 2.1 %shard_map.59 = (bf16[1024,1024]{1,0:T(8,128)(2,1)S(1)}, bf16[1024,1024]{1,0:T(8,128)(2,1)S(1)}, bf16[512,1152]{1,0:T(8,128)(2,1)S(1)}, bf16[512,1152]{1,0:T(8,128)(2,1)S(1)}) custom-call(bf16[128,2048]{1,0:T(8,128)(2,1)S(1)} %get-tuple-element.16.own, bf16[128,2048]{1,0:T(8,128)(2,1)S(1)} %collective-permute-done.q0, ...), custom_call_target="tpu_custom_call" | custom-call | flops 6442450944 | bytes 3801088 | tf_op jit(solution)/shard_map/pallas_call | solution.py:383
  9.8 0.7 collective-permute-start.7
  10.6 1.3 %collective-permute-start.11 = (bf16[128,2048]{1,0:T(8,128)(2,1)S(1)}, bf16[128,2048]{1,0:T(8,128)(2,1)S(1)}, u32[]{:S(2)}, u32[]{:S(2)}) collective-permute-start(bf16[128,2048]{1,0:T(8,128)(2,1)S(1)} %get-tuple-element.16.own), channel_id=1, source_target_pairs={{4,0},{5,1},{6,2},{7,3},{36,32},{37,33},{38,34},{39,35},{68,64},{6... | collective-permute-start | bytes 1572872 | tf_op jit(solution)/shard_map/ppermute | solution.py:37
  11.9 0.8 collective-permute-start.10
  12.7 7.8 %collective-permute-done.11.full_ref = bf16[128,2048]{1,0:T(8,128)(2,1)S(1)} collective-permute-done((bf16[128,2048]{1,0:T(8,128)(2,1)S(1)}, bf16[128,2048]{1,0:T(8,128)(2,1)S(1)}, u32[]{:S(2)}, u32[]{:S(2)}) %collective-permute-start.11) | collective-permute-done | bytes 524320 | tf_op jit(solution)/shard_map/ppermute | solution.py:37
  20.5 0.1 shard_map.62.j0
  20.6 0.7 collective-permute-start.14
  21.3 12.4 %collective-permute-start.13 = (bf16[128,3584]{1,0:T(8,128)(2,1)S(1)}, bf16[128,3584]{1,0:T(8,128)(2,1)S(1)}, u32[]{:S(2)}, u32[]{:S(2)}) collective-permute-start(bf16[128,3584]{1,0:T(8,128)(2,1)S(1)} %shard_map.62.j0), channel_id=1, source_target_pairs={{2,0},{3,1},{32,34},{33,35},{66,64},{67,65},{96,98},{97,99},{130,1... | collective-permute-start | bytes 2752520 | tf_op jit(solution)/shard_map/ppermute | solution.py:37
  33.7 1.3 %collective-permute-start.12 = (bf16[128,3584]{1,0:T(8,128)(2,1)S(1)}, bf16[128,3584]{1,0:T(8,128)(2,1)S(1)}, u32[]{:S(2)}, u32[]{:S(2)}) collective-permute-start(bf16[128,3584]{1,0:T(8,128)(2,1)S(1)} %shard_map.62.j0), channel_id=1, source_target_pairs={{1,0},{2,1},{32,35},{35,34},{65,64},{66,65},{96,99},{99,98},{129,1... | collective-permute-start | bytes 2752520 | tf_op jit(solution)/shard_map/ppermute | solution.py:37
  35.0 0.7 collective-permute-start.15
  35.8 0.9 shard_map.60.low_ref
  36.7 3.9 %shard_map.61 = bf16[512,1152]{1,0:T(8,128)(2,1)S(1)} custom-call(bf16[512,1152]{1,0:T(8,128)(2,1)S(1)} %collective-permute-done.7.pack_in.to2, bf16[1024,1024]{1,0:T(8,128)(2,1)S(1)} %get-tuple-element.19.gt_ref.gt_in, f32[1024,1024]{1,0:T(8,128)S(1)} %shard_map.60.low_ref), custom_call_target="tpu_custom_call" | custom-call | flops 4294967296 | bytes 7471104 | tf_op jit(solution)/shard_map/pallas_call | solution.py:383
  40.6 0.0 collective-permute-done.14.j3
  40.6 0.7 collective-permute-start.9
  41.3 10.1 %collective-permute-done.13.j2 = bf16[128,3584]{1,0:T(8,128)(2,1)S(1)} collective-permute-done((bf16[128,3584]{1,0:T(8,128)(2,1)S(1)}, bf16[128,3584]{1,0:T(8,128)(2,1)S(1)}, u32[]{:S(2)}, u32[]{:S(2)}) %collective-permute-start.13) | collective-permute-done | bytes 917536 | tf_op jit(solution)/shard_map/ppermute | solution.py:37
  51.4 0.7 collective-permute-start.8
  52.1 0.1 collective-permute-done.12.j1
  52.2 2.0 %shard_map.63 = (bf16[1024,1024]{1,0:T(8,128)(2,1)S(1)}, bf16[1024,1024]{1,0:T(8,128)(2,1)S(1)}) custom-call(bf16[128,3584]{1,0:T(8,128)(2,1)S(1)} %shard_map.62.j0, bf16[128,3584]{1,0:T(8,128)(2,1)S(1)} %collective-permute-done.12.j1, bf16[128,3584]{1,0:T(8,128)(2,1)S(1)} %collective-permute-done.13.j2, bf16[128,3584]{1,0:T(8,128)(2,1)S(1)} %collective-permute-done.14.j3, ...), custom_call_target="tpu_custom_call" | custom-call | flops 2147483648 | bytes 7864320 | tf_op jit(solution)/shard_map/pallas_call | solution.py:383
  54.3 1.3 %shard_map.66.gram_ref = f32[512,1024]{1,0:T(8,128)S(1)} custom-call(bf16[1024,1024]{1,0:T(8,128)(2,1)S(1)} %get-tuple-element.23.f_ref), custom_call_target="tpu_custom_call" | custom-call | flops 2147483648 | bytes 2097152 | tf_op jit(solution)/shard_map/pallas_call | solution.py:383
  55.6 3.5 %shard_map.65.base_ref = f32[1024,1024]{1,0:T(8,128)S(1)} custom-call(bf16[512,1152]{1,0:T(8,128)(2,1)S(1)} %collective-permute-done.15.fpack_next, bf16[1024,1024]{1,0:T(8,128)(2,1)S(1)} %get-tuple-element.21.gt_ref), custom_call_target="tpu_custom_call" | custom-call | flops 6442450944 | bytes 3276800 | tf_op jit(solution)/shard_map/pallas_call | solution.py:383
  59.1 1.3 %shard_map.64.left_ref = bf16[1024,1024]{1,0:T(8,128)(2,1)S(1)} custom-call(bf16[1024,1024]{1,0:T(8,128)(2,1)S(1)} %collective-permute-done.10.gt_next, bf16[1024,1024]{1,0:T(8,128)(2,1)S(1)} %get-tuple-element.21.gt_ref), custom_call_target="tpu_custom_call" | custom-call | flops 2147483648 | bytes 4194304 | tf_op jit(solution)/shard_map/pallas_call | solution.py:383
  60.4 0.0 copy-start.2
  60.4 0.0 collective-permute-done.9.to0
  60.4 0.0 collective-permute-done.8.to1
  60.4 7.7 %shard_map.67 = (bf16[2,128,1024]{2,1,0:T(8,128)(2,1)S(1)}, bf16[2,128,1024]{2,1,0:T(8,128)(2,1)S(1)}, bf16[2,128,1024]{2,1,0:T(8,128)(2,1)S(1)}, bf16[2,128,102...) custom-call(bf16[512,1152]{1,0:T(8,128)(2,1)S(1)} %collective-permute-done.7.pack_in.to2, ...), custom_call_target="tpu_custom_call" | custom-call | flops 12884901888 | bytes 16121856 | tf_op jit(solution)/shard_map/pallas_call | solution.py:383
  68.2 0.7 collective-permute-start.16
  68.9 1.3 %collective-permute-start.17 = (bf16[2,128,1024]{2,1,0:T(8,128)(2,1)S(1)}, bf16[2,128,1024]{2,1,0:T(8,128)(2,1)S(1)}, u32[]{:S(2)}, u32[]{:S(2)}) collective-permute-start(bf16[2,128,1024]{2,1,0:T(8,128)(2,1)S(1)} %get-tuple-element.27), channel_id=1, source_target_pairs={{0,3},{1,2},{12,15},{13,14},{20,23},{21,22},{24,27},{25,26},{34,33... | collective-permute-start | bytes 1572872 | tf_op jit(solution)/shard_map/ppermute | solution.py:37
  70.2 0.7 collective-permute-start.18
  70.9 42.1 %all_to_all.5.every_ref = bf16[32,8,128]{2,1,0:T(8,128)(2,1)S(1)} all-to-all(bf16[32,8,128]{2,1,0:T(8,128)(2,1)S(1)} %get-tuple-element.24), channel_id=1, replica_groups=mesh['cfg'=16,'tm'=32] {'tm'}, dimensions={0} | all-to-all | bytes 131072 | tf_op jit(solution)/shard_map/all_to_all | solution.py:437
  113.0 0.0 collective-permute-done.16.b1_ref
  113.0 1.4 %shard_map.68 = (bf16[128,1024]{1,0:T(8,128)(2,1)}, bf16[128,1024]{1,0:T(8,128)(2,1)}, f32[2,1024]{1,0:T(2,128)}) custom-call(s32[4]{0:T(128)S(1)} %copy-done.2, bf16[32,8,128]{2,1,0:T(8,128)(2,1)S(1)} %all_to_all.5.every_ref, bf16[2,128,1024]{2,1,0:T(8,128)(2,1)S(1)} %get-tuple-element.25.own_ref, bf16[2,128,1024]{2,1,0:T(8,128)(2,1)S(1)} %collective-permute-done.16.b1_ref, ...), custom_call_target="tpu_custom_call" | custom-call | flops 33554432 | bytes 2162704 | tf_op jit(solution)/shard_map/pallas_call | solution.py:383
  (8 shorter events, 0.0 us)
Async XLA Ops:
  0.6 1.0 copy-start
  1.6 0.9 copy-start.1
  2.8 3.5 %collective-permute-start.3 = (bf16[128,1536]{1,0:T(8,128)(2,1)S(1)}, bf16[128,1536]{1,0:T(8,128)(2,1)S(1)}, u32[]{:S(2)}, u32[]{:S(2)}) collective-permute-start(bf16[128,1536]{1,0:T(8,128)(2,1)S(1)} %get-tuple-element.17.short_ref), channel_id=1, source_target_pairs={{8,13},{11,12},{16,21},{19,20},{24,25},{27,24},{41,42},{42,43},{49... | collective-permute-start | bytes 1179656 | tf_op jit(solution)/shard_map/ppermute | solution.py:37
  3.4 3.5 %collective-permute-start.2 = (bf16[128,1536]{1,0:T(8,128)(2,1)S(1)}, bf16[128,1536]{1,0:T(8,128)(2,1)S(1)}, u32[]{:S(2)}, u32[]{:S(2)}) collective-permute-start(bf16[128,1536]{1,0:T(8,128)(2,1)S(1)} %get-tuple-element.17.short_ref), channel_id=1, source_target_pairs={{10,12},{11,13},{18,20},{19,21},{26,24},{27,25},{40,42},{41,43},{4... | collective-permute-start | bytes 1179656 | tf_op jit(solution)/shard_map/ppermute | solution.py:37
  4.1 3.5 %collective-permute-start.6 = (bf16[128,2048]{1,0:T(8,128)(2,1)S(1)}, bf16[128,2048]{1,0:T(8,128)(2,1)S(1)}, u32[]{:S(2)}, u32[]{:S(2)}) collective-permute-start(bf16[128,2048]{1,0:T(8,128)(2,1)S(1)} %get-tuple-element.16.own), channel_id=1, source_target_pairs={{12,13},{15,12},{20,21},{23,20},{28,25},{31,24},{45,42},{46,43},{5... | collective-permute-start | bytes 1572872 | tf_op jit(solution)/shard_map/ppermute | solution.py:37
  4.8 2.8 %collective-permute-start.5 = (bf16[128,2048]{1,0:T(8,128)(2,1)S(1)}, bf16[128,2048]{1,0:T(8,128)(2,1)S(1)}, u32[]{:S(2)}, u32[]{:S(2)}) collective-permute-start(bf16[128,2048]{1,0:T(8,128)(2,1)S(1)} %get-tuple-element.16.own), channel_id=1, source_target_pairs={{14,12},{15,13},{22,20},{23,21},{30,24},{31,25},{44,42},{45,43},{5... | collective-permute-start | bytes 1572872 | tf_op jit(solution)/shard_map/ppermute | solution.py:37
  5.5 2.2 %collective-permute-start.4 = (bf16[128,2048]{1,0:T(8,128)(2,1)S(1)}, bf16[128,2048]{1,0:T(8,128)(2,1)S(1)}, u32[]{:S(2)}, u32[]{:S(2)}) collective-permute-start(bf16[128,2048]{1,0:T(8,128)(2,1)S(1)} %get-tuple-element.16.own), channel_id=1, source_target_pairs={{13,12},{14,13},{21,20},{22,21},{29,24},{30,25},{44,43},{47,42},{5... | collective-permute-start | bytes 1572872 | tf_op jit(solution)/shard_map/ppermute | solution.py:37
  6.3 1.5 %collective-permute-start = (bf16[128,2048]{1,0:T(8,128)(2,1)S(1)}, bf16[128,2048]{1,0:T(8,128)(2,1)S(1)}, u32[]{:S(2)}, u32[]{:S(2)}) collective-permute-start(bf16[128,2048]{1,0:T(8,128)(2,1)S(1)} %get-tuple-element.16.own), channel_id=1, source_target_pairs={{8,12},{9,13},{16,20},{17,21},{28,24},{29,25},{46,42},{47,43},{54,... | collective-permute-start | bytes 1572872 | tf_op jit(solution)/shard_map/ppermute | solution.py:37
  7.0 0.7 collective-permute-start.1
  9.8 25.2 %collective-permute-start.7 = (bf16[512,1152]{1,0:T(8,128)(2,1)S(1)}, bf16[512,1152]{1,0:T(8,128)(2,1)S(1)}, u32[]{:S(2)}, u32[]{:S(2)}) collective-permute-start(bf16[512,1152]{1,0:T(8,128)(2,1)S(1)} %get-tuple-element.18), channel_id=1, source_target_pairs={{24,20},{25,21},{62,50},{63,51},{88,84},{89,85},{126,114},{127,115... | collective-permute-start | bytes 3538952 | tf_op jit(solution)/shard_map/ppermute | solution.py:37
  10.6 9.9 %collective-permute-start.11 = (bf16[128,2048]{1,0:T(8,128)(2,1)S(1)}, bf16[128,2048]{1,0:T(8,128)(2,1)S(1)}, u32[]{:S(2)}, u32[]{:S(2)}) collective-permute-start(bf16[128,2048]{1,0:T(8,128)(2,1)S(1)} %get-tuple-element.16.own), channel_id=1, source_target_pairs={{4,0},{5,1},{6,2},{7,3},{36,32},{37,33},{38,34},{39,35},{68,64},{6... | collective-permute-start | bytes 1572872 | tf_op jit(solution)/shard_map/ppermute | solution.py:37
  11.9 47.3 %collective-permute-start.10 = (bf16[1024,1024]{1,0:T(8,128)(2,1)S(1)}, bf16[1024,1024]{1,0:T(8,128)(2,1)S(1)}, u32[]{:S(2)}, u32[]{:S(2)}) collective-permute-start(bf16[1024,1024]{1,0:T(8,128)(2,1)S(1)} %get-tuple-element.19.gt_ref.gt_in), channel_id=1, source_target_pairs={{12,0},{13,1},{42,34},{43,35},{76,64},{77,65},{106,98},{107,99},{1... | collective-permute-start | bytes 6291464 | tf_op jit(solution)/shard_map/ppermute | solution.py:37
  20.6 20.0 %collective-permute-start.14 = (bf16[128,3584]{1,0:T(8,128)(2,1)S(1)}, bf16[128,3584]{1,0:T(8,128)(2,1)S(1)}, u32[]{:S(2)}, u32[]{:S(2)}) collective-permute-start(bf16[128,3584]{1,0:T(8,128)(2,1)S(1)} %shard_map.62.j0), channel_id=1, source_target_pairs={{0,1},{3,0},{33,34},{34,35},{64,65},{67,64},{97,98},{98,99},{128,1... | collective-permute-start | bytes 2752520 | tf_op jit(solution)/shard_map/ppermute | solution.py:37
  21.3 30.1 %collective-permute-start.13 = (bf16[128,3584]{1,0:T(8,128)(2,1)S(1)}, bf16[128,3584]{1,0:T(8,128)(2,1)S(1)}, u32[]{:S(2)}, u32[]{:S(2)}) collective-permute-start(bf16[128,3584]{1,0:T(8,128)(2,1)S(1)} %shard_map.62.j0), channel_id=1, source_target_pairs={{2,0},{3,1},{32,34},{33,35},{66,64},{67,65},{96,98},{97,99},{130,1... | collective-permute-start | bytes 2752520 | tf_op jit(solution)/shard_map/ppermute | solution.py:37
  33.7 18.6 %collective-permute-start.12 = (bf16[128,3584]{1,0:T(8,128)(2,1)S(1)}, bf16[128,3584]{1,0:T(8,128)(2,1)S(1)}, u32[]{:S(2)}, u32[]{:S(2)}) collective-permute-start(bf16[128,3584]{1,0:T(8,128)(2,1)S(1)} %shard_map.62.j0), channel_id=1, source_target_pairs={{1,0},{2,1},{32,35},{35,34},{65,64},{66,65},{96,99},{99,98},{129,1... | collective-permute-start | bytes 2752520 | tf_op jit(solution)/shard_map/ppermute | solution.py:37
  35.0 20.5 %collective-permute-start.15 = (bf16[512,1152]{1,0:T(8,128)(2,1)S(1)}, bf16[512,1152]{1,0:T(8,128)(2,1)S(1)}, u32[]{:S(2)}, u32[]{:S(2)}) collective-permute-start(bf16[512,1152]{1,0:T(8,128)(2,1)S(1)} %get-tuple-element.22), channel_id=1, source_target_pairs={{12,0},{13,1},{42,34},{43,35},{76,64},{77,65},{106,98},{107,99},{1... | collective-permute-start | bytes 3538952 | tf_op jit(solution)/shard_map/ppermute | solution.py:37
  40.6 19.8 %collective-permute-start.9 = (bf16[512,1152]{1,0:T(8,128)(2,1)S(1)}, bf16[512,1152]{1,0:T(8,128)(2,1)S(1)}, u32[]{:S(2)}, u32[]{:S(2)}) collective-permute-start(bf16[512,1152]{1,0:T(8,128)(2,1)S(1)} %shard_map.61), channel_id=1, source_target_pairs={{20,0},{21,1},{50,34},{51,35},{84,64},{85,65},{114,98},{115,99},{1... | collective-permute-start | bytes 3538952 | tf_op jit(solution)/shard_map/ppermute | solution.py:37
  51.4 9.0 %collective-permute-start.8 = (bf16[512,1152]{1,0:T(8,128)(2,1)S(1)}, bf16[512,1152]{1,0:T(8,128)(2,1)S(1)}, u32[]{:S(2)}, u32[]{:S(2)}) collective-permute-start(bf16[512,1152]{1,0:T(8,128)(2,1)S(1)} %shard_map.61), channel_id=1, source_target_pairs={{20,12},{21,13},{50,42},{51,43},{84,76},{85,77},{114,106},{115,107... | collective-permute-start | bytes 3538952 | tf_op jit(solution)/shard_map/ppermute | solution.py:37
  60.4 52.6 %copy-start.2 = (s32[4]{0:T(128)S(1)}, s32[4]{0:T(128)}, u32[]{:S(2)}) copy-start(s32[4]{0:T(128)} %owner_ref.1) | copy-start | bytes 52
  68.2 44.9 %collective-permute-start.16 = (bf16[2,128,1024]{2,1,0:T(8,128)(2,1)S(1)}, bf16[2,128,1024]{2,1,0:T(8,128)(2,1)S(1)}, u32[]{:S(2)}, u32[]{:S(2)}) collective-permute-start(bf16[2,128,1024]{2,1,0:T(8,128)(2,1)S(1)} %get-tuple-element.26), channel_id=1, source_target_pairs={{0,4},{1,5},{12,8},{13,9},{20,16},{21,17},{24,28},{25,29},{34,38},... | collective-permute-start | bytes 1572872 | tf_op jit(solution)/shard_map/ppermute | solution.py:37
  68.9 44.2 %collective-permute-start.17 = (bf16[2,128,1024]{2,1,0:T(8,128)(2,1)S(1)}, bf16[2,128,1024]{2,1,0:T(8,128)(2,1)S(1)}, u32[]{:S(2)}, u32[]{:S(2)}) collective-permute-start(bf16[2,128,1024]{2,1,0:T(8,128)(2,1)S(1)} %get-tuple-element.27), channel_id=1, source_target_pairs={{0,3},{1,2},{12,15},{13,14},{20,23},{21,22},{24,27},{25,26},{34,33... | collective-permute-start | bytes 1572872 | tf_op jit(solution)/shard_map/ppermute | solution.py:37
  70.2 42.9 %collective-permute-start.18 = (bf16[2,128,1024]{2,1,0:T(8,128)(2,1)S(1)}, bf16[2,128,1024]{2,1,0:T(8,128)(2,1)S(1)}, u32[]{:S(2)}, u32[]{:S(2)}) collective-permute-start(bf16[2,128,1024]{2,1,0:T(8,128)(2,1)S(1)} %get-tuple-element.28), channel_id=1, source_target_pairs={{0,7},{1,6},{12,11},{13,10},{20,19},{21,18},{24,31},{25,30},{34,37... | collective-permute-start | bytes 1572872 | tf_op jit(solution)/shard_map/ppermute | solution.py:37
